TPU v7x, 32 devices: a whole 2x2x4 slice. The times are simulated.
32 devices in a mesh: seq: 8 (over z, core), fsdp: 4 (over y, x).
Axes of the slice: x: 2, y: 2, z: 4, core: 2. Of those that a mesh axis runs over, the one named last changes fastest.
Arguments:
- tokens: bfloat16 [4, 2048, 1792], P('fsdp', 'seq'), may hold values from -4 to 4
- seq_lengths: int32 [4, 1], P('fsdp'), may hold values from 1024 to 2048, as said below
- seq_offsets: int32 [4, 1], P('fsdp'), may hold values from 0 to 1024, as said below
- norm1_gain: bfloat16 [1792], P('fsdp'), may hold values from 0.5 to 1.5
- conv_weight: bfloat16 [1792, 3], P('fsdp'), may hold values from -0.8984375 to 0.8984375
- query_weight: bfloat16 [1792, 1792], P('fsdp'), may hold values from -0.125 to 0.125
- key_weight: bfloat16 [1792, 1792], P('fsdp'), may hold values from -0.125 to 0.125
- value_weight: bfloat16 [1792, 1792], P('fsdp'), may hold values from -0.125 to 0.125
- out_weight: bfloat16 [1792, 1792], P('fsdp'), may hold values from -0.75 to 0.75
- norm2_gain: bfloat16 [1792], P('fsdp'), may hold values from 0.5 to 1.5
- gate_weight: bfloat16 [1792, 4864], P('fsdp'), may hold values from -0.125 to 0.125
- up_weight: bfloat16 [1792, 4864], P('fsdp'), may hold values from -0.125 to 0.125
- down_weight: bfloat16 [4864, 1792], P('fsdp'), may hold values from -0.15625 to 0.15625
- cotangent: bfloat16 [4, 2048, 1792], P('fsdp', 'seq'), may hold values from -4 to 4
Outputs:
- layer_out: bfloat16 [4, 2048, 1792], P('fsdp', 'seq')
- tokens_grad: float32 [4, 2048, 1792], P('fsdp', 'seq')
- norm1_grad: float32 [1792], P('fsdp')
- conv_grad: float32 [1792, 3], P('fsdp')
- query_grad: float32 [1792, 1792], P('fsdp')
- key_grad: float32 [1792, 1792], P('fsdp')
- value_grad: float32 [1792, 1792], P('fsdp')
- out_grad: float32 [1792, 1792], P('fsdp')
- norm2_grad: float32 [1792], P('fsdp')
- gate_grad: float32 [1792, 4864], P('fsdp')
- up_grad: float32 [1792, 4864], P('fsdp')
- down_grad: float32 [4864, 1792], P('fsdp')
Inputs may be any that keep to these rules, and one draw needn't show every extreme that they name: `seq_lengths`: every group holds 1 sequence, each between 1024 and 2048 tokens long; some group has one of exactly 2048 tokens and some group one of exactly 1024. `seq_offsets`: sequence j of a group lies within slots j * 2048 to (j + 1) * 2048 - 1 of the group; all other slots are padding.
All inputs are finite; a program needn't handle non-finite values.
Results may differ from a plain program's by a relative error of at most 0.015.
Values may be sent and summed in bfloat16 or wider, within the bound.
A program may use at most 512 MiB of HBM per device.

v0:
```python
import functools

import jax
import jax.numpy as jnp
from jax import lax
from jax.experimental import pallas as pl
from jax.experimental.pallas import tpu as pltpu
from jax.sharding import PartitionSpec as P

HEADS = 16
WINDOW = 64
HEAD_DIM = 112
BLOCK = 128

EPS = 1e-05
NEG = -1e30
SCALE = HEAD_DIM ** (-0.5)
MESH_ID = pl.DeviceIdType.MESH
BF = jnp.bfloat16
F32 = jnp.float32


def shifted(array, axis, by):
    length = lax.axis_size(axis)
    pairs = [(i, i + by) for i in range(length) if 0 <= i + by < length]
    return lax.ppermute(array, axis, pairs)


def segment_of(slot, count, lengths, starts):
    found = jnp.full(slot.shape, -1, jnp.int32)
    for j in range(count):
        inside = (slot >= starts(j)) & (slot < starts(j) + lengths(j))
        found = jnp.where(inside, j, found)
    return jnp.where(slot < 0, -2, found)


def dot_rows(left, right):
    return lax.dot_general(left, right, (((0,), (0,)), ((), ())), preferred_element_type=F32)


def dot_trans(left, right):
    return lax.dot_general(left, right, (((1,), (1,)), ((), ())), preferred_element_type=F32)


def dot(left, right):
    return jnp.dot(left, right, preferred_element_type=F32)


def masks_of(first, block, count, length, start):
    rows = first + block * BLOCK
    query = rows + lax.broadcasted_iota(jnp.int32, (BLOCK, 1), 0)
    keys = rows - WINDOW + lax.broadcasted_iota(jnp.int32, (1, BLOCK + WINDOW), 1)
    seg_q = segment_of(query, count, length, start)
    seg_k = segment_of(keys, count, length, start)
    far = query - keys
    return (far >= 0) & (far <= WINDOW) & (seg_q == seg_k)


def soft_of(query, keys, mask):
    scores = dot_trans(query, keys) * SCALE
    scores = jnp.where(mask, scores, NEG)
    peak = jnp.max(scores, axis=1, keepdims=True)
    exponent = jnp.exp(scores - peak)
    return exponent / jnp.sum(exponent, axis=1, keepdims=True)


def lane_head(width):
    return lax.broadcasted_iota(jnp.int32, (1, width), 1) // HEAD_DIM


def remote(src, dst, send, recv, **peer):
    return pltpu.make_async_remote_copy(
        src_ref=src,
        dst_ref=dst,
        send_sem=send,
        recv_sem=recv,
        device_id=peer,
        device_id_type=MESH_ID,
    )


def greet_group(barrier, size):
    me = lax.axis_index("fsdp")
    for step in range(1, size):
        peer = lax.rem(me + step, size)
        pl.semaphore_signal(barrier, inc=1, device_id={"fsdp": peer}, device_id_type=MESH_ID)


class Group:
    def __init__(self, size):
        self.size = size
        self.me = lax.axis_index("fsdp")
        self.square = size == 4
        if self.square:
            x, y = lax.rem(self.me, 2), self.me // 2
            self.at = lambda bx, by: lax.rem(y + by, 2) * 2 + lax.rem(x + bx, 2)
            self.x, self.y, self.far = self.at(1, 0), self.at(0, 1), self.at(1, 1)

    def from_own(self, step):
        if self.square:
            return self.at(lax.rem(step, 2), step // 2)
        return lax.rem(self.me - step + self.size, self.size)

    def to_own(self, step):
        if self.square:
            return self.at(1 - step // 2, 1 - lax.rem(step, 2))
        return lax.rem(self.me + 1 + step, self.size)


class Gather:
    def __init__(self, group, ref, send, recv):
        self.group, self.ref, self.send, self.recv = group, ref, send, recv
        self.half = ref.shape[1] // 2

    def part(self, k, slot, half, peer):
        view = self.ref.at[slot, pl.ds(half * self.half, self.half)]
        return remote(view, view, self.send.at[k], self.recv.at[k], fsdp=peer)

    def whole(self, k):
        g = self.group
        view = self.ref.at[g.me]
        sems = self.send.at[k - 1], self.recv.at[k - 1]
        return remote(view, view, *sems, fsdp=lax.rem(g.me + k, g.size))

    def copy(self, k):
        g = self.group
        if not g.square:
            return self.whole(k + 1)
        slot = (g.me, g.me, g.me, g.me, g.x, g.y)[k]
        half = (0, 1, 0, 1, 0, 1)[k]
        return self.part(k, slot, half, (g.x, g.x, g.y, g.y, g.y, g.x)[k])

    def start_half(self, half):
        if self.group.square:
            self.copy(half).start()
            self.copy(2 + half).start()
        elif half == 1:
            for k in range(self.group.size - 1):
                self.copy(k).start()

    def relay(self):
        if self.group.square:
            self.copy(0).wait_recv()
            self.copy(4).start()
            self.copy(3).wait_recv()
            self.copy(5).start()

    def ready(self, step):
        if not self.group.square:
            self.copy(step - 1).wait_recv()
        elif step == 3:
            self.copy(4).wait_recv()
            self.copy(5).wait_recv()
        else:
            self.copy(step).wait_recv()

    def finish(self):
        for k in range(transfers(self.group.size)):
            self.copy(k).wait_send()


class Scatter:
    def __init__(self, group, part, first, over, joined, last, send, recv):
        self.group, self.part = group, part
        self.first, self.over, self.joined, self.last = first, over, joined, last
        self.send, self.recv = send, recv
        self.half = part.shape[1] // 2

    def copy(self, k):
        g, half = self.group, self.half
        low, high = pl.ds(0, half), pl.ds(half, half)
        if not g.square:
            src, dst, peer = self.part.at[k], self.first.at[k], lax.rem(g.me + 1 + k, g.size)
        else:
            src, dst, peer = (
                lambda: (self.part.at[0, low], self.over.at[0], g.x),
                lambda: (self.part.at[0, high], self.over.at[1], g.y),
                lambda: (self.part.at[1, low], self.first.at[0], g.x),
                lambda: (self.part.at[2, high], self.first.at[1], g.y),
                lambda: (self.joined.at[0], self.last.at[0], g.y),
                lambda: (self.joined.at[1], self.last.at[1], g.x),
            )[k]()
        return remote(src, dst, self.send.at[k], self.recv.at[k], fsdp=peer)

    def made(self, step):
        if not self.group.square:
            self.copy(step).start()
        elif step == 0:
            self.copy(0).start()
            self.copy(1).start()
        elif step in (1, 2):
            self.copy(step + 1).start()

    def join(self):
        if not self.group.square:
            return
        half = self.half
        for k, (step, rows) in enumerate(((2, slice(0, half)), (1, slice(half, 2 * half)))):
            self.copy(k).wait_recv()
            own = self.part[step, rows].astype(F32)
            self.joined[k] = (own + self.over[k].astype(F32)).astype(BF)
            self.copy(4 + k).start()

    def total(self, half):
        count = self.half
        if self.group.square:
            self.copy(2 + half).wait_recv()
            self.copy(4 + half).wait_recv()
            return self.first[half].astype(F32) + self.last[half].astype(F32)
        if half == 0:
            for k in range(self.group.size - 1):
                self.copy(k).wait_recv()
        rows = slice(half * count, (half + 1) * count)
        out = self.first[0, rows].astype(F32)
        for k in range(1, self.group.size - 1):
            out = out + self.first[k, rows].astype(F32)
        return out

    def finish(self):
        for k in range(transfers(self.group.size)):
            self.copy(k).wait_send()


class Line:
    def __init__(self, parts, sems):
        self.rank = lax.axis_index("seq")
        self.parts, self.length = parts, parts // 2
        self.z, self.core = self.rank // 2, lax.rem(self.rank, 2)
        self.above, self.below = self.rank + 2, self.rank - 2
        self.beside = self.rank + 1 - 2 * self.core
        self.has_above, self.has_below = self.z < self.length - 1, self.z > 0
        self.sems = sems

    def greet(self, barrier):
        def one(peer):
            pl.semaphore_signal(barrier, inc=1, device_id={"seq": peer}, device_id_type=MESH_ID)

        one(self.beside)
        pl.when(self.has_above)(lambda: one(self.above))
        pl.when(self.has_below)(lambda: one(self.below))
        n, z = self.length, self.z
        return 1 + (2 * n - 2 - z) // n + (z + n - 1) // n

    def up(self, k, owner):
        view = self.view(owner)
        return remote(view, view, self.sems[0].at[k], self.sems[1].at[k], seq=self.above)

    def down(self, k, owner):
        view = self.view(owner)
        return remote(view, view, self.sems[2].at[k], self.sems[3].at[k], seq=self.below)

    def side(self, k, owner):
        view = self.view(owner)
        return remote(view, view, self.sems[4].at[k], self.sems[5].at[k], seq=self.beside)

    def gather(self, view):
        self.view = view
        pl.when(self.has_above)(lambda: self.up(0, self.rank).start())
        pl.when(self.has_below)(lambda: self.down(0, self.rank).start())
        self.side(self.z, self.rank).start()

    def own_up(self):
        pl.when(self.has_above)(lambda: self.up(0, self.rank).start())

    def own_down(self):
        pl.when(self.has_below)(lambda: self.down(0, self.rank).start())

    def relay_up(self, j):
        rank, z = self.rank, self.z

        @pl.when((z >= j) & self.has_above)
        def _():
            self.up(j - 1, rank).wait_recv()
            self.up(j, rank - 2 * j).start()
            self.side(z - j, rank - 2 * j).start()

    def relay_down(self, j):
        rank, z = self.rank, self.z

        @pl.when((z + j < self.length) & self.has_below)
        def _():
            self.down(j - 1, rank).wait_recv()
            self.down(j, rank + 2 * j).start()
            self.side(z + j, rank + 2 * j).start()

    def relay(self, j):
        self.relay_up(j)
        self.relay_down(j)

    def close(self, j):
        rank, z = self.rank, self.z

        @pl.when((z >= j) & (z == self.length - 1))
        def _():
            self.up(j - 1, rank).wait_recv()
            self.side(z - j, rank - 2 * j).start()

        @pl.when((z + j < self.length) & (z == 0))
        def _():
            self.down(j - 1, rank).wait_recv()
            self.side(z + j, rank + 2 * j).start()

    def gathered(self):
        for k in range(self.length):
            self.side(k, self.rank).wait_recv()

    def finish(self):
        rank, z = self.rank, self.z
        for k in range(self.length):
            self.side(k, rank).wait_send()
        pl.when(self.has_above)(lambda: self.up(0, rank).wait_send())
        pl.when(self.has_below)(lambda: self.down(0, rank).wait_send())
        for j in range(1, self.length):
            pl.when((z >= j) & self.has_above)(lambda: self.up(j, rank).wait_send())
            pl.when((z + j < self.length) & self.has_below)(lambda: self.down(j, rank).wait_send())


def line_sems(parts):
    return [pltpu.SemaphoreType.DMA((parts // 2,))] * 6


def transfers(size):
    return 6 if size == 4 else size - 1


def scatter_shapes(size, rows, width):
    half = rows // 2
    slots = (2, half, width) if size == 4 else (size - 1, rows, width)
    return [
        pltpu.VMEM((size - 1, rows, width), BF),
        pltpu.VMEM(slots, BF),
        pltpu.VMEM((2, half, width), BF),
        pltpu.VMEM((2, half, width), BF),
        pltpu.VMEM((2, half, width), BF),
        pltpu.SemaphoreType.DMA((transfers(size),)),
        pltpu.SemaphoreType.DMA((transfers(size),)),
    ]


def each_step(size, body):
    def one(step, carry):
        body(step, lambda k: pl.when(step == k))
        return carry

    lax.fori_loop(0, size, one, 0)


FORWARD_REFS = (
    "tokens",
    "edge_tok",
    "grad",
    "gains",
    "table",
    "qkv_piece",
    "gu_piece",
    "out_map",
    "down_map",
    "gated_hbm",
    "qkv_hbm",
    "edge",
    "qkv_map_hbm",
    "middle",
    "heads",
    "grads_hbm",
    "norm_hbm",
    "hidden_hbm",
    "gu_grad_hbm",
    "gu_map_hbm",
    "gains_all",
    "table_all",
    "part",
    "first",
    "over",
    "joined",
    "last",
    "all",
    "grads",
    "qkv",
    "qkv_map",
    "gu_map",
    "tail",
    "own",
    "hidden",
    "gu_grad",
    "s_send",
    "s_recv",
    "a_send",
    "a_recv",
    "g_send",
    "g_recv",
    "c_send",
    "c_recv",
    "m_send",
    "m_recv",
    "halo_send",
    "halo_recv",
    "loads",
    "stores",
    "hidden_store",
    "gu_store",
)


def forward_kernel(size, parts, count, *refs):
    names = FORWARD_REFS
    r = dict(zip(names, refs))
    sems = refs[len(names) :]
    rank = lax.axis_index("seq")
    rows = r["tokens"].shape[0]
    half = rows // 2
    local = r["out_map"].shape[0]
    inner = r["down_map"].shape[0]
    slot = rank * rows
    group = Group(size)
    me = group.me
    line_q, line_u = Line(parts, sems[:6]), Line(parts, sems[6:])

    barrier = pltpu.get_barrier_semaphore()
    greet_group(barrier, size)
    known = line_q.greet(barrier)

    def greet(peer):
        pl.semaphore_signal(barrier, inc=1, device_id={"seq": peer}, device_id_type=MESH_ID)

    pl.when(line_q.has_above & (line_q.core == 1))(lambda: greet(rank + 1))
    pl.when(line_q.has_below & (line_q.core == 0))(lambda: greet(rank - 1))
    n, z = line_q.length, line_q.z
    known = known + (2 * n - 2 - z) // n * line_q.core + (z + n - 1) // n * (1 - line_q.core)
    own_pieces = [
        pltpu.make_async_copy(src.at[me], dst.at[me, rank], r["loads"].at[k])
        for k, (src, dst) in enumerate(
            ((r["qkv_piece"], r["qkv_map"]), (r["gu_piece"], r["gu_map"]))
        )
    ]
    for copy in own_pieces:
        copy.start()
    r["gains_all"][me] = r["gains"][...]
    r["table_all"][me] = r["table"][...]
    r["grads"][me] = r["grad"][...]
    pl.semaphore_wait(barrier, size - 1 + known)

    def swap(k, step):
        peer = lax.rem(me + step, size)
        src, dst = (
            lambda: (r["gains_all"].at[me], r["gains_all"].at[me]),
            lambda: (r["table_all"].at[me], r["table_all"].at[me]),
            lambda: (r["qkv_piece"].at[peer], r["qkv_map"].at[me, rank]),
            lambda: (r["gu_piece"].at[peer], r["gu_map"].at[me, rank]),
        )[k]()
        return remote(src, dst, r["m_send"].at[k, step - 1], r["m_recv"].at[k, step - 1], fsdp=peer)

    others = range(1, size)
    for k in range(4):
        for step in others:
            swap(k, step).start()
    for k in range(2):
        for step in others:
            swap(k, step).wait_recv()

    gains = jnp.concatenate([r["gains_all"][f] for f in range(size)], 1).astype(F32)
    own_table = r["table_all"][me]
    slots = slot + lax.broadcasted_iota(jnp.int32, (rows, 1), 0)
    length = lambda j: own_table[0:1, j : j + 1]
    start = lambda j: own_table[1:2, j : j + 1]
    segment = segment_of(slots, count, length, start)
    same_one = (segment == segment_of(slots - 1, count, length, start)).astype(F32)
    same_two = (segment == segment_of(slots - 2, count, length, start)).astype(F32)
    tokens = r["tokens"][...].astype(F32)
    edge = r["edge_tok"][...].astype(F32)

    def norm(a):
        return a * lax.rsqrt(jnp.mean(a * a, axis=1, keepdims=True) + EPS) * gains[0:1]

    normed, edge = norm(tokens), norm(edge)
    row = lax.broadcasted_iota(jnp.int32, (rows, 1), 0)
    back_one = jnp.where(row == 0, edge[1:2], pltpu.roll(normed, 1, 0))
    back_two = jnp.where(
        row == 0, edge[0:1], jnp.where(row == 1, edge[1:2], pltpu.roll(normed, 2, 0))
    )
    mixed = (
        normed * gains[2:3]
        + same_one * back_one * gains[3:4]
        + same_two * back_two * gains[4:5]
    )
    all_ref = r["all"]
    all_ref[me] = (mixed * normed).astype(BF)
    gather = Gather(group, all_ref, r["a_send"], r["a_recv"])
    gather.start_half(0)
    gather.start_half(1)

    own_pieces[0].wait()
    for step in others:
        swap(2, step).wait_recv()
    line_q.gather(lambda owner: r["qkv_map"].at[:, owner])
    line_u.view = lambda owner: r["gu_map"].at[:, owner]
    gather.relay()
    grads = Gather(group, r["grads"], r["c_send"], r["c_recv"])
    grads.start_half(0)
    grads.start_half(1)
    own_pieces[1].wait()
    for step in others:
        swap(3, step).wait_recv()
    line_u.side(z, rank).start()
    pl.when(z == 0)(line_u.own_up)
    pl.when(z == n - 1)(line_u.own_down)
    for j in range(1, n):
        line_q.relay(j)
        line_q.close(j)
        pl.when(z == j)(line_u.own_up)
        pl.when(z == n - 1 - j)(line_u.own_down)
    for step in others:
        gather.ready(step)
    grads.relay()
    line_q.gathered()
    keeps = [
        pltpu.make_async_copy(all_ref, r["gated_hbm"], r["stores"].at[size]),
        pltpu.make_async_copy(r["qkv_map"], r["qkv_map_hbm"], r["stores"].at[size + 1]),
    ]
    for keep in keeps:
        keep.start()

    weights = r["qkv_map"][...].reshape(-1, r["qkv_map"].shape[3])

    def halo(step):
        g = group.to_own(step)
        sem = r["halo_send"].at[step], r["halo_recv"].at[step]
        return remote(r["tail"].at[g], r["edge"].at[g], *sem, seq=rank + 1)

    def project(step, is_step):
        g = group.to_own(step)
        out = dot(all_ref[g], weights).astype(BF)
        r["qkv"][g] = out
        r["tail"][g] = out[rows - WINDOW :, local:]
        pl.when(rank < parts - 1)(lambda: halo(step).start())

    each_step(size, project)

    @pl.when(rank == 0)
    def _():
        r["edge"][...] = jnp.zeros_like(r["edge"])

    keeps.append(pltpu.make_async_copy(r["qkv"], r["qkv_hbm"], r["stores"].at[size + 2]))
    keeps[2].start()
    line_u.relay(1)
    gather.finish()
    keeps[0].wait()

    scatter = Scatter(
        group, *(r[k] for k in ("part", "first", "over", "joined", "last", "s_send", "s_recv"))
    )
    head_of = lane_head(local)

    def mix(step, is_step):
        g = group.to_own(step)
        pl.when(rank > 0)(lambda: halo(step).wait_recv())
        own, edge, table = r["qkv"][g], r["edge"][g], r["table_all"][g]
        queries = own[:, :local]
        keys = jnp.concatenate([edge[:, :local], own[:, local : 2 * local]], 0)
        values = jnp.concatenate([edge[:, local:], own[:, 2 * local :]], 0)
        outs = []
        for block in range(rows // BLOCK):
            mask = masks_of(
                slot,
                block,
                count,
                lambda j: table[0:1, j : j + 1],
                lambda j: table[1:2, j : j + 1],
            )
            low = block * BLOCK
            query = queries[low : low + BLOCK]
            key = keys[low : low + BLOCK + WINDOW]
            value = values[low : low + BLOCK + WINDOW]
            out = jnp.zeros((BLOCK, local), F32)
            for head in range(local // HEAD_DIM):
                mine = head_of == head
                soft = soft_of(jnp.where(mine, query, jnp.zeros_like(query)), key, mask)
                out = jnp.where(mine, dot(soft.astype(BF), value), out)
            outs.append(out.astype(BF))
        heads = jnp.concatenate(outs, 0)
        r["heads"][g] = heads
        branch = dot(heads, r["out_map"][...])
        is_step(size - 1)(lambda: r["own"].__setitem__(..., branch))
        pl.when(step < size - 1)(lambda: r["part"].__setitem__(step, branch.astype(BF)))
        for k in range(size - 1):
            is_step(k)(functools.partial(scatter.made, k))

    each_step(size, mix)
    scatter.join()
    for j in range(2, n):
        line_u.relay(j)
    gather = Gather(group, all_ref, r["g_send"], r["g_recv"])
    for h in range(2):
        span = slice(h * half, (h + 1) * half)
        total = r["own"][span, :] + scatter.total(h)
        middle = r["tokens"][span, :].astype(F32) + total
        r["middle"][span, :] = middle
        scale = lax.rsqrt(jnp.mean(middle * middle, axis=1, keepdims=True) + EPS)
        all_ref[me, span] = (middle * scale * gains[1:2]).astype(BF)
        gather.start_half(h)
    gather.relay()
    for j in range(1, n):
        line_u.close(j)
    line_u.gathered()
    keeps.append(pltpu.make_async_copy(r["gu_map"], r["gu_map_hbm"], r["stores"].at[size + 3]))
    keeps[3].start()

    def out_copies(step):
        g, two = group.from_own(step), lax.rem(step, 2)
        return (
            pltpu.make_async_copy(
                r["hidden"].at[two], r["hidden_hbm"].at[g], r["hidden_store"].at[two]
            ),
            pltpu.make_async_copy(
                r["gu_grad"].at[two], r["gu_grad_hbm"].at[g], r["gu_store"].at[two]
            ),
        )

    def norm_copy(g):
        return pltpu.make_async_copy(all_ref.at[g], r["norm_hbm"].at[g], r["stores"].at[g])

    def feed(step, is_step):
        g, two = group.from_own(step), lax.rem(step, 2)
        for k in others:
            is_step(k)(functools.partial(gather.ready, k))
            is_step(k)(functools.partial(grads.ready, k))

        @pl.when(step >= 2)
        def _():
            for copy in out_copies(step - 2):
                copy.wait()

        norm_copy(g).start()
        weights = r["gu_map"][...].reshape(-1, r["gu_map"].shape[3])
        acts = dot(all_ref[g], weights)
        gate, up = acts[:, :inner], acts[:, inner:]
        sigma = jax.nn.sigmoid(gate)
        silu = gate * sigma
        r["hidden"][two] = (silu * up).astype(BF)
        grad_hidden = dot_trans(r["grads"][g], r["down_map"][...])
        grad_gate = grad_hidden * up * sigma * (1.0 + gate * (1.0 - sigma))
        r["gu_grad"][two] = jnp.concatenate([grad_gate, grad_hidden * silu], 1).astype(BF)
        for copy in out_copies(step):
            copy.start()

    each_step(size, feed)
    keeps.append(pltpu.make_async_copy(r["grads"], r["grads_hbm"], r["stores"].at[size + 4]))
    keeps[4].start()
    for k in range(4):
        for step in others:
            swap(k, step).wait_send()
    scatter.finish()
    gather.finish()
    grads.finish()
    line_q.finish()
    line_u.finish()

    @pl.when(rank < parts - 1)
    def _():
        for step in range(size):
            halo(step).wait_send()

    for keep in keeps[1:]:
        keep.wait()
    for g in range(size):
        norm_copy(g).wait()
    for step in (size - 2, size - 1):
        for copy in out_copies(step):
            copy.wait()


def forward_part(ident, count, tokens, edge, grad, gains, table, qkv_piece, gu_piece, out_weight, down_weight):
    size, parts = lax.axis_size("fsdp"), lax.axis_size("seq")
    rows, width = tokens.shape
    local, inner = out_weight.shape[0], down_weight.shape[0]
    piece, cols = gu_piece.shape[1:]
    vmem = pl.BlockSpec(memory_space=pltpu.VMEM)
    hbm = pl.BlockSpec(memory_space=pl.ANY)
    shape = lambda w: (size, rows, w)
    low = lambda s: jax.ShapeDtypeStruct(s, BF)
    maps = [(size, parts, piece, 3 * local), (size, parts, piece, cols)]
    dma = lambda *s: pltpu.SemaphoreType.DMA(s)
    hop = transfers(size)
    scratch = scatter_shapes(size, rows, width)
    return pl.pallas_call(
        functools.partial(forward_kernel, size, parts, count),
        out_shape=[
            low(shape(width)),
            low(shape(3 * local)),
            low((size, WINDOW, 2 * local)),
            low(maps[0]),
            jax.ShapeDtypeStruct((rows, width), F32),
            low(shape(local)),
            low(shape(width)),
            low(shape(width)),
            low(shape(inner)),
            low(shape(cols)),
            low(maps[1]),
            low((size,) + gains.shape),
            jax.ShapeDtypeStruct((size,) + table.shape, jnp.int32),
        ],
        in_specs=[vmem] * 5 + [hbm, hbm, vmem, vmem],
        out_specs=[hbm, hbm, vmem, hbm, vmem, vmem, hbm, hbm, hbm, hbm, hbm, vmem, vmem],
        scratch_shapes=scratch[:-2]
        + [
            pltpu.VMEM(shape(width), BF),
            pltpu.VMEM(shape(width), BF),
            pltpu.VMEM(shape(3 * local), BF),
            pltpu.VMEM(maps[0], BF),
            pltpu.VMEM(maps[1], BF),
            pltpu.VMEM((size, WINDOW, 2 * local), BF),
            pltpu.VMEM((rows, width), F32),
            pltpu.VMEM((2, rows, inner), BF),
            pltpu.VMEM((2, rows, cols), BF),
        ]
        + [dma(hop)] * 8
        + [dma(4, size - 1)] * 2
        + [dma(size)] * 2
        + [dma(2), dma(size + 5), dma(2), dma(2)]
        + line_sems(parts)
        + line_sems(parts),
        compiler_params=pltpu.CompilerParams(
            collective_id=ident, has_side_effects=True, vmem_limit_bytes=67_000_000
        ),
        cost_estimate=pl.CostEstimate(
            flops=2 * size * rows * width * (4 * local + 3 * inner),
            bytes_accessed=500_000_000,
            transcendentals=0,
        ),
        name="forward_part",
    )(tokens, edge, grad, gains, table, qkv_piece, gu_piece, out_weight, down_weight)


def heads_back(group, slot, count, lens_ref, starts_ref, own, edge, grad):
    rows, local = own.shape[0], own.shape[1] // 3
    head_of = lane_head(local)
    queries = own[:, :local]
    keys = jnp.concatenate([edge[:, :local], own[:, local : 2 * local]], 0)
    values = jnp.concatenate([edge[:, local:], own[:, 2 * local :]], 0)
    dqs, dks, dvs = [], [], []
    for block in range(rows // BLOCK):
        mask = masks_of(
            slot, block, count, lambda j: lens_ref[group, j], lambda j: starts_ref[group, j]
        )
        low = block * BLOCK
        span = slice(low, low + BLOCK + WINDOW)
        query, grads = queries[low : low + BLOCK], grad[low : low + BLOCK]
        key, value = keys[span], values[span]
        dq = jnp.zeros((BLOCK, local), F32)
        dk = jnp.zeros((BLOCK + WINDOW, local), F32)
        dv = jnp.zeros((BLOCK + WINDOW, local), F32)
        for head in range(local // HEAD_DIM):
            mine = head_of == head
            own_q = jnp.where(mine, query, jnp.zeros_like(query))
            own_g = jnp.where(mine, grads, jnp.zeros_like(grads))
            soft = soft_of(own_q, key, mask)
            grad_soft = dot_trans(own_g, value)
            total = jnp.sum(grad_soft * soft, axis=1, keepdims=True)
            grad_scores = (soft * (grad_soft - total)).astype(BF)
            dq = jnp.where(mine, dot(grad_scores, key), dq)
            dk = dk + dot_rows(grad_scores, own_q)
            dv = dv + dot_rows(soft.astype(BF), own_g)
        dqs.append(dq * SCALE)
        dks.append(dk * SCALE)
        dvs.append(dv)

    def joined(pieces):
        out = [pieces[0][:BLOCK]]
        for left, right in zip(pieces, pieces[1:]):
            out.append(left[BLOCK:] + right[:WINDOW])
            out.append(right[WINDOW:BLOCK])
        out.append(pieces[-1][BLOCK:])
        return jnp.concatenate(out, 0)

    return jnp.concatenate(dqs, 0), joined(dks), joined(dvs)


def back_kernel(size, parts, count, lens_ref, starts_ref, grad_gu_hbm, gu_map_hbm, middle_ref, grad_ref,
                gain_ref, out_map_ref, edge_ref, qkv_ref, qkv_map_hbm,
                grad_middle_ref, norm_ref, all_ref, dqkv_ref, own_ref,
                part, first, over, joined, last, s_send, s_recv, t_send, t_recv, g_send, g_recv,
                grad_gu_ref, gu_map_ref, qkv_map_ref, dedge_ref, back_ref, tail_ref, h_send, h_recv, loads):
    rows = middle_ref.shape[0]
    local = out_map_ref.shape[0]
    rank = lax.axis_index("seq")
    slot = rank * rows
    group = Group(size)
    barrier = pltpu.get_barrier_semaphore()
    greet_group(barrier, size)

    def greet(peer):
        pl.semaphore_signal(barrier, inc=1, device_id={"seq": peer}, device_id_type=MESH_ID)

    pl.when(rank > 0)(lambda: greet(rank - 1))
    pl.when(rank < parts - 1)(lambda: greet(rank + 1))
    fetches = [
        pltpu.make_async_copy(src, dst, loads.at[k])
        for k, (src, dst) in enumerate(
            ((grad_gu_hbm, grad_gu_ref), (gu_map_hbm, gu_map_ref), (qkv_map_hbm, qkv_map_ref))
        )
    ]
    for fetch in fetches:
        fetch.start()
    has_next = (2 * parts - 2 - rank) // parts
    has_last = (rank + parts - 1) // parts
    pl.semaphore_wait(barrier, size - 1 + has_next + has_last)
    scatter = Scatter(group, part, first, over, joined, last, s_send, s_recv)
    gather = Gather(group, all_ref, g_send, g_recv)
    fetches[0].wait()
    fetches[1].wait()

    def step_two(step, is_step):
        partial = dot_trans(grad_gu_ref[group.to_own(step)], gu_map_ref[...])
        is_step(size - 1)(lambda: own_ref.__setitem__(..., partial))
        pl.when(step < size - 1)(lambda: part.__setitem__(step, partial.astype(BF)))
        for k in range(size - 1):
            is_step(k)(functools.partial(scatter.made, k))

    each_step(size, step_two)
    scatter.join()
    half = rows // 2
    norm_sum = jnp.zeros((1, middle_ref.shape[1]), F32)
    for h in range(2):
        span = slice(h * half, (h + 1) * half)
        grad = own_ref[span, :] + scatter.total(h)
        middle = middle_ref[span, :]
        scale = lax.rsqrt(jnp.mean(middle * middle, axis=1, keepdims=True) + EPS)
        unit = middle * scale
        scaled = grad * gain_ref[...]
        norm_sum = norm_sum + jnp.sum(grad * unit, axis=0, keepdims=True)
        grad_out = grad_ref[span, :].astype(F32)
        grad_middle = grad_out + scale * (
            scaled - unit * jnp.mean(scaled * unit, axis=1, keepdims=True)
        )
        grad_middle_ref[span, :] = grad_middle
        all_ref[group.me, span] = grad_middle.astype(BF)
        gather.start_half(h)
    norm_ref[...] = norm_sum

    def halo(step):
        g = group.from_own(step)
        sems = h_send.at[step], h_recv.at[step]
        return remote(dedge_ref.at[g], back_ref.at[g], *sems, seq=rank - 1)

    def step_heads(step, is_step):
        g = group.from_own(step)

        @is_step(1)
        def _():
            gather.relay()

        for k in range(1, size):
            is_step(k)(functools.partial(gather.ready, k))
        grad = dot_trans(all_ref[g], out_map_ref[...]).astype(BF)
        dq, dk, dv = heads_back(
            g, slot, count, lens_ref, starts_ref, qkv_ref[g], edge_ref[g], grad
        )
        dedge_ref[g] = jnp.concatenate([dk[:WINDOW], dv[:WINDOW]], 1).astype(BF)
        full = jnp.concatenate([dq, dk[WINDOW:], dv[WINDOW:]], 1)
        dqkv_ref[g] = full.astype(BF)
        tail_ref[g] = full[rows - WINDOW :]
        pl.when(rank > 0)(lambda: halo(step).start())

    each_step(size, step_heads)
    scatter.finish()
    fetches[2].wait()

    @pl.when(rank == parts - 1)
    def _():
        back_ref[...] = jnp.zeros_like(back_ref)

    @pl.when(rank < parts - 1)
    def _():
        for step in range(size):
            halo(step).wait_recv()

    scatter = Scatter(group, part, first, over, joined, last, t_send, t_recv)

    def step_one(step, is_step):
        g = group.to_own(step)
        back = back_ref[g].astype(F32)
        wide = jnp.concatenate([jnp.zeros((WINDOW, local), F32), back], 1)
        dqkv_ref[g, pl.ds(rows - WINDOW, WINDOW)] = (tail_ref[g] + wide).astype(BF)
        partial = dot_trans(dqkv_ref[g], qkv_map_ref[...])
        is_step(size - 1)(lambda: own_ref.__setitem__(..., partial))
        pl.when(step < size - 1)(lambda: part.__setitem__(step, partial.astype(BF)))
        for k in range(size - 1):
            is_step(k)(functools.partial(scatter.made, k))

    each_step(size, step_one)
    scatter.join()
    for h in range(2):
        span = slice(h * half, (h + 1) * half)
        own_ref[span, :] = own_ref[span, :] + scatter.total(h)
    scatter.finish()
    gather.finish()

    @pl.when(rank > 0)
    def _():
        for step in range(size):
            halo(step).wait_send()


def back_part(ident, lens, starts, grad_gu, gu_map, middle, grad, gain, out_weight, edge, qkv, qkv_map):
    size, parts = lax.axis_size("fsdp"), lax.axis_size("seq")
    rows, width = middle.shape
    local = out_weight.shape[0]
    vmem = pl.BlockSpec(memory_space=pltpu.VMEM)
    smem = pl.BlockSpec(memory_space=pltpu.SMEM)
    hbm = pl.BlockSpec(memory_space=pl.ANY)
    sems = [pltpu.SemaphoreType.DMA((transfers(size),))] * 2
    return pl.pallas_call(
        functools.partial(back_kernel, size, parts, lens.shape[1]),
        out_shape=[
            jax.ShapeDtypeStruct((rows, width), F32),
            jax.ShapeDtypeStruct((1, width), F32),
            jax.ShapeDtypeStruct((size, rows, width), BF),
            jax.ShapeDtypeStruct(qkv.shape, BF),
            jax.ShapeDtypeStruct((rows, width), F32),
        ],
        in_specs=[smem, smem, hbm, hbm] + [vmem] * 6 + [hbm],
        out_specs=[vmem] * 5,
        scratch_shapes=scatter_shapes(size, rows, width)
        + sems
        + sems
        + [
            pltpu.VMEM(grad_gu.shape, BF),
            pltpu.VMEM(gu_map.shape, BF),
            pltpu.VMEM(qkv_map.shape, BF),
            pltpu.VMEM((size, WINDOW, 2 * local), BF),
            pltpu.VMEM((size, WINDOW, 2 * local), BF),
            pltpu.VMEM((size, WINDOW, 3 * local), F32),
            pltpu.SemaphoreType.DMA((size,)),
            pltpu.SemaphoreType.DMA((size,)),
            pltpu.SemaphoreType.DMA((3,)),
        ],
        compiler_params=pltpu.CompilerParams(
            collective_id=ident, has_side_effects=True, vmem_limit_bytes=67_000_000
        ),
        cost_estimate=pl.CostEstimate(
            flops=2 * size * rows * (gu_map.size + qkv_map.size + width * local),
            bytes_accessed=400_000_000,
            transcendentals=0,
        ),
        name="back_part",
    )(lens, starts, grad_gu, gu_map, middle, grad, gain, out_weight, edge, qkv, qkv_map)


class LineSum:
    def __init__(self, line, x, pre, acc, up_in, down_in, sems):
        self.line, self.x, self.pre, self.acc = line, x, pre, acc
        self.up_in, self.down_in, self.sems = up_in, down_in, sems

    def share(self, k):
        line = self.line
        src = self.x.at[2 * k + 1 - line.core]
        return remote(src, self.pre.at[k], self.sems[0].at[k], self.sems[1].at[k], seq=line.beside)

    def up(self, k):
        sems = self.sems[2].at[k], self.sems[3].at[k]
        return remote(self.acc.at[k], self.up_in.at[k], *sems, seq=self.line.above)

    def down(self, k):
        sems = self.sems[4].at[k], self.sems[5].at[k]
        return remote(self.acc.at[k], self.down_in.at[k], *sems, seq=self.line.below)

    def order(self):
        n = self.line.length
        return [k // 2 if k % 2 else n - 1 - k // 2 for k in range(n)]

    def trade(self):
        for k in self.order():
            self.share(k).start()

    def merge(self):
        line = self.line
        for k in self.order():
            self.share(k).wait_recv()
            own = self.x[2 * k + line.core].astype(F32)
            self.acc[k] = (own + self.pre[k].astype(F32)).astype(BF)
            if k > 0:
                pl.when(line.z == 0)(lambda: self.up(k).start())
            if k < line.length - 1:
                pl.when(line.z == line.length - 1)(lambda: self.down(k).start())

    def add(self, k, more):
        self.acc[k] = (self.acc[k].astype(F32) + more[k].astype(F32)).astype(BF)

    def pass_up(self, k):
        z = self.line.z

        @pl.when((z > 0) & (z < k))
        def _():
            self.up(k).wait_recv()
            self.add(k, self.up_in)
            self.up(k).start()

    def pass_down(self, k):
        z = self.line.z

        @pl.when((z < self.line.length - 1) & (z > k))
        def _():
            self.down(k).wait_recv()
            self.add(k, self.down_in)
            self.down(k).start()

    def total(self):
        z = self.line.z

        @pl.when(z > 0)
        def _():
            self.up(z).wait_recv()
            self.add(z, self.up_in)

        @pl.when(z < self.line.length - 1)
        def _():
            self.down(z).wait_recv()
            self.add(z, self.down_in)

    def finish(self):
        for k in range(self.line.length):
            self.share(k).wait_send()
            pl.when(k > self.line.z)(lambda: self.up(k).wait_send())
            pl.when(k < self.line.z)(lambda: self.down(k).wait_send())


CLOSE_REFS = (
    "x",
    "gu_piece",
    "terms",
    "hidden",
    "down_map",
    "every_hbm",
    "gu_every_hbm",
    "feed",
    "terms_out",
    "part",
    "first",
    "over",
    "joined",
    "last",
    "pre",
    "acc",
    "up_in",
    "down_in",
    "every",
    "slots",
    "gu_every",
    "terms_in",
    "terms_all",
    "s_send",
    "s_recv",
    "m_send",
    "m_recv",
    "t_send",
    "t_recv",
    "loads",
)


def close_kernel(size, parts, *refs):
    r = dict(zip(CLOSE_REFS, refs))
    sems = refs[len(CLOSE_REFS) :]
    rank = lax.axis_index("seq")
    group = Group(size)
    me = group.me
    line_u, line_q = Line(parts, sems[:6]), Line(parts, sems[6:12])
    n, z = line_q.length, line_q.z
    sums = LineSum(line_q, *(r[k] for k in ("x", "pre", "acc", "up_in", "down_in")), sems[12:])
    rows = r["feed"].shape[0]
    half = rows // 2
    barrier = pltpu.get_barrier_semaphore()
    greet_group(barrier, size)
    for step in range(1, parts):
        peer = lax.rem(rank + step, parts)
        pl.semaphore_signal(barrier, inc=1, device_id={"seq": peer}, device_id_type=MESH_ID)
    own_piece = pltpu.make_async_copy(
        r["gu_piece"].at[me], r["gu_every"].at[rank, me], r["loads"].at[0]
    )
    own_piece.start()
    r["terms_in"][me] = r["terms"][me]
    pl.semaphore_wait(barrier, size + parts - 2)
    sums.trade()

    def swap(k, step):
        peer = lax.rem(me + step, size)
        src, dst = (
            lambda: (r["gu_piece"].at[peer], r["gu_every"].at[rank, me]),
            lambda: (r["terms"].at[peer], r["terms_in"].at[me]),
            lambda: (r["acc"].at[z, peer], r["slots"].at[me]),
        )[k]()
        return remote(src, dst, r["m_send"].at[k, step - 1], r["m_recv"].at[k, step - 1], fsdp=peer)

    others = range(1, size)
    for k in range(2):
        for step in others:
            swap(k, step).start()

    scatter = Scatter(
        group, *(r[k] for k in ("part", "first", "over", "joined", "last", "s_send", "s_recv"))
    )

    def down(step, is_step):
        partial = dot(r["hidden"][group.to_own(step)], r["down_map"][...])
        is_step(size - 1)(lambda: r["feed"].__setitem__(..., partial))
        pl.when(step < size - 1)(lambda: r["part"].__setitem__(step, partial.astype(BF)))
        for k in range(size - 1):
            is_step(k)(functools.partial(scatter.made, k))

    each_step(size, down)
    sums.merge()
    own_piece.wait()
    for step in others:
        swap(0, step).wait_recv()
    line_u.gather(lambda owner: r["gu_every"].at[owner])

    for step in others:
        swap(1, step).wait_recv()
    small = r["terms_in"][0]
    for f in others:
        small = small + r["terms_in"][f]
    r["terms_all"][rank] = small

    def spread(step):
        peer = lax.rem(rank + step, parts)
        view = r["terms_all"].at[rank]
        return remote(view, view, r["t_send"].at[step - 1], r["t_recv"].at[step - 1], seq=peer)

    for step in range(1, parts):
        spread(step).start()
    scatter.join()

    for k in range(n - 1):
        sums.pass_up(n - 1 - k)
        sums.pass_down(k)
        if k == 0:
            pl.when(z >= 2)(lambda: line_u.relay_up(1))
            pl.when(z <= n - 3)(lambda: line_u.relay_down(1))
    sums.total()
    for step in others:
        swap(2, step).start()
    for h in range(2):
        span = slice(h * half, (h + 1) * half)
        r["feed"][span, :] = r["feed"][span, :] + scatter.total(h)
    pl.when(z < 2)(lambda: line_u.relay_up(1))
    pl.when(z > n - 3)(lambda: line_u.relay_down(1))
    r["slots"][me] = r["acc"][z, me]
    for step in others:
        swap(2, step).wait_recv()
    local = r["x"].shape[3] // 4
    lane = lax.broadcasted_iota(jnp.int32, (1, 1, 4 * local), 2)
    r["every"][rank] = jnp.where(lane < 3 * local, r["slots"][...], r["acc"][z])
    line_q.gather(lambda owner: r["every"].at[owner])
    for j in range(2, n):
        line_u.relay(j)
        line_q.relay(j - 1)
    for j in range(1, n):
        line_u.close(j)
    line_u.gathered()
    stores = [pltpu.make_async_copy(r["gu_every"], r["gu_every_hbm"], r["loads"].at[0])]
    stores[0].start()
    line_q.relay(n - 1)
    for j in range(1, n):
        line_q.close(j)
    line_q.gathered()
    stores.append(pltpu.make_async_copy(r["every"], r["every_hbm"], r["loads"].at[1]))
    stores[1].start()
    for step in range(1, parts):
        spread(step).wait_recv()
    small = r["terms_all"][0]
    for k in range(1, parts):
        small = small + r["terms_all"][k]
    r["terms_out"][...] = small
    for k in range(3):
        for step in others:
            swap(k, step).wait_send()
    for step in range(1, parts):
        spread(step).wait_send()
    scatter.finish()
    sums.finish()
    line_u.finish()
    line_q.finish()
    for store in stores:
        store.wait()


def close_part(ident, packed, gu_piece, terms, hidden, down_weight):
    parts, size, piece, cols = packed.shape
    n = parts // 2
    rows, width = hidden.shape[1], down_weight.shape[1]
    vmem = pl.BlockSpec(memory_space=pltpu.VMEM)
    hbm = pl.BlockSpec(memory_space=pl.ANY)
    dma = lambda *s: pltpu.SemaphoreType.DMA(s)
    gu_shape = (parts,) + gu_piece.shape
    scratch = scatter_shapes(size, rows, width)
    chips = pltpu.VMEM((n, size, piece, cols), BF)
    return pl.pallas_call(
        functools.partial(close_kernel, size, parts),
        out_shape=[
            jax.ShapeDtypeStruct(packed.shape, BF),
            jax.ShapeDtypeStruct(gu_shape, BF),
            jax.ShapeDtypeStruct((rows, width), F32),
            jax.ShapeDtypeStruct(terms.shape[1:], F32),
        ],
        in_specs=[vmem, hbm, vmem, vmem, vmem],
        out_specs=[hbm, hbm, vmem, vmem],
        scratch_shapes=scratch[:-2]
        + [
            chips,
            chips,
            chips,
            chips,
            pltpu.VMEM(packed.shape, BF),
            pltpu.VMEM((size, piece, cols), BF),
            pltpu.VMEM(gu_shape, BF),
            pltpu.VMEM(terms.shape, F32),
            pltpu.VMEM((parts,) + terms.shape[1:], F32),
        ]
        + scratch[-2:]
        + [dma(3, size - 1)] * 2
        + [dma(parts - 1)] * 2
        + [dma(2)]
        + line_sems(parts) * 3,
        compiler_params=pltpu.CompilerParams(
            collective_id=ident, has_side_effects=True, vmem_limit_bytes=67_000_000
        ),
        cost_estimate=pl.CostEstimate(
            flops=2 * size * rows * down_weight.size, bytes_accessed=500_000_000, transcendentals=0
        ),
        name="close_part",
    )(packed, gu_piece, terms, hidden, down_weight)


def pack_kernel(size, parts, x_ref, g_ref, *refs):
    out_ref = refs[-1]
    full = dot_rows(x_ref[...], g_ref[...])
    pair = out_ref.shape[1]
    rows = full.shape[0] // pair
    piece = rows // parts
    for k in range(pair):
        own = full[k * rows : (k + 1) * rows]
        if len(refs) == 3:
            heads_ref, gb_ref = refs[0], refs[1]
            side = dot_rows(heads_ref[...], gb_ref[...])
            wide = side.shape[1] // pair
            own = jnp.concatenate([own, side[:, k * wide : (k + 1) * wide]], 1)
        out_ref[:, k] = own.astype(BF).reshape(parts, piece, own.shape[1])


def pack_grads(parts, size, x, g, heads=None, gb=None):
    width, cols = x.shape[1], g.shape[1]
    rows = width // size
    piece = rows // parts
    if piece % 8 or (2 * rows) % 128:
        full = dot_rows(x, g).reshape(size, parts, piece, cols)
        if heads is not None:
            side = dot_rows(heads, gb).reshape(parts, piece, size, -1).transpose(2, 0, 1, 3)
            full = jnp.concatenate([full, side], 3)
        return full.transpose(1, 0, 2, 3).astype(BF)
    total = x.shape[0]
    pair = pl.BlockSpec((total, 2 * rows), lambda i: (0, i))
    whole = lambda a: pl.BlockSpec(a.shape, lambda i: (0, 0), pipeline_mode=pl.Buffered(1))
    args, specs = [x, g], [pair, whole(g)]
    out_cols = cols
    if heads is not None:
        args += [heads, gb]
        specs += [whole(heads), pair]
        out_cols += rows
    return pl.pallas_call(
        functools.partial(pack_kernel, size, parts),
        grid=(size // 2,),
        out_shape=jax.ShapeDtypeStruct((parts, size, piece, out_cols), BF),
        in_specs=specs,
        out_specs=pl.BlockSpec((parts, 2, piece, out_cols), lambda i: (0, i, 0, 0)),
        cost_estimate=pl.CostEstimate(
            flops=2 * total * width * out_cols,
            bytes_accessed=2 * (x.size + g.size + width * out_cols),
            transcendentals=0,
        ),
        name="pack_grads",
    )(*args)


def unpack_kernel(widths, every_ref, *outs):
    size = every_ref.shape[1]
    blocks = [every_ref[0, i].astype(F32) for i in range(size)]
    low = 0
    for width, out in zip(widths, outs):
        out[...] = jnp.concatenate([b[:, low : low + width] for b in blocks], 1)
        low += width


def unpack_grads(every, widths):
    parts, size, piece, cols = every.shape
    if piece % 8:
        outs, low = [], 0
        for width in widths:
            block = every[:, :, :, low : low + width].transpose(0, 2, 1, 3)
            outs.append(block.reshape(parts * piece, size * width).astype(F32))
            low += width
        return outs
    return pl.pallas_call(
        functools.partial(unpack_kernel, widths),
        grid=(parts,),
        out_shape=[jax.ShapeDtypeStruct((parts * piece, size * w), F32) for w in widths],
        in_specs=[pl.BlockSpec((1, size, piece, cols), lambda i: (i, 0, 0, 0))],
        out_specs=[pl.BlockSpec((piece, size * w), lambda i: (i, 0)) for w in widths],
        cost_estimate=pl.CostEstimate(flops=0, bytes_accessed=every.size * 6, transcendentals=0),
        name="unpack_grads",
    )(every)


def columns_piece(weights, part, parts):
    size = lax.axis_size("fsdp")
    rows = weights[0].shape[0] // parts
    pieces = []
    for weight in weights:
        own = lax.dynamic_slice_in_dim(weight, part * rows, rows, 0)
        pieces.append(own.reshape(rows, size, -1))
    return jnp.concatenate(pieces, 2).transpose(1, 0, 2)


def shards(
    tokens,
    seq_lengths,
    seq_offsets,
    norm1_gain,
    conv_weight,
    query_weight,
    key_weight,
    value_weight,
    out_weight,
    norm2_gain,
    gate_weight,
    up_weight,
    down_weight,
    cotangent,
):
    size = lax.axis_size("fsdp")
    parts = lax.axis_size("seq")
    part = lax.axis_index("seq")
    me = lax.axis_index("fsdp")
    own_tokens = tokens[0]
    rows, width = own_tokens.shape
    slice_width = norm1_gain.shape[0]
    first_slot = part * rows
    count = seq_lengths.shape[1]

    slot_ext = first_slot - 2 + jnp.arange(rows + 2, dtype=jnp.int32)
    segment_ext = segment_of(
        slot_ext, count, lambda j: seq_lengths[0, j], lambda j: seq_offsets[0, j]
    )
    segment_own = segment_ext[2:]
    same_one = (segment_own == segment_ext[1:-1]).astype(F32)[:, None]
    same_two = (segment_own == segment_ext[:-2]).astype(F32)[:, None]
    live_mask = (segment_own >= 0).astype(F32)[:, None]

    gains = jnp.concatenate(
        [
            norm1_gain[None],
            norm2_gain[None],
            conv_weight.T,
            jnp.zeros((3, slice_width), BF),
        ],
        0,
    )
    table = jnp.zeros((8, 128), jnp.int32)
    table = table.at[0, :count].set(seq_lengths[0]).at[1, :count].set(seq_offsets[0])
    qkv_piece = columns_piece((query_weight, key_weight, value_weight), part, parts)
    gu_piece = columns_piece((gate_weight, up_weight), part, parts)
    edge_tokens = shifted(own_tokens[rows - 2 :], "seq", 1)
    grad_down = (cotangent[0].astype(F32) * live_mask).astype(BF)
    (
        gated_all,
        qkv,
        edge,
        qkv_map,
        middle,
        heads_out,
        grad_down_all,
        normed_all,
        hidden,
        grad_gu,
        gu_map,
        gains_all,
        table_all,
    ) = forward_part(
        0,
        count,
        own_tokens,
        jnp.pad(edge_tokens, ((0, 6), (0, 0))),
        grad_down,
        gains,
        table,
        qkv_piece,
        gu_piece,
        out_weight,
        down_weight,
    )
    local = out_weight.shape[0]
    flat = lambda a: a.reshape(-1, a.shape[-1])
    lens_all, starts_all = table_all[:, 0, :count], table_all[:, 1, :count]
    gains_all = gains_all.transpose(1, 0, 2).reshape(8, width)
    norm_one = gains_all[0].astype(F32)
    norm_two = gains_all[1].astype(F32)
    taps = gains_all[2:5].astype(F32)
    qkv_map, gu_map = qkv_map.reshape(width, -1), gu_map.reshape(width, -1)
    grad_down_all = flat(grad_down_all)

    extended = jnp.concatenate([edge_tokens, own_tokens], 0).astype(F32)
    scale_one = lax.rsqrt(jnp.mean(extended * extended, axis=1, keepdims=True) + EPS)
    normed = extended * scale_one * norm_one
    conv_mix = (
        normed[2:] * taps[0]
        + same_one * normed[1:-1] * taps[1]
        + same_two * normed[:-2] * taps[2]
    )

    gu_packed = pack_grads(parts, size, flat(normed_all), flat(grad_gu))
    gu_packed, grad_gu = lax.optimization_barrier((gu_packed, grad_gu))
    gu_piece = lax.psum_scatter(gu_packed, "seq", scatter_dimension=0)
    down_sum = dot_rows(flat(hidden), grad_down_all).astype(BF)
    grad_gu, down_sum = lax.optimization_barrier((grad_gu, down_sum))
    down_total = lax.psum(down_sum, "seq").astype(F32)
    grad_middle, norm2_term, grad_branch_all, dqkv, grad_gated = back_part(
        4,
        lens_all,
        starts_all,
        grad_gu,
        gu_map,
        middle,
        grad_down,
        norm_two[None],
        out_weight,
        edge,
        qkv,
        qkv_map,
    )
    norm2_term = norm2_term[0]
    qkvo_packed = pack_grads(
        parts, size, flat(gated_all), flat(dqkv), flat(heads_out), flat(grad_branch_all)
    )

    normed_own = normed[2:]
    grad_mix = grad_gated * normed_own
    part_zero = jnp.pad(grad_gated * conv_mix + grad_mix * taps[0], ((2, 0), (0, 0)))
    part_one = jnp.pad(grad_mix * same_one * taps[1], ((1, 1), (0, 0)))
    part_two = jnp.pad(grad_mix * same_two * taps[2], ((0, 2), (0, 0)))
    grad_normed = part_zero + part_one + part_two
    unit_one = extended * scale_one
    grad_unit_one = grad_normed * norm_one
    grad_extended = scale_one * (
        grad_unit_one - unit_one * jnp.mean(grad_unit_one * unit_one, axis=1, keepdims=True)
    )
    edge_back = shifted(grad_extended[:2], "seq", -1)
    tokens_grad = grad_middle + grad_extended[2:] + jnp.pad(edge_back, ((rows - 2, 0), (0, 0)))

    terms = jnp.stack(
        [
            jnp.sum(grad_normed * unit_one, axis=0),
            norm2_term,
            jnp.sum(grad_mix * normed_own, axis=0),
            jnp.sum(grad_mix * same_one * normed[1:-1], axis=0),
            jnp.sum(grad_mix * same_two * normed[:-2], axis=0),
        ]
    )
    terms = jnp.pad(terms, ((0, 3), (0, 0))).reshape(8, size, slice_width).transpose(1, 0, 2)
    qkvo_packed, gu_piece, terms, down_total, tokens_grad = lax.optimization_barrier(
        (qkvo_packed, gu_piece, terms, down_total, tokens_grad)
    )
    qkvo_every, gu_every, feed, terms = close_part(
        5, qkvo_packed, gu_piece, terms, hidden, down_weight
    )
    gate_total, up_total = unpack_grads(gu_every, (gu_map.shape[1] // 2,) * 2)
    query_total, key_total, value_total, out_total = unpack_grads(qkvo_every, (local,) * 4)

    layer_out = (live_mask * (middle + feed)).astype(BF)[None]
    return (
        layer_out,
        tokens_grad[None],
        terms[0],
        terms[2:5].T,
        query_total,
        key_total,
        value_total,
        out_total,
        terms[1],
        gate_total,
        up_total,
        down_total,
    )


def solution(mesh):
    placed = (
        P("fsdp", "seq", None),
        P("fsdp", None),
        P("fsdp", None),
        P("fsdp"),
        P("fsdp", None),
        P("fsdp", None),
        P("fsdp", None),
        P("fsdp", None),
        P("fsdp", None),
        P("fsdp"),
        P("fsdp", None),
        P("fsdp", None),
        P("fsdp", None),
        P("fsdp", "seq", None),
    )
    return jax.shard_map(
        shards,
        mesh=mesh,
        in_specs=placed,
        out_specs=(
            P("fsdp", "seq", None),
            P("fsdp", "seq", None),
            P("fsdp"),
            P("fsdp", None),
            P("fsdp", None),
            P("fsdp", None),
            P("fsdp", None),
            P("fsdp", None),
            P("fsdp"),
            P("fsdp", None),
            P("fsdp", None),
            P("fsdp", None),
        ),
        check_vma=False,
    )
```

profile of v0, /device:TPU:0, one launch (start us, length us, event | category | flops | bytes accessed | tf_op | source)
XLA Modules:
  0.0 660.1 jit_solution(16527423212681274340)
XLA Ops:
  8.0 2.4 collective-permute-start
  11.3 1.3 constant_dynamic-slice_fusion
  17.3 1.3 maximum_bitcast_fusion.refs_6_
  18.5 1.1 fusion.10.refs_2_.grad_ref
  23.2 173.7 %forward_part.1 = (bf16[4,256,1792]{2,1,0:T(8,128)(2,1)}, bf16[4,256,1344]{2,1,0:T(8,128)(2,1)}, bf16[4,64,896]{2,1,0:T(8,128)(2,1)}, bf16[4,8,56,1344]{3,2,1,0:...) custom-call(bf16[256,1792]{1,0:T(8,128)(2,1)} %bitcast.41, ...), custom_call_target="tpu_custom_call" | custom-call | flops 19964887040 | bytes 500000000 | tf_op jit(solution)/shard_map/forward_part/pallas_call | solution.py:684
  196.8 15.1 %pack_grads.2 = bf16[8,4,56,2432]{3,2,1,0:T(8,128)(2,1)} custom-call(bf16[1024,1792]{1,0:T(8,128)(2,1)} %bitcast.62, bf16[1024,2432]{1,0:T(8,128)(2,1)} %bitcast.59), custom_call_target="tpu_custom_call" | custom-call | flops 8925478912 | bytes 17367040 | tf_op jit(solution)/shard_map/pack_grads/pallas_call | solution.py:1268
  211.9 8.8 %bitcast_convert_fusion = bf16[1216,1792]{1,0:T(8,128)(2,1)} fusion(bf16[4,256,1216]{2,1,0:T(8,128)(2,1)S(1)} %copy-done.15, bf16[4,256,1792]{2,1,0:T(8,128)(2,1)} %get-tuple-element.80), kind=kOutput, calls=%fused_computation | convolution fusion | flops 4464918528 | bytes 10518528 | tf_op jit(solution)/shard_map/dot_general | solution.py:38
  223.7 1.4 fusion.19
  225.0 1.7 fusion.3
  226.7 121.5 %back_part.1 = (f32[256,1792]{1,0:T(8,128)}, f32[1,1792]{1,0:T(1,128)}, bf16[4,256,1792]{2,1,0:T(8,128)(2,1)}, bf16[4,256,1344]{2,1,0:T(8,128)(2,1)}, f32[256,1792]{1,0:T(8,128)}) custom-call(s32[4,1]{1,0:T(4,128)} %bitcast.55, s32[4,1]{1,0:T(4,128)} %bitcast.54, bf16[4,256,2432]{2,1,0:T(8,128)(2,1)} %get-tuple-element.81.grad_gu_hbm, ...), custom_call_target="tpu_custom_call" | custom-call | flops 15502147584 | bytes 400000000 | tf_op jit(solution)/shard_map/back_part/pallas_call | solution.py:911
  348.2 4.5 multiply_reduce_fusion
  352.7 1.2 multiply_add_fusion
  354.0 1.4 fusion.5
  356.1 1.3 collective-permute-start.1
  357.4 13.7 %pack_grads.3.refs_0_ = bf16[8,4,56,1792]{3,2,1,0:T(8,128)(2,1)} custom-call(bf16[1024,1792]{1,0:T(8,128)(2,1)} %bitcast.60, bf16[1024,1344]{1,0:T(8,128)(2,1)} %bitcast.63, bf16[1024,448]{1,0:T(8,128)(2,1)} %bitcast.64, bf16[1024,1792]{1,0:T(8,128)(2,1)} %bitcast.61), custom_call_target="tpu_custom_call" | custom-call | flops 6576668672 | bytes 12845056 | tf_op jit(solution)/shard_map/pack_grads/pallas_call | solution.py:1268
  372.0 3.0 fusion.9
  375.0 6.5 convert_element_type.82
  381.5 43.9 %reduce-scatter.2.cloned.1.call-done = bf16[1,4,56,2432]{3,2,1,0:T(8,128)(2,1)} async-done(((bf16[8,4,56,2432]{3,2,1,0:T(8,128)(2,1)}), bf16[1,4,56,2432]{3,2,1,0:T(8,128)(2,1)}) %reduce-scatter.2.cloned.1.call-update) | async-done | bytes 1089552 | tf_op jit(solution)/shard_map/reduce_scatter | solution.py:1420
  425.4 202.3 %close_part.1 = (bf16[8,4,56,1792]{3,2,1,0:T(8,128)(2,1)}, bf16[8,4,56,2432]{3,2,1,0:T(8,128)(2,1)}, f32[256,1792]{1,0:T(8,128)}, f32[8,448]{1,0:T(8,128)}) custom-call(bf16[8,4,56,1792]{3,2,1,0:T(8,128)(2,1)} %pack_grads.3.refs_0_, bf16[4,56,2432]{2,1,0:T(8,128)(2,1)} %bitcast.56, f32[4,8,448]{2,1,0:T(8,128)} %bitcast.48, ...), custom_call_target="tpu_custom_call" | custom-call | flops 4462739456 | bytes 500000000 | tf_op jit(solution)/shard_map/close_part/pallas_call | solution.py:1196
  627.7 1.3 slice_bitcast_fusion
  629.0 1.4 fusion.18
  630.4 10.8 %unpack_grads.3 = (f32[448,4864]{1,0:T(8,128)}, f32[448,4864]{1,0:T(8,128)}) custom-call(bf16[8,4,56,2432]{3,2,1,0:T(8,128)(2,1)} %get-tuple-element.106.every_ref), custom_call_target="tpu_custom_call" | custom-call | bytes 26148864 | tf_op jit(solution)/shard_map/unpack_grads/pallas_call | solution.py:1301
  641.2 9.2 %unpack_grads.2 = (f32[448,1792]{1,0:T(8,128)}, f32[448,1792]{1,0:T(8,128)}, f32[448,1792]{1,0:T(8,128)}, f32[448,1792]{1,0:T(8,128)}) custom-call(bf16[8,4,56,1792]{3,2,1,0:T(8,128)(2,1)} %get-tuple-element.101.every_ref), custom_call_target="tpu_custom_call" | custom-call | bytes 19267584 | tf_op jit(solution)/shard_map/unpack_grads/pallas_call | solution.py:1301
  650.5 2.6 fusion.11
  (84 shorter events, 12.9 us)
Async XLA Ops:
  7.2 367.8 %all-reduce.9.cloned.1.call-start = ((), (), s32[]{:S(2)}) async-start(), calls=%async_computation.2 | async-start | bytes 8716288 | tf_op jit(solution)/shard_map/psum | solution.py:1423
  8.0 14.6 %collective-permute-start = (bf16[2,1792]{1,0:T(2,128)(2,1)S(1)}, bf16[2,1792]{1,0:T(2,128)(2,1)S(1)}, u32[]{:S(2)}, u32[]{:S(2)}) collective-permute-start(bf16[2,1792]{1,0:T(2,128)(2,1)S(1)} %slice_bitcast_fusion.1), channel_id=1, source_target_pairs={{0,4},{4,8},{8,12},{12,16},{16,20},{20,24},{24,28},{1,5},{5,9},{9,... | collective-permute-start | bytes 21512 | tf_op jit(solution)/shard_map/ppermute | solution.py:26
  13.3 2.9 copy-start.13
  13.3 2.9 copy-start.14
  14.1 4.5 copy-start.5
  17.3 2.5 copy-start.12
  21.4 1.7 copy-start.11
  196.8 15.1 %copy-start.15 = (bf16[4,256,1216]{2,1,0:T(8,128)(2,1)S(1)}, bf16[4,256,1216]{2,1,0:T(8,128)(2,1)}, u32[]{:S(2)}) copy-start(bf16[4,256,1216]{2,1,0:T(8,128)(2,1)} %get-tuple-element.79.refs_3_) | copy-start | bytes 7471108
  220.7 0.8 copy-start.7
  220.7 2.5 copy-start.1
  220.7 204.7 %reduce-scatter.2.cloned.1.call-start = ((), (), s32[]{:S(2)}) async-start(), calls=%async_computation.1 | async-start | bytes 9805824 | tf_op jit(solution)/shard_map/reduce_scatter | solution.py:1420
  348.2 4.5 copy-start
  348.2 4.5 copy-start.3
  348.2 4.5 copy-start.6
  348.2 4.5 copy-start.8
  348.2 4.5 copy-start.9
  352.7 1.2 copy-start.2
  356.1 15.9 %collective-permute-start.1 = (f32[2,1792]{1,0:T(2,128)S(1)}, f32[2,1792]{1,0:T(2,128)S(1)}, u32[]{:S(2)}, u32[]{:S(2)}) collective-permute-start(f32[2,1792]{1,0:T(2,128)S(1)} %slice.141), channel_id=1, source_target_pairs={{4,0},{8,4},{12,8},{16,12},{20,16},{24,20},{28,24},{5,1},{9,5},{13... | collective-permute-start | bytes 43016 | tf_op jit(solution)/shard_map/ppermute | solution.py:26
  357.4 13.8 %copy-start.10 = (f32[1,1792]{1,0:T(1,128)S(1)}, f32[1,1792]{1,0:T(1,128)}, u32[]{:S(2)}) copy-start(f32[1,1792]{1,0:T(1,128)} %get-tuple-element.92) | copy-start | bytes 21508
  641.2 9.3 %copy-start.4 = (f32[256,1792]{1,0:T(8,128)S(1)}, f32[256,1792]{1,0:T(8,128)}, u32[]{:S(2)}) copy-start(f32[256,1792]{1,0:T(8,128)} %get-tuple-element.73.middle_ref) | copy-start | bytes 5505028
Sparse Core Ops, SparseCore 0:
  220.8 109.0 all-reduce.8
  332.8 92.5 reduce-scatter.1
where the time goes:
time: 669 us; the launch traced here: 660 us
  Pallas kernels  546 us (82%)
  waiting for transfers between devices  44.6 us (7%)
  other arithmetic  25.7 us (4%)
  between operations  16 us (2%)
  local copies, waits for them, and re-layouts  15 us (2%)
  matrix products  8.76 us (1%)
    pallas_call x1, Pallas kernels, close_part(): pl.pallas_call(functools.partial(close_kernel, size, parts), out_shape=[j...  202 us
    pallas_call x1, Pallas kernels, forward_part(): pl.pallas_call(functools.partial(forward_kernel, size, parts, count), out...  174 us
    pallas_call x1, Pallas kernels, back_part(): pl.pallas_call(functools.partial(back_kernel, size, parts, lens.shape[1])...  121 us
    reduce_scatter x1, waiting for transfers between devices, shards(): gu_piece = lax.psum_scatter(gu_packed, 'seq', scatter_dimension=0)  43.9 us
    pallas_call x2, Pallas kernels, pack_grads(): pl.pallas_call(functools.partial(pack_kernel, size, parts), grid=(size //...  28.8 us
    pallas_call x2, Pallas kernels, unpack_grads(): pl.pallas_call(functools.partial(unpack_kernel, widths), grid=(parts,), o...  20.1 us
  transfers between devices with their start and end apart: 4, of which 1 were waited for; matrix products, arithmetic and copies ran while one was open for 5% of the time, Pallas kernels for 20%

commit v1 on v0

--- a/solution.py
+++ b/solution.py
@@ -1,4 +1,5 @@
 import functools
+from typing import Any, NamedTuple
 
 import jax
 import jax.numpy as jnp
@@ -315,6 +316,112 @@
             pl.when((z + j < self.length) & self.has_below)(lambda: self.down(j, rank).wait_send())
 
 
+class LineSum:
+    def __init__(self, line, x, pre, acc, up_in, down_in, sems):
+        self.line, self.x, self.pre, self.acc = line, x, pre, acc
+        self.up_in, self.down_in, self.sems = up_in, down_in, sems
+
+    def share(self, k):
+        line = self.line
+        src = self.x.at[2 * k + 1 - line.core]
+        return remote(src, self.pre.at[k], self.sems[0].at[k], self.sems[1].at[k], seq=line.beside)
+
+    def up(self, k):
+        sems = self.sems[2].at[k], self.sems[3].at[k]
+        return remote(self.acc.at[k], self.up_in.at[k], *sems, seq=self.line.above)
+
+    def down(self, k):
+        sems = self.sems[4].at[k], self.sems[5].at[k]
+        return remote(self.acc.at[k], self.down_in.at[k], *sems, seq=self.line.below)
+
+    def pair(self, m):
+        return self.line.length - 1 - m, m
+
+    def trade(self):
+        n = self.line.length
+        for m in range((n + 1) // 2):
+            for k in sorted(set(self.pair(m))):
+                self.share(k).start()
+
+    def merge(self, k):
+        self.share(k).wait_recv()
+        own = self.x[2 * k + self.line.core].astype(F32)
+        self.acc[k] = (own + self.pre[k].astype(F32)).astype(BF)
+
+    def begin(self, m):
+        n, z = self.line.length, self.line.z
+        far, near = self.pair(m)
+        if m < (n + 1) // 2:
+            for k in sorted({far, near}):
+                self.merge(k)
+        if m < n - 1:
+            pl.when(z == 0)(lambda: self.up(far).start())
+            pl.when(z == n - 1)(lambda: self.down(near).start())
+
+    def add(self, k, more):
+        self.acc[k] = (self.acc[k].astype(F32) + more[k].astype(F32)).astype(BF)
+
+    def advance(self, m):
+        z, n = self.line.z, self.line.length
+        far, near = self.pair(m)
+
+        @pl.when((z > 0) & (z < far))
+        def _():
+            self.up(far).wait_recv()
+            self.add(far, self.up_in)
+            self.up(far).start()
+
+        @pl.when((z < n - 1) & (z > near))
+        def _():
+            self.down(near).wait_recv()
+            self.add(near, self.down_in)
+            self.down(near).start()
+
+    def total(self):
+        z = self.line.z
+
+        @pl.when(z > 0)
+        def _():
+            self.up(z).wait_recv()
+            self.add(z, self.up_in)
+
+        @pl.when(z < self.line.length - 1)
+        def _():
+            self.down(z).wait_recv()
+            self.add(z, self.down_in)
+
+    def finish(self):
+        for k in range(self.line.length):
+            self.share(k).wait_send()
+            pl.when(k > self.line.z)(lambda: self.up(k).wait_send())
+            pl.when(k < self.line.z)(lambda: self.down(k).wait_send())
+
+
+class StagedSum(LineSum):
+    def __init__(self, stage, load, *args):
+        super().__init__(*args)
+        self.stage, self.load = stage, load
+
+    def fetch(self, slot, src):
+        return pltpu.make_async_copy(src, self.stage.at[slot], self.load.at[slot])
+
+    def merge(self, k):
+        self.share(k).wait_recv()
+        own = self.fetch(0, self.x.at[2 * k + self.line.core])
+        other = self.fetch(1, self.pre.at[k])
+        own.start()
+        other.start()
+        own.wait()
+        other.wait()
+        self.acc[k] = (self.stage[0].astype(F32) + self.stage[1].astype(F32)).astype(BF)
+
+    def add(self, k, more):
+        came = self.fetch(0, more.at[k])
+        came.start()
+        came.wait()
+        self.acc[k] = (self.acc[k].astype(F32) + self.stage[0].astype(F32)).astype(BF)
+
+
 def line_sems(parts):
     return [pltpu.SemaphoreType.DMA((parts // 2,))] * 6
 
@@ -345,71 +452,69 @@
     lax.fori_loop(0, size, one, 0)
 
 
-FORWARD_REFS = (
-    "tokens",
-    "edge_tok",
-    "grad",
-    "gains",
-    "table",
-    "qkv_piece",
-    "gu_piece",
-    "out_map",
-    "down_map",
-    "gated_hbm",
-    "qkv_hbm",
-    "edge",
-    "qkv_map_hbm",
-    "middle",
-    "heads",
-    "grads_hbm",
-    "norm_hbm",
-    "hidden_hbm",
-    "gu_grad_hbm",
-    "gu_map_hbm",
-    "gains_all",
-    "table_all",
-    "part",
-    "first",
-    "over",
-    "joined",
-    "last",
-    "all",
-    "grads",
-    "qkv",
-    "qkv_map",
-    "gu_map",
-    "tail",
-    "own",
-    "hidden",
-    "gu_grad",
-    "s_send",
-    "s_recv",
-    "a_send",
-    "a_recv",
-    "g_send",
-    "g_recv",
-    "c_send",
-    "c_recv",
-    "m_send",
-    "m_recv",
-    "halo_send",
-    "halo_recv",
-    "loads",
-    "stores",
-    "hidden_store",
-    "gu_store",
-)
+class ForwardRefs(NamedTuple):
+    tokens: Any
+    edge_tok: Any
+    grad: Any
+    gains: Any
+    table: Any
+    qkv_piece: Any
+    gu_piece: Any
+    out_map: Any
+    down_map: Any
+    gated_hbm: Any
+    qkv_hbm: Any
+    edge: Any
+    qkv_map_hbm: Any
+    middle: Any
+    heads: Any
+    grads_hbm: Any
+    norm_hbm: Any
+    hidden_hbm: Any
+    gu_grad_hbm: Any
+    gu_map_hbm: Any
+    gains_all: Any
+    table_all: Any
+    part: Any
+    first: Any
+    over: Any
+    joined: Any
+    last: Any
+    all: Any
+    grads: Any
+    qkv: Any
+    qkv_map: Any
+    gu_map: Any
+    tail: Any
+    own: Any
+    hidden: Any
+    gu_grad: Any
+    s_send: Any
+    s_recv: Any
+    a_send: Any
+    a_recv: Any
+    g_send: Any
+    g_recv: Any
+    c_send: Any
+    c_recv: Any
+    m_send: Any
+    m_recv: Any
+    halo_send: Any
+    halo_recv: Any
+    loads: Any
+    stores: Any
+    hidden_store: Any
+    gu_store: Any
 
 
 def forward_kernel(size, parts, count, *refs):
-    names = FORWARD_REFS
-    r = dict(zip(names, refs))
-    sems = refs[len(names) :]
+    named = len(ForwardRefs._fields)
+    r, sems = ForwardRefs(*refs[:named]), refs[named:]
     rank = lax.axis_index("seq")
-    rows = r["tokens"].shape[0]
+    rows = r.tokens.shape[0]
     half = rows // 2
-    local = r["out_map"].shape[0]
-    inner = r["down_map"].shape[0]
+    local = r.out_map.shape[0]
+    inner = r.down_map.shape[0]
     slot = rank * rows
     group = Group(size)
     me = group.me
@@ -427,27 +532,27 @@
     n, z = line_q.length, line_q.z
     known = known + (2 * n - 2 - z) // n * line_q.core + (z + n - 1) // n * (1 - line_q.core)
     own_pieces = [
-        pltpu.make_async_copy(src.at[me], dst.at[me, rank], r["loads"].at[k])
+        pltpu.make_async_copy(src.at[me], dst.at[me, rank], r.loads.at[k])
         for k, (src, dst) in enumerate(
-            ((r["qkv_piece"], r["qkv_map"]), (r["gu_piece"], r["gu_map"]))
+            ((r.qkv_piece, r.qkv_map), (r.gu_piece, r.gu_map))
         )
     ]
     for copy in own_pieces:
         copy.start()
-    r["gains_all"][me] = r["gains"][...]
-    r["table_all"][me] = r["table"][...]
-    r["grads"][me] = r["grad"][...]
+    r.gains_all[me] = r.gains[...]
+    r.table_all[me] = r.table[...]
+    r.grads[me] = r.grad[...]
     pl.semaphore_wait(barrier, size - 1 + known)
 
     def swap(k, step):
         peer = lax.rem(me + step, size)
         src, dst = (
-            lambda: (r["gains_all"].at[me], r["gains_all"].at[me]),
-            lambda: (r["table_all"].at[me], r["table_all"].at[me]),
-            lambda: (r["qkv_piece"].at[peer], r["qkv_map"].at[me, rank]),
-            lambda: (r["gu_piece"].at[peer], r["gu_map"].at[me, rank]),
+            lambda: (r.gains_all.at[me], r.gains_all.at[me]),
+            lambda: (r.table_all.at[me], r.table_all.at[me]),
+            lambda: (r.qkv_piece.at[peer], r.qkv_map.at[me, rank]),
+            lambda: (r.gu_piece.at[peer], r.gu_map.at[me, rank]),
         )[k]()
-        return remote(src, dst, r["m_send"].at[k, step - 1], r["m_recv"].at[k, step - 1], fsdp=peer)
+        return remote(src, dst, r.m_send.at[k, step - 1], r.m_recv.at[k, step - 1], fsdp=peer)
 
     others = range(1, size)
     for k in range(4):
@@ -457,16 +562,16 @@
         for step in others:
             swap(k, step).wait_recv()
 
-    gains = jnp.concatenate([r["gains_all"][f] for f in range(size)], 1).astype(F32)
-    own_table = r["table_all"][me]
+    gains = jnp.concatenate([r.gains_all[f] for f in range(size)], 1).astype(F32)
+    own_table = r.table_all[me]
     slots = slot + lax.broadcasted_iota(jnp.int32, (rows, 1), 0)
     length = lambda j: own_table[0:1, j : j + 1]
     start = lambda j: own_table[1:2, j : j + 1]
     segment = segment_of(slots, count, length, start)
     same_one = (segment == segment_of(slots - 1, count, length, start)).astype(F32)
     same_two = (segment == segment_of(slots - 2, count, length, start)).astype(F32)
-    tokens = r["tokens"][...].astype(F32)
-    edge = r["edge_tok"][...].astype(F32)
+    tokens = r.tokens[...].astype(F32)
+    edge = r.edge_tok[...].astype(F32)
 
     def norm(a):
         return a * lax.rsqrt(jnp.mean(a * a, axis=1, keepdims=True) + EPS) * gains[0:1]
@@ -482,19 +587,19 @@
         + same_one * back_one * gains[3:4]
         + same_two * back_two * gains[4:5]
     )
-    all_ref = r["all"]
+    all_ref = r.all
     all_ref[me] = (mixed * normed).astype(BF)
-    gather = Gather(group, all_ref, r["a_send"], r["a_recv"])
+    gather = Gather(group, all_ref, r.a_send, r.a_recv)
     gather.start_half(0)
     gather.start_half(1)
 
     own_pieces[0].wait()
     for step in others:
         swap(2, step).wait_recv()
-    line_q.gather(lambda owner: r["qkv_map"].at[:, owner])
-    line_u.view = lambda owner: r["gu_map"].at[:, owner]
+    line_q.gather(lambda owner: r.qkv_map.at[:, owner])
+    line_u.view = lambda owner: r.gu_map.at[:, owner]
     gather.relay()
-    grads = Gather(group, r["grads"], r["c_send"], r["c_recv"])
+    grads = Gather(group, r.grads, r.c_send, r.c_recv)
     grads.start_half(0)
     grads.start_half(1)
     own_pieces[1].wait()
@@ -513,47 +618,47 @@
     grads.relay()
     line_q.gathered()
     keeps = [
-        pltpu.make_async_copy(all_ref, r["gated_hbm"], r["stores"].at[size]),
-        pltpu.make_async_copy(r["qkv_map"], r["qkv_map_hbm"], r["stores"].at[size + 1]),
+        pltpu.make_async_copy(all_ref, r.gated_hbm, r.stores.at[size]),
+        pltpu.make_async_copy(r.qkv_map, r.qkv_map_hbm, r.stores.at[size + 1]),
     ]
     for keep in keeps:
         keep.start()
 
-    weights = r["qkv_map"][...].reshape(-1, r["qkv_map"].shape[3])
+    weights = r.qkv_map[...].reshape(-1, r.qkv_map.shape[3])
 
     def halo(step):
         g = group.to_own(step)
-        sem = r["halo_send"].at[step], r["halo_recv"].at[step]
-        return remote(r["tail"].at[g], r["edge"].at[g], *sem, seq=rank + 1)
+        sem = r.halo_send.at[step], r.halo_recv.at[step]
+        return remote(r.tail.at[g], r.edge.at[g], *sem, seq=rank + 1)
 
     def project(step, is_step):
         g = group.to_own(step)
         out = dot(all_ref[g], weights).astype(BF)
-        r["qkv"][g] = out
-        r["tail"][g] = out[rows - WINDOW :, local:]
+        r.qkv[g] = out
+        r.tail[g] = out[rows - WINDOW :, local:]
         pl.when(rank < parts - 1)(lambda: halo(step).start())
 
     each_step(size, project)
 
     @pl.when(rank == 0)
     def _():
-        r["edge"][...] = jnp.zeros_like(r["edge"])
-
-    keeps.append(pltpu.make_async_copy(r["qkv"], r["qkv_hbm"], r["stores"].at[size + 2]))
+        r.edge[...] = jnp.zeros_like(r.edge)
+
+    keeps.append(pltpu.make_async_copy(r.qkv, r.qkv_hbm, r.stores.at[size + 2]))
     keeps[2].start()
     line_u.relay(1)
     gather.finish()
     keeps[0].wait()
 
     scatter = Scatter(
-        group, *(r[k] for k in ("part", "first", "over", "joined", "last", "s_send", "s_recv"))
+        group, r.part, r.first, r.over, r.joined, r.last, r.s_send, r.s_recv
     )
     head_of = lane_head(local)
 
     def mix(step, is_step):
         g = group.to_own(step)
         pl.when(rank > 0)(lambda: halo(step).wait_recv())
-        own, edge, table = r["qkv"][g], r["edge"][g], r["table_all"][g]
+        own, edge, table = r.qkv[g], r.edge[g], r.table_all[g]
         queries = own[:, :local]
         keys = jnp.concatenate([edge[:, :local], own[:, local : 2 * local]], 0)
         values = jnp.concatenate([edge[:, local:], own[:, 2 * local :]], 0)
@@ -577,10 +682,10 @@
                 out = jnp.where(mine, dot(soft.astype(BF), value), out)
             outs.append(out.astype(BF))
         heads = jnp.concatenate(outs, 0)
-        r["heads"][g] = heads
-        branch = dot(heads, r["out_map"][...])
-        is_step(size - 1)(lambda: r["own"].__setitem__(..., branch))
-        pl.when(step < size - 1)(lambda: r["part"].__setitem__(step, branch.astype(BF)))
+        r.heads[g] = heads
+        branch = dot(heads, r.out_map[...])
+        is_step(size - 1)(lambda: r.own.__setitem__(..., branch))
+        pl.when(step < size - 1)(lambda: r.part.__setitem__(step, branch.astype(BF)))
         for k in range(size - 1):
             is_step(k)(functools.partial(scatter.made, k))
 
@@ -588,12 +693,12 @@
     scatter.join()
     for j in range(2, n):
         line_u.relay(j)
-    gather = Gather(group, all_ref, r["g_send"], r["g_recv"])
+    gather = Gather(group, all_ref, r.g_send, r.g_recv)
     for h in range(2):
         span = slice(h * half, (h + 1) * half)
-        total = r["own"][span, :] + scatter.total(h)
-        middle = r["tokens"][span, :].astype(F32) + total
-        r["middle"][span, :] = middle
+        total = r.own[span, :] + scatter.total(h)
+        middle = r.tokens[span, :].astype(F32) + total
+        r.middle[span, :] = middle
         scale = lax.rsqrt(jnp.mean(middle * middle, axis=1, keepdims=True) + EPS)
         all_ref[me, span] = (middle * scale * gains[1:2]).astype(BF)
         gather.start_half(h)
@@ -601,22 +706,22 @@
     for j in range(1, n):
         line_u.close(j)
     line_u.gathered()
-    keeps.append(pltpu.make_async_copy(r["gu_map"], r["gu_map_hbm"], r["stores"].at[size + 3]))
+    keeps.append(pltpu.make_async_copy(r.gu_map, r.gu_map_hbm, r.stores.at[size + 3]))
     keeps[3].start()
 
     def out_copies(step):
         g, two = group.from_own(step), lax.rem(step, 2)
         return (
             pltpu.make_async_copy(
-                r["hidden"].at[two], r["hidden_hbm"].at[g], r["hidden_store"].at[two]
+                r.hidden.at[two], r.hidden_hbm.at[g], r.hidden_store.at[two]
             ),
             pltpu.make_async_copy(
-                r["gu_grad"].at[two], r["gu_grad_hbm"].at[g], r["gu_store"].at[two]
+                r.gu_grad.at[two], r.gu_grad_hbm.at[g], r.gu_store.at[two]
             ),
         )
 
     def norm_copy(g):
-        return pltpu.make_async_copy(all_ref.at[g], r["norm_hbm"].at[g], r["stores"].at[g])
+        return pltpu.make_async_copy(all_ref.at[g], r.norm_hbm.at[g], r.stores.at[g])
 
     def feed(step, is_step):
         g, two = group.from_own(step), lax.rem(step, 2)
@@ -630,20 +735,20 @@
                 copy.wait()
 
         norm_copy(g).start()
-        weights = r["gu_map"][...].reshape(-1, r["gu_map"].shape[3])
+        weights = r.gu_map[...].reshape(-1, r.gu_map.shape[3])
         acts = dot(all_ref[g], weights)
         gate, up = acts[:, :inner], acts[:, inner:]
         sigma = jax.nn.sigmoid(gate)
         silu = gate * sigma
-        r["hidden"][two] = (silu * up).astype(BF)
-        grad_hidden = dot_trans(r["grads"][g], r["down_map"][...])
+        r.hidden[two] = (silu * up).astype(BF)
+        grad_hidden = dot_trans(r.grads[g], r.down_map[...])
         grad_gate = grad_hidden * up * sigma * (1.0 + gate * (1.0 - sigma))
-        r["gu_grad"][two] = jnp.concatenate([grad_gate, grad_hidden * silu], 1).astype(BF)
+        r.gu_grad[two] = jnp.concatenate([grad_gate, grad_hidden * silu], 1).astype(BF)
         for copy in out_copies(step):
             copy.start()
 
     each_step(size, feed)
-    keeps.append(pltpu.make_async_copy(r["grads"], r["grads_hbm"], r["stores"].at[size + 4]))
+    keeps.append(pltpu.make_async_copy(r.grads, r.grads_hbm, r.stores.at[size + 4]))
     keeps[4].start()
     for k in range(4):
         for step in others:
@@ -774,13 +879,81 @@
     return jnp.concatenate(dqs, 0), joined(dks), joined(dvs)
 
 
-def back_kernel(size, parts, count, lens_ref, starts_ref, grad_gu_hbm, gu_map_hbm, middle_ref, grad_ref,
-                gain_ref, out_map_ref, edge_ref, qkv_ref, qkv_map_hbm,
-                grad_middle_ref, norm_ref, all_ref, dqkv_ref, own_ref,
-                part, first, over, joined, last, s_send, s_recv, t_send, t_recv, g_send, g_recv,
-                grad_gu_ref, gu_map_ref, qkv_map_ref, dedge_ref, back_ref, tail_ref, h_send, h_recv, loads):
-    rows = middle_ref.shape[0]
-    local = out_map_ref.shape[0]
+class BackRefs(NamedTuple):
+    lens: Any
+    starts: Any
+    grad_gu_hbm: Any
+    gu_map_hbm: Any
+    middle: Any
+    grad: Any
+    gain: Any
+    out_map: Any
+    edge: Any
+    qkv: Any
+    qkv_map_hbm: Any
+    gu_x: Any
+    down_x: Any
+    grad_middle: Any
+    norm: Any
+    all: Any
+    dqkv: Any
+    own: Any
+    gu_piece: Any
+    down_every: Any
+    gu_pre: Any
+    gu_up: Any
+    gu_down: Any
+    down_pre: Any
+    down_up: Any
+    down_down: Any
+    part: Any
+    first: Any
+    over: Any
+    joined: Any
+    last: Any
+    s_send: Any
+    s_recv: Any
+    t_send: Any
+    t_recv: Any
+    g_send: Any
+    g_recv: Any
+    grad_gu: Any
+    gu_map: Any
+    qkv_map: Any
+    dedge: Any
+    back: Any
+    tail: Any
+    h_send: Any
+    h_recv: Any
+    loads: Any
+    gu_acc: Any
+    gu_stage: Any
+    gu_load: Any
+    down_acc: Any
+    down_stage: Any
+    down_load: Any
+
+
+def back_kernel(size, parts, count, *refs):
+    named = len(BackRefs._fields)
+    r, sems = BackRefs(*refs[:named]), refs[named:]
+    line = Line(parts, sems[:6])
+    gu_sum = StagedSum(
+        r.gu_stage, r.gu_load, line, r.gu_x, r.gu_pre, r.gu_acc, r.gu_up, r.gu_down, sems[6:12]
+    )
+    down_sum = StagedSum(
+        r.down_stage,
+        r.down_load,
+        line,
+        r.down_x,
+        r.down_pre,
+        r.down_acc,
+        r.down_up,
+        r.down_down,
+        sems[12:],
+    )
+    rows = r.middle.shape[0]
+    local = r.out_map.shape[0]
     rank = lax.axis_index("seq")
     slot = rank * rows
     group = Group(size)
@@ -790,56 +963,69 @@
     def greet(peer):
         pl.semaphore_signal(barrier, inc=1, device_id={"seq": peer}, device_id_type=MESH_ID)
 
-    pl.when(rank > 0)(lambda: greet(rank - 1))
-    pl.when(rank < parts - 1)(lambda: greet(rank + 1))
+    known = line.greet(barrier)
+    pl.when(line.has_above & (line.core == 1))(lambda: greet(rank + 1))
+    pl.when(line.has_below & (line.core == 0))(lambda: greet(rank - 1))
+    n, z = line.length, line.z
+    known = known + (2 * n - 2 - z) // n * line.core + (z + n - 1) // n * (1 - line.core)
     fetches = [
-        pltpu.make_async_copy(src, dst, loads.at[k])
+        pltpu.make_async_copy(src, dst, r.loads.at[k])
         for k, (src, dst) in enumerate(
-            ((grad_gu_hbm, grad_gu_ref), (gu_map_hbm, gu_map_ref), (qkv_map_hbm, qkv_map_ref))
+            ((r.grad_gu_hbm, r.grad_gu), (r.gu_map_hbm, r.gu_map), (r.qkv_map_hbm, r.qkv_map))
         )
     ]
     for fetch in fetches:
         fetch.start()
-    has_next = (2 * parts - 2 - rank) // parts
-    has_last = (rank + parts - 1) // parts
-    pl.semaphore_wait(barrier, size - 1 + has_next + has_last)
-    scatter = Scatter(group, part, first, over, joined, last, s_send, s_recv)
-    gather = Gather(group, all_ref, g_send, g_recv)
+    pl.semaphore_wait(barrier, size - 1 + known)
+    down_sum.trade()
+    gu_sum.trade()
+    scatter = Scatter(
+        group, r.part, r.first, r.over, r.joined, r.last, r.s_send, r.s_recv
+    )
+    gather = Gather(group, r.all, r.g_send, r.g_recv)
     fetches[0].wait()
     fetches[1].wait()
 
     def step_two(step, is_step):
-        partial = dot_trans(grad_gu_ref[group.to_own(step)], gu_map_ref[...])
-        is_step(size - 1)(lambda: own_ref.__setitem__(..., partial))
-        pl.when(step < size - 1)(lambda: part.__setitem__(step, partial.astype(BF)))
+        partial = dot_trans(r.grad_gu[group.to_own(step)], r.gu_map[...])
+        is_step(size - 1)(lambda: r.own.__setitem__(..., partial))
+        pl.when(step < size - 1)(lambda: r.part.__setitem__(step, partial.astype(BF)))
         for k in range(size - 1):
             is_step(k)(functools.partial(scatter.made, k))
 
     each_step(size, step_two)
+    for m in range(n):
+        down_sum.begin(m)
     scatter.join()
+    gu_sum.begin(0)
     half = rows // 2
-    norm_sum = jnp.zeros((1, middle_ref.shape[1]), F32)
+    norm_sum = jnp.zeros((1, r.middle.shape[1]), F32)
     for h in range(2):
         span = slice(h * half, (h + 1) * half)
-        grad = own_ref[span, :] + scatter.total(h)
-        middle = middle_ref[span, :]
+        grad = r.own[span, :] + scatter.total(h)
+        middle = r.middle[span, :]
         scale = lax.rsqrt(jnp.mean(middle * middle, axis=1, keepdims=True) + EPS)
         unit = middle * scale
-        scaled = grad * gain_ref[...]
+        scaled = grad * r.gain[...]
         norm_sum = norm_sum + jnp.sum(grad * unit, axis=0, keepdims=True)
-        grad_out = grad_ref[span, :].astype(F32)
+        grad_out = r.grad[span, :].astype(F32)
         grad_middle = grad_out + scale * (
             scaled - unit * jnp.mean(scaled * unit, axis=1, keepdims=True)
         )
-        grad_middle_ref[span, :] = grad_middle
-        all_ref[group.me, span] = grad_middle.astype(BF)
+        r.grad_middle[span, :] = grad_middle
+        r.all[group.me, span] = grad_middle.astype(BF)
         gather.start_half(h)
-    norm_ref[...] = norm_sum
+    r.norm[...] = norm_sum
+    for m in range(1, n - 2):
+        gu_sum.begin(m)
+    down_sum.advance(0)
+    own_down = pltpu.make_async_copy(r.down_acc.at[z], r.down_every.at[rank], r.down_load.at[0])
+    last_step = size - 1
 
     def halo(step):
         g = group.from_own(step)
-        sems = h_send.at[step], h_recv.at[step]
-        return remote(dedge_ref.at[g], back_ref.at[g], *sems, seq=rank - 1)
+        sems = r.h_send.at[step], r.h_recv.at[step]
+        return remote(r.dedge.at[g], r.back.at[g], *sems, seq=rank - 1)
 
     def step_heads(step, is_step):
         g = group.from_own(step)
@@ -847,17 +1033,32 @@
         @is_step(1)
         def _():
             gather.relay()
+            for m in range(1, n - 1):
+                down_sum.advance(m)
+
+        @is_step(2)
+        def _():
+            down_sum.total()
+            own_down.start()
+            own_down.wait()
+            line.gather(lambda owner: r.down_every.at[owner])
+            for m in range(max(1, n - 2), n):
+                gu_sum.begin(m)
+
+        @is_step(last_step)
+        def _():
+            gu_sum.advance(0)
 
         for k in range(1, size):
             is_step(k)(functools.partial(gather.ready, k))
-        grad = dot_trans(all_ref[g], out_map_ref[...]).astype(BF)
+        grad = dot_trans(r.all[g], r.out_map[...]).astype(BF)
         dq, dk, dv = heads_back(
-            g, slot, count, lens_ref, starts_ref, qkv_ref[g], edge_ref[g], grad
+            g, slot, count, r.lens, r.starts, r.qkv[g], r.edge[g], grad
         )
-        dedge_ref[g] = jnp.concatenate([dk[:WINDOW], dv[:WINDOW]], 1).astype(BF)
+        r.dedge[g] = jnp.concatenate([dk[:WINDOW], dv[:WINDOW]], 1).astype(BF)
         full = jnp.concatenate([dq, dk[WINDOW:], dv[WINDOW:]], 1)
-        dqkv_ref[g] = full.astype(BF)
-        tail_ref[g] = full[rows - WINDOW :]
+        r.dqkv[g] = full.astype(BF)
+        r.tail[g] = full[rows - WINDOW :]
         pl.when(rank > 0)(lambda: halo(step).start())
 
     each_step(size, step_heads)
@@ -866,33 +1067,49 @@
 
     @pl.when(rank == parts - 1)
     def _():
-        back_ref[...] = jnp.zeros_like(back_ref)
+        r.back[...] = jnp.zeros_like(r.back)
 
     @pl.when(rank < parts - 1)
     def _():
         for step in range(size):
             halo(step).wait_recv()
 
-    scatter = Scatter(group, part, first, over, joined, last, t_send, t_recv)
+    scatter = Scatter(
+        group, r.part, r.first, r.over, r.joined, r.last, r.t_send, r.t_recv
+    )
 
     def step_one(step, is_step):
         g = group.to_own(step)
-        back = back_ref[g].astype(F32)
+        back = r.back[g].astype(F32)
         wide = jnp.concatenate([jnp.zeros((WINDOW, local), F32), back], 1)
-        dqkv_ref[g, pl.ds(rows - WINDOW, WINDOW)] = (tail_ref[g] + wide).astype(BF)
-        partial = dot_trans(dqkv_ref[g], qkv_map_ref[...])
-        is_step(size - 1)(lambda: own_ref.__setitem__(..., partial))
-        pl.when(step < size - 1)(lambda: part.__setitem__(step, partial.astype(BF)))
+        r.dqkv[g, pl.ds(rows - WINDOW, WINDOW)] = (r.tail[g] + wide).astype(BF)
+        partial = dot_trans(r.dqkv[g], r.qkv_map[...])
+        is_step(size - 1)(lambda: r.own.__setitem__(..., partial))
+        pl.when(step < size - 1)(lambda: r.part.__setitem__(step, partial.astype(BF)))
         for k in range(size - 1):
             is_step(k)(functools.partial(scatter.made, k))
 
     each_step(size, step_one)
     scatter.join()
+    line.relay(1)
+    for m in range(1, n - 1):
+        gu_sum.advance(m)
+        line.relay(m + 1)
     for h in range(2):
         span = slice(h * half, (h + 1) * half)
-        own_ref[span, :] = own_ref[span, :] + scatter.total(h)
+        r.own[span, :] = r.own[span, :] + scatter.total(h)
+    gu_sum.total()
+    out_piece = pltpu.make_async_copy(r.gu_acc.at[z], r.gu_piece, r.gu_load.at[0])
+    out_piece.start()
+    for j in range(1, n):
+        line.close(j)
+    line.gathered()
     scatter.finish()
     gather.finish()
+    down_sum.finish()
+    gu_sum.finish()
+    line.finish()
+    out_piece.wait()
 
     @pl.when(rank > 0)
     def _():
@@ -900,25 +1117,35 @@
             halo(step).wait_send()
 
 
-def back_part(ident, lens, starts, grad_gu, gu_map, middle, grad, gain, out_weight, edge, qkv, qkv_map):
+def back_part(
+    ident, lens, starts, grad_gu, gu_map, middle, grad, gain, out_weight, edge, qkv, qkv_map, gu_x, down_x
+):
     size, parts = lax.axis_size("fsdp"), lax.axis_size("seq")
     rows, width = middle.shape
     local = out_weight.shape[0]
+    n = parts // 2
     vmem = pl.BlockSpec(memory_space=pltpu.VMEM)
     smem = pl.BlockSpec(memory_space=pltpu.SMEM)
     hbm = pl.BlockSpec(memory_space=pl.ANY)
-    sems = [pltpu.SemaphoreType.DMA((transfers(size),))] * 2
-    return pl.pallas_call(
+    dma = lambda *s: pltpu.SemaphoreType.DMA(s)
+    low = lambda *s: jax.ShapeDtypeStruct(s, BF)
+    sems = [dma(transfers(size))] * 2
+    gu, down = gu_x.shape[1:], down_x.shape[1:]
+    outs = pl.pallas_call(
         functools.partial(back_kernel, size, parts, lens.shape[1]),
         out_shape=[
             jax.ShapeDtypeStruct((rows, width), F32),
             jax.ShapeDtypeStruct((1, width), F32),
-            jax.ShapeDtypeStruct((size, rows, width), BF),
-            jax.ShapeDtypeStruct(qkv.shape, BF),
+            low(size, rows, width),
+            low(*qkv.shape),
             jax.ShapeDtypeStruct((rows, width), F32),
-        ],
-        in_specs=[smem, smem, hbm, hbm] + [vmem] * 6 + [hbm],
-        out_specs=[vmem] * 5,
+            low(*gu),
+            low(parts, *down),
+        ]
+        + [low(n, *gu)] * 3
+        + [low(n, *down)] * 3,
+        in_specs=[smem, smem, hbm, hbm] + [vmem] * 6 + [hbm] * 3,
+        out_specs=[vmem] * 5 + [hbm] * 8,
         scratch_shapes=scatter_shapes(size, rows, width)
         + sems
         + sems
@@ -929,10 +1156,17 @@
             pltpu.VMEM((size, WINDOW, 2 * local), BF),
             pltpu.VMEM((size, WINDOW, 2 * local), BF),
             pltpu.VMEM((size, WINDOW, 3 * local), F32),
-            pltpu.SemaphoreType.DMA((size,)),
-            pltpu.SemaphoreType.DMA((size,)),
-            pltpu.SemaphoreType.DMA((3,)),
-        ],
+            dma(size),
+            dma(size),
+            dma(3),
+            pltpu.VMEM((n,) + gu, BF),
+            pltpu.VMEM((2,) + gu, BF),
+            dma(2),
+            pltpu.VMEM((n,) + down, BF),
+            pltpu.VMEM((2,) + down, BF),
+            dma(2),
+        ]
+        + line_sems(parts) * 3,
         compiler_params=pltpu.CompilerParams(
             collective_id=ident, has_side_effects=True, vmem_limit_bytes=67_000_000
         ),
@@ -942,131 +1176,53 @@
             transcendentals=0,
         ),
         name="back_part",
-    )(lens, starts, grad_gu, gu_map, middle, grad, gain, out_weight, edge, qkv, qkv_map)
-
-
-class LineSum:
-    def __init__(self, line, x, pre, acc, up_in, down_in, sems):
-        self.line, self.x, self.pre, self.acc = line, x, pre, acc
-        self.up_in, self.down_in, self.sems = up_in, down_in, sems
-
-    def share(self, k):
-        line = self.line
-        src = self.x.at[2 * k + 1 - line.core]
-        return remote(src, self.pre.at[k], self.sems[0].at[k], self.sems[1].at[k], seq=line.beside)
-
-    def up(self, k):
-        sems = self.sems[2].at[k], self.sems[3].at[k]
-        return remote(self.acc.at[k], self.up_in.at[k], *sems, seq=self.line.above)
-
-    def down(self, k):
-        sems = self.sems[4].at[k], self.sems[5].at[k]
-        return remote(self.acc.at[k], self.down_in.at[k], *sems, seq=self.line.below)
-
-    def order(self):
-        n = self.line.length
-        return [k // 2 if k % 2 else n - 1 - k // 2 for k in range(n)]
-
-    def trade(self):
-        for k in self.order():
-            self.share(k).start()
-
-    def merge(self):
-        line = self.line
-        for k in self.order():
-            self.share(k).wait_recv()
-            own = self.x[2 * k + line.core].astype(F32)
-            self.acc[k] = (own + self.pre[k].astype(F32)).astype(BF)
-            if k > 0:
-                pl.when(line.z == 0)(lambda: self.up(k).start())
-            if k < line.length - 1:
-                pl.when(line.z == line.length - 1)(lambda: self.down(k).start())
-
-    def add(self, k, more):
-        self.acc[k] = (self.acc[k].astype(F32) + more[k].astype(F32)).astype(BF)
-
-    def pass_up(self, k):
-        z = self.line.z
-
-        @pl.when((z > 0) & (z < k))
-        def _():
-            self.up(k).wait_recv()
-            self.add(k, self.up_in)
-            self.up(k).start()
-
-    def pass_down(self, k):
-        z = self.line.z
-
-        @pl.when((z < self.line.length - 1) & (z > k))
-        def _():
-            self.down(k).wait_recv()
-            self.add(k, self.down_in)
-            self.down(k).start()
-
-    def total(self):
-        z = self.line.z
-
-        @pl.when(z > 0)
-        def _():
-            self.up(z).wait_recv()
-            self.add(z, self.up_in)
-
-        @pl.when(z < self.line.length - 1)
-        def _():
-            self.down(z).wait_recv()
-            self.add(z, self.down_in)
-
-    def finish(self):
-        for k in range(self.line.length):
-            self.share(k).wait_send()
-            pl.when(k > self.line.z)(lambda: self.up(k).wait_send())
-            pl.when(k < self.line.z)(lambda: self.down(k).wait_send())
-
-
-CLOSE_REFS = (
-    "x",
-    "gu_piece",
-    "terms",
-    "hidden",
-    "down_map",
-    "every_hbm",
-    "gu_every_hbm",
-    "feed",
-    "terms_out",
-    "part",
-    "first",
-    "over",
-    "joined",
-    "last",
-    "pre",
-    "acc",
-    "up_in",
-    "down_in",
-    "every",
-    "slots",
-    "gu_every",
-    "terms_in",
-    "terms_all",
-    "s_send",
-    "s_recv",
-    "m_send",
-    "m_recv",
-    "t_send",
-    "t_recv",
-    "loads",
-)
+    )(lens, starts, grad_gu, gu_map, middle, grad, gain, out_weight, edge, qkv, qkv_map, gu_x, down_x)
+    return outs[:7]
+
+
+class CloseRefs(NamedTuple):
+    x: Any
+    gu_piece: Any
+    terms: Any
+    hidden: Any
+    down_map: Any
+    every_hbm: Any
+    gu_every_hbm: Any
+    feed: Any
+    terms_out: Any
+    part: Any
+    first: Any
+    over: Any
+    joined: Any
+    last: Any
+    pre: Any
+    acc: Any
+    up_in: Any
+    down_in: Any
+    every: Any
+    slots: Any
+    gu_every: Any
+    terms_in: Any
+    terms_all: Any
+    s_send: Any
+    s_recv: Any
+    m_send: Any
+    m_recv: Any
+    t_send: Any
+    t_recv: Any
+    loads: Any
 
 
 def close_kernel(size, parts, *refs):
-    r = dict(zip(CLOSE_REFS, refs))
-    sems = refs[len(CLOSE_REFS) :]
+    named = len(CloseRefs._fields)
+    r, sems = CloseRefs(*refs[:named]), refs[named:]
     rank = lax.axis_index("seq")
     group = Group(size)
     me = group.me
     line_u, line_q = Line(parts, sems[:6]), Line(parts, sems[6:12])
     n, z = line_q.length, line_q.z
-    sums = LineSum(line_q, *(r[k] for k in ("x", "pre", "acc", "up_in", "down_in")), sems[12:])
-    rows = r["feed"].shape[0]
+    sums = LineSum(line_q, r.x, r.pre, r.acc, r.up_in, r.down_in, sems[12:])
+    rows = r.feed.shape[0]
     half = rows // 2
     barrier = pltpu.get_barrier_semaphore()
     greet_group(barrier, size)
@@ -1074,21 +1230,21 @@
         peer = lax.rem(rank + step, parts)
         pl.semaphore_signal(barrier, inc=1, device_id={"seq": peer}, device_id_type=MESH_ID)
     own_piece = pltpu.make_async_copy(
-        r["gu_piece"].at[me], r["gu_every"].at[rank, me], r["loads"].at[0]
+        r.gu_piece.at[me], r.gu_every.at[rank, me], r.loads.at[0]
     )
     own_piece.start()
-    r["terms_in"][me] = r["terms"][me]
+    r.terms_in[me] = r.terms[me]
     pl.semaphore_wait(barrier, size + parts - 2)
     sums.trade()
 
     def swap(k, step):
         peer = lax.rem(me + step, size)
         src, dst = (
-            lambda: (r["gu_piece"].at[peer], r["gu_every"].at[rank, me]),
-            lambda: (r["terms"].at[peer], r["terms_in"].at[me]),
-            lambda: (r["acc"].at[z, peer], r["slots"].at[me]),
+            lambda: (r.gu_piece.at[peer], r.gu_every.at[rank, me]),
+            lambda: (r.terms.at[peer], r.terms_in.at[me]),
+            lambda: (r.acc.at[z, peer], r.slots.at[me]),
         )[k]()
-        return remote(src, dst, r["m_send"].at[k, step - 1], r["m_recv"].at[k, step - 1], fsdp=peer)
+        return remote(src, dst, r.m_send.at[k, step - 1], r.m_recv.at[k, step - 1], fsdp=peer)
 
     others = range(1, size)
     for k in range(2):
@@ -1096,43 +1252,43 @@
             swap(k, step).start()
 
     scatter = Scatter(
-        group, *(r[k] for k in ("part", "first", "over", "joined", "last", "s_send", "s_recv"))
+        group, r.part, r.first, r.over, r.joined, r.last, r.s_send, r.s_recv
     )
 
     def down(step, is_step):
-        partial = dot(r["hidden"][group.to_own(step)], r["down_map"][...])
-        is_step(size - 1)(lambda: r["feed"].__setitem__(..., partial))
-        pl.when(step < size - 1)(lambda: r["part"].__setitem__(step, partial.astype(BF)))
+        partial = dot(r.hidden[group.to_own(step)], r.down_map[...])
+        is_step(size - 1)(lambda: r.feed.__setitem__(..., partial))
+        pl.when(step < size - 1)(lambda: r.part.__setitem__(step, partial.astype(BF)))
         for k in range(size - 1):
             is_step(k)(functools.partial(scatter.made, k))
 
     each_step(size, down)
-    sums.merge()
+    for m in range(n):
+        sums.begin(m)
     own_piece.wait()
     for step in others:
         swap(0, step).wait_recv()
-    line_u.gather(lambda owner: r["gu_every"].at[owner])
+    line_u.gather(lambda owner: r.gu_every.at[owner])
 
     for step in others:
         swap(1, step).wait_recv()
-    small = r["terms_in"][0]
+    small = r.terms_in[0]
     for f in others:
-        small = small + r["terms_in"][f]
-    r["terms_all"][rank] = small
+        small = small + r.terms_in[f]
+    r.terms_all[rank] = small
 
     def spread(step):
         peer = lax.rem(rank + step, parts)
-        view = r["terms_all"].at[rank]
-        return remote(view, view, r["t_send"].at[step - 1], r["t_recv"].at[step - 1], seq=peer)
+        view = r.terms_all.at[rank]
+        return remote(view, view, r.t_send.at[step - 1], r.t_recv.at[step - 1], seq=peer)
 
     for step in range(1, parts):
         spread(step).start()
     scatter.join()
 
-    for k in range(n - 1):
-        sums.pass_up(n - 1 - k)
-        sums.pass_down(k)
-        if k == 0:
+    for m in range(n - 1):
+        sums.advance(m)
+        if m == 0:
             pl.when(z >= 2)(lambda: line_u.relay_up(1))
             pl.when(z <= n - 3)(lambda: line_u.relay_down(1))
     sums.total()
@@ -1140,36 +1296,36 @@
         swap(2, step).start()
     for h in range(2):
         span = slice(h * half, (h + 1) * half)
-        r["feed"][span, :] = r["feed"][span, :] + scatter.total(h)
+        r.feed[span, :] = r.feed[span, :] + scatter.total(h)
     pl.when(z < 2)(lambda: line_u.relay_up(1))
     pl.when(z > n - 3)(lambda: line_u.relay_down(1))
-    r["slots"][me] = r["acc"][z, me]
+    r.slots[me] = r.acc[z, me]
     for step in others:
         swap(2, step).wait_recv()
-    local = r["x"].shape[3] // 4
+    local = r.x.shape[3] // 4
     lane = lax.broadcasted_iota(jnp.int32, (1, 1, 4 * local), 2)
-    r["every"][rank] = jnp.where(lane < 3 * local, r["slots"][...], r["acc"][z])
-    line_q.gather(lambda owner: r["every"].at[owner])
+    r.every[rank] = jnp.where(lane < 3 * local, r.slots[...], r.acc[z])
+    line_q.gather(lambda owner: r.every.at[owner])
     for j in range(2, n):
         line_u.relay(j)
         line_q.relay(j - 1)
     for j in range(1, n):
         line_u.close(j)
     line_u.gathered()
-    stores = [pltpu.make_async_copy(r["gu_every"], r["gu_every_hbm"], r["loads"].at[0])]
+    stores = [pltpu.make_async_copy(r.gu_every, r.gu_every_hbm, r.loads.at[0])]
     stores[0].start()
     line_q.relay(n - 1)
     for j in range(1, n):
         line_q.close(j)
     line_q.gathered()
-    stores.append(pltpu.make_async_copy(r["every"], r["every_hbm"], r["loads"].at[1]))
+    stores.append(pltpu.make_async_copy(r.every, r.every_hbm, r.loads.at[1]))
     stores[1].start()
     for step in range(1, parts):
         spread(step).wait_recv()
-    small = r["terms_all"][0]
+    small = r.terms_all[0]
     for k in range(1, parts):
-        small = small + r["terms_all"][k]
-    r["terms_out"][...] = small
+        small = small + r.terms_all[k]
+    r.terms_out[...] = small
     for k in range(3):
         for step in others:
             swap(k, step).wait_send()
@@ -1416,12 +1572,8 @@
     )
 
     gu_packed = pack_grads(parts, size, flat(normed_all), flat(grad_gu))
-    gu_packed, grad_gu = lax.optimization_barrier((gu_packed, grad_gu))
-    gu_piece = lax.psum_scatter(gu_packed, "seq", scatter_dimension=0)
-    down_sum = dot_rows(flat(hidden), grad_down_all).astype(BF)
-    grad_gu, down_sum = lax.optimization_barrier((grad_gu, down_sum))
-    down_total = lax.psum(down_sum, "seq").astype(F32)
-    grad_middle, norm2_term, grad_branch_all, dqkv, grad_gated = back_part(
+    down_packed = dot_rows(flat(hidden), grad_down_all).astype(BF)
+    grad_middle, norm2_term, grad_branch_all, dqkv, grad_gated, gu_piece, down_every = back_part(
         4,
         lens_all,
         starts_all,
@@ -1434,8 +1586,11 @@
         edge,
         qkv,
         qkv_map,
+        gu_packed,
+        down_packed.reshape(parts, -1, width),
     )
     norm2_term = norm2_term[0]
+    down_total = down_every.reshape(-1, width).astype(F32)
     qkvo_packed = pack_grads(
         parts, size, flat(gated_all), flat(dqkv), flat(heads_out), flat(grad_branch_all)
     )

time: 669 us -> 706 us (1.055)
  Pallas kernels: 546 us -> 642 us
  waiting for transfers between devices: 44.6 us -> 0.01 us
  between operations: 16 us -> 2.83 us
    pallas_call x1, Pallas kernels: 121 us -> 214 us  [back_part(): pl.pallas_call(functools.partial(back_kernel, size, parts, lens.shape[1])...]
    reduce_scatter x1 -> x0, waiting for transfers between devices: 43.9 us -> none  [shards(): gu_piece = lax.psum_scatter(gu_packed, 'seq', scatter_dimension=0)]
  transfers between devices with their start and end apart: 4 -> 2, of which waited for: 1 -> 0; matrix products, arithmetic and copies ran while one was open for 5% -> 2% of each run, Pallas kernels for 20% -> 2%
where the time goes in v1:
time: 706 us; the launch traced here: 696 us
  Pallas kernels  642 us (91%)
  other arithmetic  23.2 us (3%)
  local copies, waits for them, and re-layouts  15.2 us (2%)
  matrix products  9.64 us (1%)
    pallas_call x1, Pallas kernels, back_part(): pl.pallas_call(functools.partial(back_kernel, size, parts, lens.shape[1])...  214 us
    pallas_call x1, Pallas kernels, close_part(): pl.pallas_call(functools.partial(close_kernel, size, parts), out_shape=[j...  205 us
    pallas_call x1, Pallas kernels, forward_part(): pl.pallas_call(functools.partial(forward_kernel, size, parts, count), out...  174 us
    pallas_call x2, Pallas kernels, pack_grads(): pl.pallas_call(functools.partial(pack_kernel, size, parts), grid=(size //...  28.6 us
    pallas_call x2, Pallas kernels, unpack_grads(): pl.pallas_call(functools.partial(unpack_kernel, widths), grid=(parts,), o...  20.1 us
  transfers between devices with their start and end apart: 2, of which 0 were waited for; matrix products, arithmetic and copies ran while one was open for 2% of the time, Pallas kernels for 2%

profile of v1, /device:TPU:0, one launch (start us, length us, event | category | flops | bytes accessed | tf_op | source)
XLA Modules:
  0.0 696.4 jit_solution(10733094862734171849)
XLA Ops:
  1.4 2.4 collective-permute-start
  4.8 1.3 constant_dynamic-slice_fusion
  10.7 1.3 maximum_bitcast_fusion.refs_6_
  12.0 1.1 fusion.10.refs_2_.refs_5_
  14.9 1.1 concatenate.17
  16.6 174.4 %forward_part.1 = (bf16[4,256,1792]{2,1,0:T(8,128)(2,1)}, bf16[4,256,1344]{2,1,0:T(8,128)(2,1)}, bf16[4,64,896]{2,1,0:T(8,128)(2,1)}, bf16[4,8,56,1344]{3,2,1,0:...) custom-call(bf16[256,1792]{1,0:T(8,128)(2,1)} %bitcast.44, ...), custom_call_target="tpu_custom_call" | custom-call | flops 19964887040 | bytes 500000000 | tf_op jit(solution)/shard_map/forward_part/pallas_call | solution.py:789
  193.3 1.4 fusion.19
  194.8 1.6 fusion.8
  197.3 9.6 %bitcast_convert_fusion = bf16[1216,1792]{1,0:T(8,128)(2,1)} fusion(bf16[4,256,1216]{2,1,0:T(8,128)(2,1)} %get-tuple-element.81.refs_3_, bf16[4,256,1792]{2,1,0:T(8,128)(2,1)} %get-tuple-element.82), kind=kOutput, calls=%fused_computation | convolution fusion | flops 4464918528 | bytes 10518528 | tf_op jit(solution)/shard_map/dot_general | solution.py:39
  206.9 14.9 %pack_grads.2.refs_11_ = bf16[8,4,56,2432]{3,2,1,0:T(8,128)(2,1)} custom-call(bf16[1024,1792]{1,0:T(8,128)(2,1)} %bitcast.67, bf16[1024,2432]{1,0:T(8,128)(2,1)} %bitcast.63), custom_call_target="tpu_custom_call" | custom-call | flops 8925478912 | bytes 17367040 | tf_op jit(solution)/shard_map/pack_grads/pallas_call | solution.py:1424
  221.8 213.7 %back_part.1 = (f32[256,1792]{1,0:T(8,128)}, f32[1,1792]{1,0:T(1,128)}, bf16[4,256,1792]{2,1,0:T(8,128)(2,1)}, bf16[4,256,1344]{2,1,0:T(8,128)(2,1)}, f32[256,17...) custom-call(s32[4,1]{1,0:T(4,128)} %bitcast.58, ...), custom_call_target="tpu_custom_call" | custom-call | flops 15502147584 | bytes 400000000 | tf_op jit(solution)/shard_map/back_part/pallas_call | solution.py:1134
  435.6 1.7 fusion.3
  438.3 1.2 multiply_add_fusion
  439.8 1.5 fusion.5
  442.0 1.3 collective-permute-start.1
  443.3 4.4 bitcast_convert_fusion.1
  447.8 13.7 %pack_grads.3.refs_0_ = bf16[8,4,56,1792]{3,2,1,0:T(8,128)(2,1)} custom-call(bf16[1024,1792]{1,0:T(8,128)(2,1)} %bitcast.65, bf16[1024,1344]{1,0:T(8,128)(2,1)} %bitcast.68, bf16[1024,448]{1,0:T(8,128)(2,1)} %bitcast.69, bf16[1024,1792]{1,0:T(8,128)(2,1)} %bitcast.66), custom_call_target="tpu_custom_call" | custom-call | flops 6576668672 | bytes 12845056 | tf_op jit(solution)/shard_map/pack_grads/pallas_call | solution.py:1424
  462.4 3.0 fusion.9
  465.4 205.0 %close_part.1 = (bf16[8,4,56,1792]{3,2,1,0:T(8,128)(2,1)}, bf16[8,4,56,2432]{3,2,1,0:T(8,128)(2,1)}, f32[256,1792]{1,0:T(8,128)}, f32[8,448]{1,0:T(8,128)}) custom-call(bf16[8,4,56,1792]{3,2,1,0:T(8,128)(2,1)} %pack_grads.3.refs_0_, bf16[4,56,2432]{2,1,0:T(8,128)(2,1)} %get-tuple-element.92.refs_1_, f32[4,8,448]{2,1,0:T(8,128)} %bitcast.53, ...), custom_call_target="tpu_custom_call" | custom-call | flops 4462739456 | bytes 500000000 | tf_op jit(solution)/shard_map/close_part/pallas_call | solution.py:1352
  670.4 1.3 slice_bitcast_fusion
  671.8 1.4 fusion.18
  673.1 10.8 %unpack_grads.3 = (f32[448,4864]{1,0:T(8,128)}, f32[448,4864]{1,0:T(8,128)}) custom-call(bf16[8,4,56,2432]{3,2,1,0:T(8,128)(2,1)} %get-tuple-element.102.every_ref), custom_call_target="tpu_custom_call" | custom-call | bytes 26148864 | tf_op jit(solution)/shard_map/unpack_grads/pallas_call | solution.py:1457
  684.0 9.2 %unpack_grads.2 = (f32[448,1792]{1,0:T(8,128)}, f32[448,1792]{1,0:T(8,128)}, f32[448,1792]{1,0:T(8,128)}, f32[448,1792]{1,0:T(8,128)}) custom-call(bf16[8,4,56,1792]{3,2,1,0:T(8,128)(2,1)} %get-tuple-element.97.every_ref), custom_call_target="tpu_custom_call" | custom-call | bytes 19267584 | tf_op jit(solution)/shard_map/unpack_grads/pallas_call | solution.py:1457
  693.2 2.8 fusion.11
  (75 shorter events, 13.4 us)
Async XLA Ops:
  1.4 14.6 %collective-permute-start = (bf16[2,1792]{1,0:T(2,128)(2,1)S(1)}, bf16[2,1792]{1,0:T(2,128)(2,1)S(1)}, u32[]{:S(2)}, u32[]{:S(2)}) collective-permute-start(bf16[2,1792]{1,0:T(2,128)(2,1)S(1)} %slice_bitcast_fusion.1), channel_id=1, source_target_pairs={{0,4},{4,8},{8,12},{12,16},{16,20},{20,24},{24,28},{1,5},{5,9},{9,... | collective-permute-start | bytes 21512 | tf_op jit(solution)/shard_map/ppermute | solution.py:27
  6.7 2.9 copy-start.10
  6.7 2.9 copy-start.11
  7.5 4.5 copy-start.3
  10.7 2.5 copy-start.9
  14.9 1.7 copy-start.8
  435.6 1.8 copy-start.1
  435.6 1.8 copy-start.5
  435.6 1.8 copy-start.6
  437.3 1.0 copy-start.4
  437.4 5.9 slice-start
  438.3 1.5 copy-start
  438.3 5.0 slice-start.1
  442.0 20.4 %collective-permute-start.1 = (f32[2,1792]{1,0:T(2,128)S(1)}, f32[2,1792]{1,0:T(2,128)S(1)}, u32[]{:S(2)}, u32[]{:S(2)}) collective-permute-start(f32[2,1792]{1,0:T(2,128)S(1)} %slice.141), channel_id=1, source_target_pairs={{4,0},{8,4},{12,8},{16,12},{20,16},{24,20},{28,24},{5,1},{9,5},{13... | collective-permute-start | bytes 43016 | tf_op jit(solution)/shard_map/ppermute | solution.py:27
  447.8 13.8 %copy-start.7 = (f32[1,1792]{1,0:T(1,128)S(1)}, f32[1,1792]{1,0:T(1,128)}, u32[]{:S(2)}) copy-start(f32[1,1792]{1,0:T(1,128)} %get-tuple-element.88) | copy-start | bytes 21508
  684.0 9.3 %copy-start.2 = (f32[256,1792]{1,0:T(8,128)S(1)}, f32[256,1792]{1,0:T(8,128)}, u32[]{:S(2)}) copy-start(f32[256,1792]{1,0:T(8,128)} %get-tuple-element.71.refs_4_) | copy-start | bytes 5505028

commit v2 on v1

--- a/solution.py
+++ b/solution.py
@@ -361,17 +361,17 @@
     def add(self, k, more):
         self.acc[k] = (self.acc[k].astype(F32) + more[k].astype(F32)).astype(BF)
 
-    def advance(self, m):
+    def advance(self, t):
         z, n = self.line.z, self.line.length
-        far, near = self.pair(m)
-
-        @pl.when((z > 0) & (z < far))
+        far, near = n - 1 + z - t, t - n + 1 + z
+
+        @pl.when((z >= 1) & (z <= t))
         def _():
             self.up(far).wait_recv()
             self.add(far, self.up_in)
             self.up(far).start()
 
-        @pl.when((z < n - 1) & (z > near))
+        @pl.when((z <= n - 2) & (z >= n - 1 - t))
         def _():
             self.down(near).wait_recv()
             self.add(near, self.down_in)
@@ -998,6 +998,7 @@
         down_sum.begin(m)
     scatter.join()
     gu_sum.begin(0)
+    down_sum.advance(1)
     half = rows // 2
     norm_sum = jnp.zeros((1, r.middle.shape[1]), F32)
     for h in range(2):
@@ -1016,11 +1017,7 @@
         r.all[group.me, span] = grad_middle.astype(BF)
         gather.start_half(h)
     r.norm[...] = norm_sum
-    for m in range(1, n - 2):
-        gu_sum.begin(m)
-    down_sum.advance(0)
     own_down = pltpu.make_async_copy(r.down_acc.at[z], r.down_every.at[rank], r.down_load.at[0])
-    last_step = size - 1
 
     def halo(step):
         g = group.from_own(step)
@@ -1033,8 +1030,8 @@
         @is_step(1)
         def _():
             gather.relay()
-            for m in range(1, n - 1):
-                down_sum.advance(m)
+            for t in range(2, n - 1):
+                down_sum.advance(t)
 
         @is_step(2)
         def _():
@@ -1042,12 +1039,8 @@
             own_down.start()
             own_down.wait()
             line.gather(lambda owner: r.down_every.at[owner])
-            for m in range(max(1, n - 2), n):
+            for m in range(1, n):
                 gu_sum.begin(m)
-
-        @is_step(last_step)
-        def _():
-            gu_sum.advance(0)
 
         for k in range(1, size):
             is_step(k)(functools.partial(gather.ready, k))
@@ -1062,6 +1055,7 @@
         pl.when(rank > 0)(lambda: halo(step).start())
 
     each_step(size, step_heads)
+    gu_sum.advance(1)
     scatter.finish()
     fetches[2].wait()
 
@@ -1090,11 +1084,12 @@
             is_step(k)(functools.partial(scatter.made, k))
 
     each_step(size, step_one)
+    line.relay(1)
     scatter.join()
-    line.relay(1)
-    for m in range(1, n - 1):
-        gu_sum.advance(m)
-        line.relay(m + 1)
+    for t in range(2, n - 1):
+        gu_sum.advance(t)
+        line.relay(t)
+    line.relay(n - 1)
     for h in range(2):
         span = slice(h * half, (h + 1) * half)
         r.own[span, :] = r.own[span, :] + scatter.total(h)
@@ -1262,9 +1257,9 @@
         for k in range(size - 1):
             is_step(k)(functools.partial(scatter.made, k))
 
-    each_step(size, down)
     for m in range(n):
         sums.begin(m)
+    each_step(size, down)
     own_piece.wait()
     for step in others:
         swap(0, step).wait_recv()
@@ -1286,9 +1281,9 @@
         spread(step).start()
     scatter.join()
 
-    for m in range(n - 1):
-        sums.advance(m)
-        if m == 0:
+    for t in range(1, n - 1):
+        sums.advance(t)
+        if t == 1:
             pl.when(z >= 2)(lambda: line_u.relay_up(1))
             pl.when(z <= n - 3)(lambda: line_u.relay_down(1))
     sums.total()

time: 706 us -> 653 us (0.925)
  Pallas kernels: 642 us -> 589 us
    pallas_call x1, Pallas kernels: 214 us -> 180 us  [back_part(): pl.pallas_call(functools.partial(back_kernel, size, parts, lens.shape[1])...]
    pallas_call x1, Pallas kernels: 205 us -> 186 us  [close_part(): pl.pallas_call(functools.partial(close_kernel, size, parts), out_shape=[j...]
where the time goes in v2:
time: 653 us; the launch traced here: 644 us
  Pallas kernels  589 us (90%)
  other arithmetic  23.2 us (4%)
  local copies, waits for them, and re-layouts  15.2 us (2%)
  matrix products  9.64 us (1%)
    pallas_call x1, Pallas kernels, close_part(): pl.pallas_call(functools.partial(close_kernel, size, parts), out_shape=[j...  186 us
    pallas_call x1, Pallas kernels, back_part(): pl.pallas_call(functools.partial(back_kernel, size, parts, lens.shape[1])...  180 us
    pallas_call x1, Pallas kernels, forward_part(): pl.pallas_call(functools.partial(forward_kernel, size, parts, count), out...  175 us
    pallas_call x2, Pallas kernels, pack_grads(): pl.pallas_call(functools.partial(pack_kernel, size, parts), grid=(size //...  28.4 us
    pallas_call x2, Pallas kernels, unpack_grads(): pl.pallas_call(functools.partial(unpack_kernel, widths), grid=(parts,), o...  20.1 us
  transfers between devices with their start and end apart: 2, of which 0 were waited for; matrix products, arithmetic and copies ran while one was open for 2% of the time, Pallas kernels for 2%

profile of v2, /device:TPU:0, one launch (start us, length us, event | category | flops | bytes accessed | tf_op | source)
XLA Modules:
  0.0 643.8 jit_solution(6637339058669233027)
XLA Ops:
  1.4 2.4 collective-permute-start
  4.8 1.3 constant_dynamic-slice_fusion
  10.7 1.3 maximum_bitcast_fusion.refs_6_
  12.0 1.1 fusion.10.refs_2_.refs_5_
  14.9 1.1 concatenate.17
  16.6 174.5 %forward_part.1 = (bf16[4,256,1792]{2,1,0:T(8,128)(2,1)}, bf16[4,256,1344]{2,1,0:T(8,128)(2,1)}, bf16[4,64,896]{2,1,0:T(8,128)(2,1)}, bf16[4,8,56,1344]{3,2,1,0:...) custom-call(bf16[256,1792]{1,0:T(8,128)(2,1)} %bitcast.44, ...), custom_call_target="tpu_custom_call" | custom-call | flops 19964887040 | bytes 500000000 | tf_op jit(solution)/shard_map/forward_part/pallas_call | solution.py:789
  193.5 1.4 fusion.19
  194.9 1.6 fusion.8
  197.4 9.6 %bitcast_convert_fusion = bf16[1216,1792]{1,0:T(8,128)(2,1)} fusion(bf16[4,256,1216]{2,1,0:T(8,128)(2,1)} %get-tuple-element.81.refs_3_, bf16[4,256,1792]{2,1,0:T(8,128)(2,1)} %get-tuple-element.82), kind=kOutput, calls=%fused_computation | convolution fusion | flops 4464918528 | bytes 10518528 | tf_op jit(solution)/shard_map/dot_general | solution.py:39
  207.1 14.9 %pack_grads.2.refs_11_ = bf16[8,4,56,2432]{3,2,1,0:T(8,128)(2,1)} custom-call(bf16[1024,1792]{1,0:T(8,128)(2,1)} %bitcast.67, bf16[1024,2432]{1,0:T(8,128)(2,1)} %bitcast.63), custom_call_target="tpu_custom_call" | custom-call | flops 8925478912 | bytes 17367040 | tf_op jit(solution)/shard_map/pack_grads/pallas_call | solution.py:1419
  222.0 180.0 %back_part.1 = (f32[256,1792]{1,0:T(8,128)}, f32[1,1792]{1,0:T(1,128)}, bf16[4,256,1792]{2,1,0:T(8,128)(2,1)}, bf16[4,256,1344]{2,1,0:T(8,128)(2,1)}, f32[256,17...) custom-call(s32[4,1]{1,0:T(4,128)} %bitcast.58, ...), custom_call_target="tpu_custom_call" | custom-call | flops 15502147584 | bytes 400000000 | tf_op jit(solution)/shard_map/back_part/pallas_call | solution.py:1129
  402.1 1.7 fusion.3
  404.8 1.2 multiply_add_fusion
  406.3 1.5 fusion.5
  408.5 1.5 collective-permute-start.1
  410.0 4.4 bitcast_convert_fusion.1
  414.4 13.5 %pack_grads.3.refs_0_ = bf16[8,4,56,1792]{3,2,1,0:T(8,128)(2,1)} custom-call(bf16[1024,1792]{1,0:T(8,128)(2,1)} %bitcast.65, bf16[1024,1344]{1,0:T(8,128)(2,1)} %bitcast.68, bf16[1024,448]{1,0:T(8,128)(2,1)} %bitcast.69, bf16[1024,1792]{1,0:T(8,128)(2,1)} %bitcast.66), custom_call_target="tpu_custom_call" | custom-call | flops 6576668672 | bytes 12845056 | tf_op jit(solution)/shard_map/pack_grads/pallas_call | solution.py:1419
  428.8 3.0 fusion.9
  431.8 186.2 %close_part.1 = (bf16[8,4,56,1792]{3,2,1,0:T(8,128)(2,1)}, bf16[8,4,56,2432]{3,2,1,0:T(8,128)(2,1)}, f32[256,1792]{1,0:T(8,128)}, f32[8,448]{1,0:T(8,128)}) custom-call(bf16[8,4,56,1792]{3,2,1,0:T(8,128)(2,1)} %pack_grads.3.refs_0_, bf16[4,56,2432]{2,1,0:T(8,128)(2,1)} %get-tuple-element.92.refs_1_, f32[4,8,448]{2,1,0:T(8,128)} %bitcast.53, ...), custom_call_target="tpu_custom_call" | custom-call | flops 4462739456 | bytes 500000000 | tf_op jit(solution)/shard_map/close_part/pallas_call | solution.py:1347
  618.0 1.3 slice_bitcast_fusion
  619.4 1.4 fusion.18
  620.7 10.8 %unpack_grads.3 = (f32[448,4864]{1,0:T(8,128)}, f32[448,4864]{1,0:T(8,128)}) custom-call(bf16[8,4,56,2432]{3,2,1,0:T(8,128)(2,1)} %get-tuple-element.102.every_ref), custom_call_target="tpu_custom_call" | custom-call | bytes 26148864 | tf_op jit(solution)/shard_map/unpack_grads/pallas_call | solution.py:1452
  631.6 9.2 %unpack_grads.2 = (f32[448,1792]{1,0:T(8,128)}, f32[448,1792]{1,0:T(8,128)}, f32[448,1792]{1,0:T(8,128)}, f32[448,1792]{1,0:T(8,128)}) custom-call(bf16[8,4,56,1792]{3,2,1,0:T(8,128)(2,1)} %get-tuple-element.97.every_ref), custom_call_target="tpu_custom_call" | custom-call | bytes 19267584 | tf_op jit(solution)/shard_map/unpack_grads/pallas_call | solution.py:1452
  640.8 2.8 fusion.11
  (75 shorter events, 13.4 us)
Async XLA Ops:
  1.4 14.6 %collective-permute-start = (bf16[2,1792]{1,0:T(2,128)(2,1)S(1)}, bf16[2,1792]{1,0:T(2,128)(2,1)S(1)}, u32[]{:S(2)}, u32[]{:S(2)}) collective-permute-start(bf16[2,1792]{1,0:T(2,128)(2,1)S(1)} %slice_bitcast_fusion.1), channel_id=1, source_target_pairs={{0,4},{4,8},{8,12},{12,16},{16,20},{20,24},{24,28},{1,5},{5,9},{9,... | collective-permute-start | bytes 21512 | tf_op jit(solution)/shard_map/ppermute | solution.py:27
  6.7 2.9 copy-start.10
  6.7 2.9 copy-start.11
  7.5 4.5 copy-start.3
  10.7 2.5 copy-start.9
  14.9 1.7 copy-start.8
  402.1 1.8 copy-start.1
  402.1 1.8 copy-start.5
  402.1 1.8 copy-start.6
  403.8 1.0 copy-start.4
  403.8 6.1 slice-start
  404.8 1.5 copy-start
  404.8 5.2 slice-start.1
  408.5 20.3 %collective-permute-start.1 = (f32[2,1792]{1,0:T(2,128)S(1)}, f32[2,1792]{1,0:T(2,128)S(1)}, u32[]{:S(2)}, u32[]{:S(2)}) collective-permute-start(f32[2,1792]{1,0:T(2,128)S(1)} %slice.141), channel_id=1, source_target_pairs={{4,0},{8,4},{12,8},{16,12},{20,16},{24,20},{28,24},{5,1},{9,5},{13... | collective-permute-start | bytes 43016 | tf_op jit(solution)/shard_map/ppermute | solution.py:27
  414.4 13.5 %copy-start.7 = (f32[1,1792]{1,0:T(1,128)S(1)}, f32[1,1792]{1,0:T(1,128)}, u32[]{:S(2)}) copy-start(f32[1,1792]{1,0:T(1,128)} %get-tuple-element.88) | copy-start | bytes 21508
  631.6 9.3 %copy-start.2 = (f32[256,1792]{1,0:T(8,128)S(1)}, f32[256,1792]{1,0:T(8,128)}, u32[]{:S(2)}) copy-start(f32[256,1792]{1,0:T(8,128)} %get-tuple-element.71.refs_4_) | copy-start | bytes 5505028

commit v3 on v2

--- a/solution.py
+++ b/solution.py
@@ -898,7 +898,7 @@
     all: Any
     dqkv: Any
     own: Any
-    gu_piece: Any
+    gu_slots: Any
     down_every: Any
     gu_pre: Any
     gu_up: Any
@@ -932,6 +932,8 @@
     down_acc: Any
     down_stage: Any
     down_load: Any
+    m_send: Any
+    m_recv: Any
 
 
 def back_kernel(size, parts, count, *refs):
@@ -979,6 +981,8 @@
     pl.semaphore_wait(barrier, size - 1 + known)
     down_sum.trade()
     gu_sum.trade()
+    for m in range(n):
+        down_sum.begin(m)
     scatter = Scatter(
         group, r.part, r.first, r.over, r.joined, r.last, r.s_send, r.s_recv
     )
@@ -994,8 +998,6 @@
             is_step(k)(functools.partial(scatter.made, k))
 
     each_step(size, step_two)
-    for m in range(n):
-        down_sum.begin(m)
     scatter.join()
     gu_sum.begin(0)
     down_sum.advance(1)
@@ -1094,17 +1096,29 @@
         span = slice(h * half, (h + 1) * half)
         r.own[span, :] = r.own[span, :] + scatter.total(h)
     gu_sum.total()
-    out_piece = pltpu.make_async_copy(r.gu_acc.at[z], r.gu_piece, r.gu_load.at[0])
-    out_piece.start()
+
+    def swap(step):
+        peer = lax.rem(group.me + step, size)
+        sems = r.m_send.at[step - 1], r.m_recv.at[step - 1]
+        return remote(r.gu_acc.at[z, peer], r.gu_slots.at[group.me], *sems, fsdp=peer)
+
+    for step in range(1, size):
+        swap(step).start()
+    own_slot = pltpu.make_async_copy(
+        r.gu_acc.at[z, group.me], r.gu_slots.at[group.me], r.gu_load.at[0]
+    )
+    own_slot.start()
     for j in range(1, n):
         line.close(j)
     line.gathered()
+    for step in range(1, size):
+        swap(step).wait()
     scatter.finish()
     gather.finish()
     down_sum.finish()
     gu_sum.finish()
     line.finish()
-    out_piece.wait()
+    own_slot.wait()
 
     @pl.when(rank > 0)
     def _():
@@ -1160,6 +1174,8 @@
             pltpu.VMEM((n,) + down, BF),
             pltpu.VMEM((2,) + down, BF),
             dma(2),
+            dma(size - 1),
+            dma(size - 1),
         ]
         + line_sems(parts) * 3,
         compiler_params=pltpu.CompilerParams(
@@ -1177,7 +1193,7 @@
 
 class CloseRefs(NamedTuple):
     x: Any
-    gu_piece: Any
+    gu_slots: Any
     terms: Any
     hidden: Any
     down_map: Any
@@ -1224,27 +1240,25 @@
     for step in range(1, parts):
         peer = lax.rem(rank + step, parts)
         pl.semaphore_signal(barrier, inc=1, device_id={"seq": peer}, device_id_type=MESH_ID)
-    own_piece = pltpu.make_async_copy(
-        r.gu_piece.at[me], r.gu_every.at[rank, me], r.loads.at[0]
-    )
-    own_piece.start()
+    own_slots = pltpu.make_async_copy(r.gu_slots, r.gu_every.at[rank], r.loads.at[0])
+    own_slots.start()
     r.terms_in[me] = r.terms[me]
     pl.semaphore_wait(barrier, size + parts - 2)
     sums.trade()
+    own_slots.wait()
+    line_u.gather(lambda owner: r.gu_every.at[owner])
 
     def swap(k, step):
         peer = lax.rem(me + step, size)
         src, dst = (
-            lambda: (r.gu_piece.at[peer], r.gu_every.at[rank, me]),
             lambda: (r.terms.at[peer], r.terms_in.at[me]),
             lambda: (r.acc.at[z, peer], r.slots.at[me]),
         )[k]()
         return remote(src, dst, r.m_send.at[k, step - 1], r.m_recv.at[k, step - 1], fsdp=peer)
 
     others = range(1, size)
-    for k in range(2):
-        for step in others:
-            swap(k, step).start()
+    for step in others:
+        swap(0, step).start()
 
     scatter = Scatter(
         group, r.part, r.first, r.over, r.joined, r.last, r.s_send, r.s_recv
@@ -1260,13 +1274,10 @@
     for m in range(n):
         sums.begin(m)
     each_step(size, down)
-    own_piece.wait()
+    line_u.relay(1)
+
     for step in others:
         swap(0, step).wait_recv()
-    line_u.gather(lambda owner: r.gu_every.at[owner])
-
-    for step in others:
-        swap(1, step).wait_recv()
     small = r.terms_in[0]
     for f in others:
         small = small + r.terms_in[f]
@@ -1283,33 +1294,27 @@
 
     for t in range(1, n - 1):
         sums.advance(t)
-        if t == 1:
-            pl.when(z >= 2)(lambda: line_u.relay_up(1))
-            pl.when(z <= n - 3)(lambda: line_u.relay_down(1))
-    sums.total()
-    for step in others:
-        swap(2, step).start()
+        line_u.relay(t + 1)
     for h in range(2):
         span = slice(h * half, (h + 1) * half)
         r.feed[span, :] = r.feed[span, :] + scatter.total(h)
-    pl.when(z < 2)(lambda: line_u.relay_up(1))
-    pl.when(z > n - 3)(lambda: line_u.relay_down(1))
+    sums.total()
+    for step in others:
+        swap(1, step).start()
+    for j in range(1, n):
+        line_u.close(j)
     r.slots[me] = r.acc[z, me]
     for step in others:
-        swap(2, step).wait_recv()
+        swap(1, step).wait_recv()
     local = r.x.shape[3] // 4
     lane = lax.broadcasted_iota(jnp.int32, (1, 1, 4 * local), 2)
     r.every[rank] = jnp.where(lane < 3 * local, r.slots[...], r.acc[z])
     line_q.gather(lambda owner: r.every.at[owner])
-    for j in range(2, n):
-        line_u.relay(j)
-        line_q.relay(j - 1)
-    for j in range(1, n):
-        line_u.close(j)
     line_u.gathered()
     stores = [pltpu.make_async_copy(r.gu_every, r.gu_every_hbm, r.loads.at[0])]
     stores[0].start()
-    line_q.relay(n - 1)
+    for j in range(1, n):
+        line_q.relay(j)
     for j in range(1, n):
         line_q.close(j)
     line_q.gathered()
@@ -1321,7 +1326,7 @@
     for k in range(1, parts):
         small = small + r.terms_all[k]
     r.terms_out[...] = small
-    for k in range(3):
+    for k in range(2):
         for step in others:
             swap(k, step).wait_send()
     for step in range(1, parts):
@@ -1334,14 +1339,14 @@
         store.wait()
 
 
-def close_part(ident, packed, gu_piece, terms, hidden, down_weight):
+def close_part(ident, packed, gu_slots, terms, hidden, down_weight):
     parts, size, piece, cols = packed.shape
     n = parts // 2
     rows, width = hidden.shape[1], down_weight.shape[1]
     vmem = pl.BlockSpec(memory_space=pltpu.VMEM)
     hbm = pl.BlockSpec(memory_space=pl.ANY)
     dma = lambda *s: pltpu.SemaphoreType.DMA(s)
-    gu_shape = (parts,) + gu_piece.shape
+    gu_shape = (parts,) + gu_slots.shape
     scratch = scatter_shapes(size, rows, width)
     chips = pltpu.VMEM((n, size, piece, cols), BF)
     return pl.pallas_call(
@@ -1367,7 +1372,7 @@
             pltpu.VMEM((parts,) + terms.shape[1:], F32),
         ]
         + scratch[-2:]
-        + [dma(3, size - 1)] * 2
+        + [dma(2, size - 1)] * 2
         + [dma(parts - 1)] * 2
         + [dma(2)]
         + line_sems(parts) * 3,
@@ -1378,7 +1383,7 @@
             flops=2 * size * rows * down_weight.size, bytes_accessed=500_000_000, transcendentals=0
         ),
         name="close_part",
-    )(packed, gu_piece, terms, hidden, down_weight)
+    )(packed, gu_slots, terms, hidden, down_weight)
 
 
 def pack_kernel(size, parts, x_ref, g_ref, *refs):
@@ -1568,7 +1573,7 @@
 
     gu_packed = pack_grads(parts, size, flat(normed_all), flat(grad_gu))
     down_packed = dot_rows(flat(hidden), grad_down_all).astype(BF)
-    grad_middle, norm2_term, grad_branch_all, dqkv, grad_gated, gu_piece, down_every = back_part(
+    grad_middle, norm2_term, grad_branch_all, dqkv, grad_gated, gu_slots, down_every = back_part(
         4,
         lens_all,
         starts_all,
@@ -1614,11 +1619,11 @@
         ]
     )
     terms = jnp.pad(terms, ((0, 3), (0, 0))).reshape(8, size, slice_width).transpose(1, 0, 2)
-    qkvo_packed, gu_piece, terms, down_total, tokens_grad = lax.optimization_barrier(
-        (qkvo_packed, gu_piece, terms, down_total, tokens_grad)
+    qkvo_packed, gu_slots, terms, down_total, tokens_grad = lax.optimization_barrier(
+        (qkvo_packed, gu_slots, terms, down_total, tokens_grad)
     )
     qkvo_every, gu_every, feed, terms = close_part(
-        5, qkvo_packed, gu_piece, terms, hidden, down_weight
+        5, qkvo_packed, gu_slots, terms, hidden, down_weight
     )
     gate_total, up_total = unpack_grads(gu_every, (gu_map.shape[1] // 2,) * 2)
     query_total, key_total, value_total, out_total = unpack_grads(qkvo_every, (local,) * 4)

time: 653 us -> 640 us (0.980)
  Pallas kernels: 589 us -> 575 us
    pallas_call x1, Pallas kernels: 186 us -> 176 us  [close_part(): pl.pallas_call(functools.partial(close_kernel, size, parts), out_shape=[j...]
  transfers between devices with their start and end apart: 2 -> 2, of which waited for: 0 -> 0; matrix products, arithmetic and copies ran while one was open for 2% -> 3% of each run, Pallas kernels for 2% -> 2%
where the time goes in v3:
time: 640 us; the launch traced here: 630 us
  Pallas kernels  575 us (90%)
  other arithmetic  23.2 us (4%)
  local copies, waits for them, and re-layouts  15.2 us (2%)
  matrix products  9.64 us (2%)
    pallas_call x1, Pallas kernels, back_part(): pl.pallas_call(functools.partial(back_kernel, size, parts, lens.shape[1])...  176 us
    pallas_call x1, Pallas kernels, close_part(): pl.pallas_call(functools.partial(close_kernel, size, parts), out_shape=[j...  176 us
    pallas_call x1, Pallas kernels, forward_part(): pl.pallas_call(functools.partial(forward_kernel, size, parts, count), out...  175 us
    pallas_call x2, Pallas kernels, pack_grads(): pl.pallas_call(functools.partial(pack_kernel, size, parts), grid=(size //...  28.4 us
    pallas_call x2, Pallas kernels, unpack_grads(): pl.pallas_call(functools.partial(unpack_kernel, widths), grid=(parts,), o...  20.1 us
  transfers between devices with their start and end apart: 2, of which 0 were waited for; matrix products, arithmetic and copies ran while one was open for 3% of the time, Pallas kernels for 2%

profile of v3, /device:TPU:0, one launch (start us, length us, event | category | flops | bytes accessed | tf_op | source)
XLA Modules:
  0.0 629.5 jit_solution(12311328095118023661)
XLA Ops:
  1.4 2.4 collective-permute-start
  4.8 1.3 constant_dynamic-slice_fusion
  10.7 1.3 maximum_bitcast_fusion.refs_6_
  12.0 1.1 fusion.10.refs_2_.refs_5_
  14.9 1.1 concatenate.17
  16.6 174.5 %forward_part.1 = (bf16[4,256,1792]{2,1,0:T(8,128)(2,1)}, bf16[4,256,1344]{2,1,0:T(8,128)(2,1)}, bf16[4,64,896]{2,1,0:T(8,128)(2,1)}, bf16[4,8,56,1344]{3,2,1,0:...) custom-call(bf16[256,1792]{1,0:T(8,128)(2,1)} %bitcast.44, ...), custom_call_target="tpu_custom_call" | custom-call | flops 19964887040 | bytes 500000000 | tf_op jit(solution)/shard_map/forward_part/pallas_call | solution.py:789
  193.5 1.4 fusion.19
  194.9 1.6 fusion.8
  197.4 9.6 %bitcast_convert_fusion = bf16[1216,1792]{1,0:T(8,128)(2,1)} fusion(bf16[4,256,1216]{2,1,0:T(8,128)(2,1)} %get-tuple-element.81.refs_3_, bf16[4,256,1792]{2,1,0:T(8,128)(2,1)} %get-tuple-element.82), kind=kOutput, calls=%fused_computation | convolution fusion | flops 4464918528 | bytes 10518528 | tf_op jit(solution)/shard_map/dot_general | solution.py:39
  207.1 14.9 %pack_grads.2.refs_11_ = bf16[8,4,56,2432]{3,2,1,0:T(8,128)(2,1)} custom-call(bf16[1024,1792]{1,0:T(8,128)(2,1)} %bitcast.67, bf16[1024,2432]{1,0:T(8,128)(2,1)} %bitcast.63), custom_call_target="tpu_custom_call" | custom-call | flops 8925478912 | bytes 17367040 | tf_op jit(solution)/shard_map/pack_grads/pallas_call | solution.py:1424
  222.0 176.2 %back_part.1 = (f32[256,1792]{1,0:T(8,128)}, f32[1,1792]{1,0:T(1,128)}, bf16[4,256,1792]{2,1,0:T(8,128)(2,1)}, bf16[4,256,1344]{2,1,0:T(8,128)(2,1)}, f32[256,17...) custom-call(s32[4,1]{1,0:T(4,128)} %bitcast.58, ...), custom_call_target="tpu_custom_call" | custom-call | flops 15502147584 | bytes 400000000 | tf_op jit(solution)/shard_map/back_part/pallas_call | solution.py:1143
  398.2 1.7 fusion.3
  400.9 1.2 multiply_add_fusion
  402.4 1.5 fusion.5
  404.6 1.5 collective-permute-start.1
  406.1 4.4 bitcast_convert_fusion.1
  410.5 13.5 %pack_grads.3.refs_0_ = bf16[8,4,56,1792]{3,2,1,0:T(8,128)(2,1)} custom-call(bf16[1024,1792]{1,0:T(8,128)(2,1)} %bitcast.65, bf16[1024,1344]{1,0:T(8,128)(2,1)} %bitcast.68, bf16[1024,448]{1,0:T(8,128)(2,1)} %bitcast.69, bf16[1024,1792]{1,0:T(8,128)(2,1)} %bitcast.66), custom_call_target="tpu_custom_call" | custom-call | flops 6576668672 | bytes 12845056 | tf_op jit(solution)/shard_map/pack_grads/pallas_call | solution.py:1424
  424.9 3.0 fusion.9
  427.9 175.8 %close_part.1 = (bf16[8,4,56,1792]{3,2,1,0:T(8,128)(2,1)}, bf16[8,4,56,2432]{3,2,1,0:T(8,128)(2,1)}, f32[256,1792]{1,0:T(8,128)}, f32[8,448]{1,0:T(8,128)}) custom-call(bf16[8,4,56,1792]{3,2,1,0:T(8,128)(2,1)} %pack_grads.3.refs_0_, bf16[4,56,2432]{2,1,0:T(8,128)(2,1)} %get-tuple-element.92.refs_1_, f32[4,8,448]{2,1,0:T(8,128)} %bitcast.53, ...), custom_call_target="tpu_custom_call" | custom-call | flops 4462739456 | bytes 500000000 | tf_op jit(solution)/shard_map/close_part/pallas_call | solution.py:1352
  603.8 1.3 slice_bitcast_fusion
  605.1 1.4 fusion.18
  606.5 10.8 %unpack_grads.3 = (f32[448,4864]{1,0:T(8,128)}, f32[448,4864]{1,0:T(8,128)}) custom-call(bf16[8,4,56,2432]{3,2,1,0:T(8,128)(2,1)} %get-tuple-element.102.every_ref), custom_call_target="tpu_custom_call" | custom-call | bytes 26148864 | tf_op jit(solution)/shard_map/unpack_grads/pallas_call | solution.py:1457
  617.3 9.2 %unpack_grads.2 = (f32[448,1792]{1,0:T(8,128)}, f32[448,1792]{1,0:T(8,128)}, f32[448,1792]{1,0:T(8,128)}, f32[448,1792]{1,0:T(8,128)}) custom-call(bf16[8,4,56,1792]{3,2,1,0:T(8,128)(2,1)} %get-tuple-element.97.every_ref), custom_call_target="tpu_custom_call" | custom-call | bytes 19267584 | tf_op jit(solution)/shard_map/unpack_grads/pallas_call | solution.py:1457
  626.6 2.8 fusion.11
  (75 shorter events, 13.4 us)
Async XLA Ops:
  1.4 14.6 %collective-permute-start = (bf16[2,1792]{1,0:T(2,128)(2,1)S(1)}, bf16[2,1792]{1,0:T(2,128)(2,1)S(1)}, u32[]{:S(2)}, u32[]{:S(2)}) collective-permute-start(bf16[2,1792]{1,0:T(2,128)(2,1)S(1)} %slice_bitcast_fusion.1), channel_id=1, source_target_pairs={{0,4},{4,8},{8,12},{12,16},{16,20},{20,24},{24,28},{1,5},{5,9},{9,... | collective-permute-start | bytes 21512 | tf_op jit(solution)/shard_map/ppermute | solution.py:27
  6.7 2.9 copy-start.10
  6.7 2.9 copy-start.11
  7.5 4.5 copy-start.3
  10.7 2.5 copy-start.9
  14.9 1.7 copy-start.8
  398.2 1.8 copy-start.1
  398.2 1.8 copy-start.5
  398.2 1.8 copy-start.6
  400.0 1.0 copy-start.4
  400.0 6.1 slice-start
  400.9 1.5 copy-start
  400.9 5.2 slice-start.1
  404.6 20.3 %collective-permute-start.1 = (f32[2,1792]{1,0:T(2,128)S(1)}, f32[2,1792]{1,0:T(2,128)S(1)}, u32[]{:S(2)}, u32[]{:S(2)}) collective-permute-start(f32[2,1792]{1,0:T(2,128)S(1)} %slice.141), channel_id=1, source_target_pairs={{4,0},{8,4},{12,8},{16,12},{20,16},{24,20},{28,24},{5,1},{9,5},{13... | collective-permute-start | bytes 43016 | tf_op jit(solution)/shard_map/ppermute | solution.py:27
  410.5 13.5 %copy-start.7 = (f32[1,1792]{1,0:T(1,128)S(1)}, f32[1,1792]{1,0:T(1,128)}, u32[]{:S(2)}) copy-start(f32[1,1792]{1,0:T(1,128)} %get-tuple-element.88) | copy-start | bytes 21508
  617.3 9.3 %copy-start.2 = (f32[256,1792]{1,0:T(8,128)S(1)}, f32[256,1792]{1,0:T(8,128)}, u32[]{:S(2)}) copy-start(f32[256,1792]{1,0:T(8,128)} %get-tuple-element.71.refs_4_) | copy-start | bytes 5505028

commit v4 on v3

--- a/solution.py
+++ b/solution.py
@@ -420,6 +420,16 @@
         came.start()
         came.wait()
         self.acc[k] = (self.acc[k].astype(F32) + self.stage[0].astype(F32)).astype(BF)
+
+
+class MixedSum(StagedSum):
+    def merge(self, k):
+        self.share(k).wait_recv()
+        other = self.fetch(1, self.pre.at[k])
+        other.start()
+        other.wait()
+        own = self.x[2 * k + self.line.core].astype(F32)
+        self.acc[k] = (own + self.stage[1].astype(F32)).astype(BF)
 
 
 def line_sems(parts):
@@ -1044,6 +1054,8 @@
             for m in range(1, n):
                 gu_sum.begin(m)
 
+        is_step(size - 1)(lambda: gu_sum.advance(1))
+
         for k in range(1, size):
             is_step(k)(functools.partial(gather.ready, k))
         grad = dot_trans(r.all[g], r.out_map[...]).astype(BF)
@@ -1057,7 +1069,6 @@
         pl.when(rank > 0)(lambda: halo(step).start())
 
     each_step(size, step_heads)
-    gu_sum.advance(1)
     scatter.finish()
     fetches[2].wait()
 
@@ -1192,27 +1203,39 @@
 
 
 class CloseRefs(NamedTuple):
-    x: Any
+    gated_hbm: Any
+    dqkv_hbm: Any
+    heads_hbm: Any
+    gb_hbm: Any
     gu_slots: Any
     terms: Any
-    hidden: Any
-    down_map: Any
+    hidden_hbm: Any
+    down_hbm: Any
     every_hbm: Any
-    gu_every_hbm: Any
+    gu_every: Any
     feed: Any
     terms_out: Any
+    pre: Any
+    up_in: Any
+    down_in: Any
     part: Any
     first: Any
     over: Any
     joined: Any
     last: Any
-    pre: Any
+    x: Any
     acc: Any
-    up_in: Any
-    down_in: Any
+    stage: Any
+    stage_load: Any
     every: Any
     slots: Any
-    gu_every: Any
+    gu_own: Any
+    gated: Any
+    dqkv: Any
+    heads: Any
+    gb: Any
+    hidden: Any
+    down_map: Any
     terms_in: Any
     terms_all: Any
     s_send: Any
@@ -1224,7 +1247,7 @@
     loads: Any
 
 
-def close_kernel(size, parts, *refs):
+def close_kernel(size, parts, made, *refs):
     named = len(CloseRefs._fields)
     r, sems = CloseRefs(*refs[:named]), refs[named:]
     rank = lax.axis_index("seq")
@@ -1232,7 +1255,9 @@
     me = group.me
     line_u, line_q = Line(parts, sems[:6]), Line(parts, sems[6:12])
     n, z = line_q.length, line_q.z
-    sums = LineSum(line_q, r.x, r.pre, r.acc, r.up_in, r.down_in, sems[12:])
+    sums = MixedSum(
+        r.stage, r.stage_load, line_q, r.x, r.pre, r.acc, r.up_in, r.down_in, sems[12:]
+    )
     rows = r.feed.shape[0]
     half = rows // 2
     barrier = pltpu.get_barrier_semaphore()
@@ -1240,12 +1265,31 @@
     for step in range(1, parts):
         peer = lax.rem(rank + step, parts)
         pl.semaphore_signal(barrier, inc=1, device_id={"seq": peer}, device_id_type=MESH_ID)
-    own_slots = pltpu.make_async_copy(r.gu_slots, r.gu_every.at[rank], r.loads.at[0])
+    moves = [
+        (r.gu_slots, r.gu_own),
+        (r.hidden_hbm, r.hidden),
+        (r.down_hbm, r.down_map),
+    ]
+    if made:
+        moves += [
+            (r.gated_hbm, r.gated),
+            (r.dqkv_hbm, r.dqkv),
+            (r.heads_hbm, r.heads),
+            (r.gb_hbm, r.gb),
+        ]
+    else:
+        moves += [(r.gated_hbm, r.x)]
+    fetches = [
+        pltpu.make_async_copy(src, dst, r.loads.at[k]) for k, (src, dst) in enumerate(moves)
+    ]
+    for k in [0] + list(range(3, len(moves))) + [1, 2]:
+        fetches[k].start()
+    r.terms_in[me] = r.terms[me]
+    own_slots = pltpu.make_async_copy(r.gu_own, r.gu_every.at[rank], r.loads.at[0])
+    fetches[0].wait()
     own_slots.start()
-    r.terms_in[me] = r.terms[me]
+    own_slots.wait()
     pl.semaphore_wait(barrier, size + parts - 2)
-    sums.trade()
-    own_slots.wait()
     line_u.gather(lambda owner: r.gu_every.at[owner])
 
     def swap(k, step):
@@ -1271,10 +1315,22 @@
         for k in range(size - 1):
             is_step(k)(functools.partial(scatter.made, k))
 
+    for fetch in fetches[3:]:
+        fetch.wait()
+    if made:
+        span = r.gated.shape[1] // (size // 2)
+        for h in range(size // 2):
+            lanes = slice(h * span, (h + 1) * span)
+            pack_pair(
+                r.x, h, r.gated[:, lanes], r.dqkv[...], r.heads[...], r.gb[:, lanes]
+            )
+    sums.trade()
+    line_u.relay(1)
+    fetches[1].wait()
+    fetches[2].wait()
     for m in range(n):
         sums.begin(m)
     each_step(size, down)
-    line_u.relay(1)
 
     for step in others:
         swap(0, step).wait_recv()
@@ -1311,15 +1367,13 @@
     r.every[rank] = jnp.where(lane < 3 * local, r.slots[...], r.acc[z])
     line_q.gather(lambda owner: r.every.at[owner])
     line_u.gathered()
-    stores = [pltpu.make_async_copy(r.gu_every, r.gu_every_hbm, r.loads.at[0])]
-    stores[0].start()
     for j in range(1, n):
         line_q.relay(j)
     for j in range(1, n):
         line_q.close(j)
     line_q.gathered()
-    stores.append(pltpu.make_async_copy(r.every, r.every_hbm, r.loads.at[1]))
-    stores[1].start()
+    store = pltpu.make_async_copy(r.every, r.every_hbm, r.loads.at[1])
+    store.start()
     for step in range(1, parts):
         spread(step).wait_recv()
     small = r.terms_all[0]
@@ -1335,105 +1389,124 @@
     sums.finish()
     line_u.finish()
     line_q.finish()
-    for store in stores:
-        store.wait()
-
-
-def close_part(ident, packed, gu_slots, terms, hidden, down_weight):
-    parts, size, piece, cols = packed.shape
+    store.wait()
+
+
+def close_part(ident, gated, dqkv, heads, gb, gu_slots, terms, hidden, down_weight):
+    size, parts = lax.axis_size("fsdp"), lax.axis_size("seq")
+    width = gated.shape[1]
+    made = packs(size, parts, width)
+    piece, cols = width // (size * parts), dqkv.shape[1] + heads.shape[1]
+    if not made:
+        gated = pack_plain(parts, size, gated, dqkv, heads, gb)
     n = parts // 2
-    rows, width = hidden.shape[1], down_weight.shape[1]
+    rows = hidden.shape[1]
     vmem = pl.BlockSpec(memory_space=pltpu.VMEM)
     hbm = pl.BlockSpec(memory_space=pl.ANY)
     dma = lambda *s: pltpu.SemaphoreType.DMA(s)
     gu_shape = (parts,) + gu_slots.shape
+    packed = (parts, size, piece, cols)
     scratch = scatter_shapes(size, rows, width)
-    chips = pltpu.VMEM((n, size, piece, cols), BF)
+    low = lambda *s: jax.ShapeDtypeStruct(s, BF)
+    copy_of = lambda a: pltpu.VMEM(a.shape if made else (8, 128), BF)
     return pl.pallas_call(
-        functools.partial(close_kernel, size, parts),
+        functools.partial(close_kernel, size, parts, made),
         out_shape=[
-            jax.ShapeDtypeStruct(packed.shape, BF),
-            jax.ShapeDtypeStruct(gu_shape, BF),
+            low(*packed),
+            low(*gu_shape),
             jax.ShapeDtypeStruct((rows, width), F32),
             jax.ShapeDtypeStruct(terms.shape[1:], F32),
-        ],
-        in_specs=[vmem, hbm, vmem, vmem, vmem],
-        out_specs=[hbm, hbm, vmem, vmem],
+        ]
+        + [low(n, size, piece, cols)] * 3,
+        in_specs=[hbm] * 5 + [vmem, hbm, hbm],
+        out_specs=[hbm, hbm, vmem, vmem, hbm, hbm, hbm],
         scratch_shapes=scratch[:-2]
         + [
-            chips,
-            chips,
-            chips,
-            chips,
-            pltpu.VMEM(packed.shape, BF),
+            pltpu.VMEM(packed, BF),
+            pltpu.VMEM((n, size, piece, cols), BF),
+            pltpu.VMEM((2, size, piece, cols), BF),
+            dma(2),
+            pltpu.VMEM(packed, BF),
             pltpu.VMEM((size, piece, cols), BF),
-            pltpu.VMEM(gu_shape, BF),
+            pltpu.VMEM(gu_slots.shape, BF),
+            copy_of(gated),
+            copy_of(dqkv),
+            copy_of(heads),
+            copy_of(gb),
+            pltpu.VMEM(hidden.shape, BF),
+            pltpu.VMEM(down_weight.shape, BF),
             pltpu.VMEM(terms.shape, F32),
             pltpu.VMEM((parts,) + terms.shape[1:], F32),
         ]
         + scratch[-2:]
         + [dma(2, size - 1)] * 2
         + [dma(parts - 1)] * 2
-        + [dma(2)]
+        + [dma(7)]
         + line_sems(parts) * 3,
         compiler_params=pltpu.CompilerParams(
             collective_id=ident, has_side_effects=True, vmem_limit_bytes=67_000_000
         ),
         cost_estimate=pl.CostEstimate(
-            flops=2 * size * rows * down_weight.size, bytes_accessed=500_000_000, transcendentals=0
+            flops=2 * size * rows * (down_weight.size + width * cols),
+            bytes_accessed=500_000_000,
+            transcendentals=0,
         ),
         name="close_part",
-    )(packed, gu_slots, terms, hidden, down_weight)
-
-
-def pack_kernel(size, parts, x_ref, g_ref, *refs):
-    out_ref = refs[-1]
-    full = dot_rows(x_ref[...], g_ref[...])
-    pair = out_ref.shape[1]
-    rows = full.shape[0] // pair
-    piece = rows // parts
-    for k in range(pair):
+    )(gated, dqkv, heads, gb, gu_slots, terms, hidden, down_weight)[:4]
+
+
+def pack_pair(out, pair, x, g, heads=None, gb=None):
+    parts, _, piece, _ = out.shape
+    rows = parts * piece
+    full = dot_rows(x, g)
+    side = None if heads is None else dot_rows(heads, gb)
+    for k in range(2):
         own = full[k * rows : (k + 1) * rows]
-        if len(refs) == 3:
-            heads_ref, gb_ref = refs[0], refs[1]
-            side = dot_rows(heads_ref[...], gb_ref[...])
-            wide = side.shape[1] // pair
+        if side is not None:
+            wide = side.shape[1] // 2
             own = jnp.concatenate([own, side[:, k * wide : (k + 1) * wide]], 1)
-        out_ref[:, k] = own.astype(BF).reshape(parts, piece, own.shape[1])
-
-
-def pack_grads(parts, size, x, g, heads=None, gb=None):
+        out[:, pair * 2 + k] = own.astype(BF).reshape(parts, piece, own.shape[1])
+
+
+def pack_kernel(x_ref, g_ref, out_ref):
+    pack_pair(out_ref, 0, x_ref[...], g_ref[...])
+
+
+def packs(size, parts, width):
+    return width // (size * parts) % 8 == 0 and 2 * width // size % 128 == 0
+
+
+def pack_plain(parts, size, x, g, heads=None, gb=None):
     width, cols = x.shape[1], g.shape[1]
-    rows = width // size
-    piece = rows // parts
-    if piece % 8 or (2 * rows) % 128:
-        full = dot_rows(x, g).reshape(size, parts, piece, cols)
-        if heads is not None:
-            side = dot_rows(heads, gb).reshape(parts, piece, size, -1).transpose(2, 0, 1, 3)
-            full = jnp.concatenate([full, side], 3)
-        return full.transpose(1, 0, 2, 3).astype(BF)
-    total = x.shape[0]
-    pair = pl.BlockSpec((total, 2 * rows), lambda i: (0, i))
-    whole = lambda a: pl.BlockSpec(a.shape, lambda i: (0, 0), pipeline_mode=pl.Buffered(1))
-    args, specs = [x, g], [pair, whole(g)]
-    out_cols = cols
+    piece = width // (size * parts)
+    full = dot_rows(x, g).reshape(size, parts, piece, cols)
     if heads is not None:
-        args += [heads, gb]
-        specs += [whole(heads), pair]
-        out_cols += rows
+        side = dot_rows(heads, gb).reshape(parts, piece, size, -1).transpose(2, 0, 1, 3)
+        full = jnp.concatenate([full, side], 3)
+    return full.transpose(1, 0, 2, 3).astype(BF)
+
+
+def pack_grads(parts, size, x, g):
+    total, width = x.shape
+    cols = g.shape[1]
+    if not packs(size, parts, width):
+        return pack_plain(parts, size, x, g)
+    piece = width // (size * parts)
+    pair = pl.BlockSpec((total, 2 * width // size), lambda i: (0, i))
+    whole = pl.BlockSpec(g.shape, lambda i: (0, 0), pipeline_mode=pl.Buffered(1))
     return pl.pallas_call(
-        functools.partial(pack_kernel, size, parts),
+        pack_kernel,
         grid=(size // 2,),
-        out_shape=jax.ShapeDtypeStruct((parts, size, piece, out_cols), BF),
-        in_specs=specs,
-        out_specs=pl.BlockSpec((parts, 2, piece, out_cols), lambda i: (0, i, 0, 0)),
+        out_shape=jax.ShapeDtypeStruct((parts, size, piece, cols), BF),
+        in_specs=[pair, whole],
+        out_specs=pl.BlockSpec((parts, 2, piece, cols), lambda i: (0, i, 0, 0)),
         cost_estimate=pl.CostEstimate(
-            flops=2 * total * width * out_cols,
-            bytes_accessed=2 * (x.size + g.size + width * out_cols),
+            flops=2 * total * width * cols,
+            bytes_accessed=2 * (x.size + g.size + width * cols),
             transcendentals=0,
         ),
         name="pack_grads",
-    )(*args)
+    )(x, g)
 
 
 def unpack_kernel(widths, every_ref, *outs):
@@ -1591,10 +1664,6 @@
     )
     norm2_term = norm2_term[0]
     down_total = down_every.reshape(-1, width).astype(F32)
-    qkvo_packed = pack_grads(
-        parts, size, flat(gated_all), flat(dqkv), flat(heads_out), flat(grad_branch_all)
-    )
-
     normed_own = normed[2:]
     grad_mix = grad_gated * normed_own
     part_zero = jnp.pad(grad_gated * conv_mix + grad_mix * taps[0], ((2, 0), (0, 0)))
@@ -1619,11 +1688,19 @@
         ]
     )
     terms = jnp.pad(terms, ((0, 3), (0, 0))).reshape(8, size, slice_width).transpose(1, 0, 2)
-    qkvo_packed, gu_slots, terms, down_total, tokens_grad = lax.optimization_barrier(
-        (qkvo_packed, gu_slots, terms, down_total, tokens_grad)
+    gu_slots, terms, down_total, tokens_grad = lax.optimization_barrier(
+        (gu_slots, terms, down_total, tokens_grad)
     )
     qkvo_every, gu_every, feed, terms = close_part(
-        5, qkvo_packed, gu_slots, terms, hidden, down_weight
+        5,
+        flat(gated_all),
+        flat(dqkv),
+        flat(heads_out),
+        flat(grad_branch_all),
+        gu_slots,
+        terms,
+        hidden,
+        down_weight,
     )
     gate_total, up_total = unpack_grads(gu_every, (gu_map.shape[1] // 2,) * 2)
     query_total, key_total, value_total, out_total = unpack_grads(qkvo_every, (local,) * 4)

time: 640 us -> 629 us (0.983)
  Pallas kernels: 575 us -> 562 us
    pallas_call x3 -> x2, Pallas kernels: 204 us -> 189 us  [the longest x1 174 us: close_part(): pl.pallas_call(functools.partial(close_kernel, size, parts, made), out_sh...]
  transfers between devices with their start and end apart: 2 -> 2, of which waited for: 0 -> 0; matrix products, arithmetic and copies ran while one was open for 3% -> 3% of each run, Pallas kernels for 2% -> 0%
where the time goes in v4:
time: 629 us; the launch traced here: 617 us
  Pallas kernels  562 us (89%)
  other arithmetic  23.2 us (4%)
  local copies, waits for them, and re-layouts  15.2 us (2%)
  matrix products  9.64 us (2%)
    pallas_call x1, Pallas kernels, back_part(): pl.pallas_call(functools.partial(back_kernel, size, parts, lens.shape[1])...  179 us
    pallas_call x1, Pallas kernels, forward_part(): pl.pallas_call(functools.partial(forward_kernel, size, parts, count), out...  175 us
    pallas_call x1, Pallas kernels, close_part(): pl.pallas_call(functools.partial(close_kernel, size, parts, made), out_sh...  174 us
    pallas_call x2, Pallas kernels, unpack_grads(): pl.pallas_call(functools.partial(unpack_kernel, widths), grid=(parts,), o...  20.1 us
    pallas_call x1, Pallas kernels, pack_grads(): pl.pallas_call(pack_kernel, grid=(size // 2,), out_shape=jax.ShapeDtypeSt...  14.9 us
  transfers between devices with their start and end apart: 2, of which 0 were waited for; matrix products, arithmetic and copies ran while one was open for 3% of the time, Pallas kernels for 0%

profile of v4, /device:TPU:0, one launch (start us, length us, event | category | flops | bytes accessed | tf_op | source)
XLA Modules:
  0.0 617.0 jit_solution(10494765696304997270)
XLA Ops:
  1.4 2.4 collective-permute-start
  4.8 1.3 constant_dynamic-slice_fusion
  9.6 1.1 constant_dynamic-slice_fusion.2
  10.7 1.3 maximum_bitcast_fusion.refs_6_
  12.0 1.1 fusion.10.refs_2_.refs_5_
  14.9 1.1 concatenate.17
  16.6 174.5 %forward_part.1 = (bf16[4,256,1792]{2,1,0:T(8,128)(2,1)}, bf16[4,256,1344]{2,1,0:T(8,128)(2,1)}, bf16[4,64,896]{2,1,0:T(8,128)(2,1)}, bf16[4,8,56,1344]{3,2,1,0:...) custom-call(bf16[256,1792]{1,0:T(8,128)(2,1)} %bitcast.44, ...), custom_call_target="tpu_custom_call" | custom-call | flops 19964887040 | bytes 500000000 | tf_op jit(solution)/shard_map/forward_part/pallas_call | solution.py:799
  193.5 1.4 fusion.19
  194.9 1.6 fusion.8
  197.5 9.6 %bitcast_convert_fusion = bf16[1216,1792]{1,0:T(8,128)(2,1)} fusion(bf16[4,256,1216]{2,1,0:T(8,128)(2,1)} %get-tuple-element.80.refs_6_, bf16[4,256,1792]{2,1,0:T(8,128)(2,1)} %get-tuple-element.81), kind=kOutput, calls=%fused_computation | convolution fusion | flops 4464918528 | bytes 10518528 | tf_op jit(solution)/shard_map/dot_general | solution.py:39
  207.1 14.9 %pack_grads.1.refs_11_ = bf16[8,4,56,2432]{3,2,1,0:T(8,128)(2,1)} custom-call(bf16[1024,1792]{1,0:T(8,128)(2,1)} %bitcast.67, bf16[1024,2432]{1,0:T(8,128)(2,1)} %bitcast.63), custom_call_target="tpu_custom_call" | custom-call | flops 8925478912 | bytes 17367040 | tf_op jit(solution)/shard_map/pack_grads/pallas_call | solution.py:1497
  222.0 179.3 %back_part.1 = (f32[256,1792]{1,0:T(8,128)}, f32[1,1792]{1,0:T(1,128)}, bf16[4,256,1792]{2,1,0:T(8,128)(2,1)}, bf16[4,256,1344]{2,1,0:T(8,128)(2,1)}, f32[256,17...) custom-call(s32[4,1]{1,0:T(4,128)} %bitcast.58, ...), custom_call_target="tpu_custom_call" | custom-call | flops 15502147584 | bytes 400000000 | tf_op jit(solution)/shard_map/back_part/pallas_call | solution.py:1154
  401.4 1.7 fusion.3
  404.1 1.2 multiply_add_fusion
  405.6 1.5 fusion.5
  407.8 1.5 collective-permute-start.1
  409.3 4.4 bitcast_convert_fusion.1
  414.7 3.0 fusion.9
  417.7 173.6 %close_part.1 = (bf16[8,4,56,1792]{3,2,1,0:T(8,128)(2,1)}, bf16[8,4,56,2432]{3,2,1,0:T(8,128)(2,1)}, f32[256,1792]{1,0:T(8,128)}, f32[8,448]{1,0:T(8,128)}, bf16...) custom-call(bf16[1024,1792]{1,0:T(8,128)(2,1)} %bitcast.65, ...), custom_call_target="tpu_custom_call" | custom-call | flops 11039408128 | bytes 500000000 | tf_op jit(solution)/shard_map/close_part/pallas_call | solution.py:1412
  591.3 1.3 slice_bitcast_fusion
  592.6 1.4 fusion.18
  594.0 10.8 %unpack_grads.3 = (f32[448,4864]{1,0:T(8,128)}, f32[448,4864]{1,0:T(8,128)}) custom-call(bf16[8,4,56,2432]{3,2,1,0:T(8,128)(2,1)} %get-tuple-element.100.every_ref), custom_call_target="tpu_custom_call" | custom-call | bytes 26148864 | tf_op jit(solution)/shard_map/unpack_grads/pallas_call | solution.py:1530
  604.8 9.2 %unpack_grads.2 = (f32[448,1792]{1,0:T(8,128)}, f32[448,1792]{1,0:T(8,128)}, f32[448,1792]{1,0:T(8,128)}, f32[448,1792]{1,0:T(8,128)}) custom-call(bf16[8,4,56,1792]{3,2,1,0:T(8,128)(2,1)} %get-tuple-element.95.every_ref), custom_call_target="tpu_custom_call" | custom-call | bytes 19267584 | tf_op jit(solution)/shard_map/unpack_grads/pallas_call | solution.py:1530
  614.0 2.8 fusion.11
  (74 shorter events, 12.4 us)
Async XLA Ops:
  1.4 14.6 %collective-permute-start = (bf16[2,1792]{1,0:T(2,128)(2,1)S(1)}, bf16[2,1792]{1,0:T(2,128)(2,1)S(1)}, u32[]{:S(2)}, u32[]{:S(2)}) collective-permute-start(bf16[2,1792]{1,0:T(2,128)(2,1)S(1)} %slice_bitcast_fusion.1), channel_id=1, source_target_pairs={{0,4},{4,8},{8,12},{12,16},{16,20},{20,24},{24,28},{1,5},{5,9},{9,... | collective-permute-start | bytes 21512 | tf_op jit(solution)/shard_map/ppermute | solution.py:27
  6.7 2.9 copy-start.10
  6.7 2.9 copy-start.11
  7.5 4.5 copy-start.3
  10.7 2.5 copy-start.9
  14.9 1.7 copy-start.8
  401.4 1.8 copy-start.1
  401.4 1.8 copy-start.5
  401.4 1.8 copy-start.6
  403.2 1.0 copy-start.4
  403.2 6.1 slice-start
  404.1 1.5 copy-start
  404.1 5.2 slice-start.1
  407.8 6.9 %collective-permute-start.1 = (f32[2,1792]{1,0:T(2,128)S(1)}, f32[2,1792]{1,0:T(2,128)S(1)}, u32[]{:S(2)}, u32[]{:S(2)}) collective-permute-start(f32[2,1792]{1,0:T(2,128)S(1)} %slice.141), channel_id=1, source_target_pairs={{4,0},{8,4},{12,8},{16,12},{20,16},{24,20},{28,24},{5,1},{9,5},{13... | collective-permute-start | bytes 43016 | tf_op jit(solution)/shard_map/ppermute | solution.py:27
  409.3 4.5 copy-start.7
  604.8 9.3 %copy-start.2 = (f32[256,1792]{1,0:T(8,128)S(1)}, f32[256,1792]{1,0:T(8,128)}, u32[]{:S(2)}) copy-start(f32[256,1792]{1,0:T(8,128)} %get-tuple-element.70.refs_4_) | copy-start | bytes 5505028

commit v5 on v4

--- a/solution.py
+++ b/solution.py
@@ -497,6 +497,7 @@
     gu_map: Any
     tail: Any
     own: Any
+    grad_hidden: Any
     hidden: Any
     gu_grad: Any
     s_send: Any
@@ -713,6 +714,14 @@
         all_ref[me, span] = (middle * scale * gains[1:2]).astype(BF)
         gather.start_half(h)
     gather.relay()
+
+    def grad_of(step, is_step):
+        g = group.from_own(step)
+        for k in others:
+            is_step(k)(functools.partial(grads.ready, k))
+        r.grad_hidden[g] = dot_trans(r.grads[g], r.down_map[...])
+
+    each_step(size, grad_of)
     for j in range(1, n):
         line_u.close(j)
     line_u.gathered()
@@ -737,7 +746,6 @@
         g, two = group.from_own(step), lax.rem(step, 2)
         for k in others:
             is_step(k)(functools.partial(gather.ready, k))
-            is_step(k)(functools.partial(grads.ready, k))
 
         @pl.when(step >= 2)
         def _():
@@ -751,7 +759,7 @@
         sigma = jax.nn.sigmoid(gate)
         silu = gate * sigma
         r.hidden[two] = (silu * up).astype(BF)
-        grad_hidden = dot_trans(r.grads[g], r.down_map[...])
+        grad_hidden = r.grad_hidden[g]
         grad_gate = grad_hidden * up * sigma * (1.0 + gate * (1.0 - sigma))
         r.gu_grad[two] = jnp.concatenate([grad_gate, grad_hidden * silu], 1).astype(BF)
         for copy in out_copies(step):
@@ -824,6 +832,7 @@
             pltpu.VMEM(maps[1], BF),
             pltpu.VMEM((size, WINDOW, 2 * local), BF),
             pltpu.VMEM((rows, width), F32),
+            pltpu.VMEM(shape(inner), F32),
             pltpu.VMEM((2, rows, inner), BF),
             pltpu.VMEM((2, rows, cols), BF),
         ]
@@ -1050,9 +1059,9 @@
             down_sum.total()
             own_down.start()
             own_down.wait()
-            line.gather(lambda owner: r.down_every.at[owner])
             for m in range(1, n):
                 gu_sum.begin(m)
+            line.gather(lambda owner: r.down_every.at[owner])
 
         is_step(size - 1)(lambda: gu_sum.advance(1))
 
@@ -1472,6 +1481,31 @@
     pack_pair(out_ref, 0, x_ref[...], g_ref[...])
 
 
+def down_kernel(x_ref, g_ref, out_ref):
+    out_ref[...] = dot_rows(x_ref[...], g_ref[...]).astype(BF)
+
+
+def down_grad(x, g):
+    total, inner = x.shape
+    half = g.shape[1] // 2
+    return pl.pallas_call(
+        down_kernel,
+        grid=(2,),
+        out_shape=jax.ShapeDtypeStruct((inner, 2 * half), BF),
+        in_specs=[
+            pl.BlockSpec(x.shape, lambda i: (0, 0), pipeline_mode=pl.Buffered(1)),
+            pl.BlockSpec((total, half), lambda i: (0, i)),
+        ],
+        out_specs=pl.BlockSpec((inner, half), lambda i: (0, i)),
+        cost_estimate=pl.CostEstimate(
+            flops=4 * total * inner * half,
+            bytes_accessed=2 * (x.size + g.size) + 4 * inner * half,
+            transcendentals=0,
+        ),
+        name="down_grad",
+    )(x, g)
+
+
 def packs(size, parts, width):
     return width // (size * parts) % 8 == 0 and 2 * width // size % 128 == 0
 
@@ -1509,33 +1543,41 @@
     )(x, g)
 
 
-def unpack_kernel(widths, every_ref, *outs):
-    size = every_ref.shape[1]
-    blocks = [every_ref[0, i].astype(F32) for i in range(size)]
-    low = 0
-    for width, out in zip(widths, outs):
-        out[...] = jnp.concatenate([b[:, low : low + width] for b in blocks], 1)
-        low += width
-
-
-def unpack_grads(every, widths):
-    parts, size, piece, cols = every.shape
+def unpack_kernel(widths, *refs):
+    outs = list(refs[len(widths) :])
+    for every_ref, wide in zip(refs, widths):
+        blocks = [every_ref[0, i].astype(F32) for i in range(every_ref.shape[1])]
+        low = 0
+        for width in wide:
+            outs.pop(0)[...] = jnp.concatenate([b[:, low : low + width] for b in blocks], 1)
+            low += width
+
+
+def unpack_grads(arrays, widths):
+    parts, size, piece, _ = arrays[0].shape
+    every = [w for wide in widths for w in wide]
     if piece % 8:
-        outs, low = [], 0
-        for width in widths:
-            block = every[:, :, :, low : low + width].transpose(0, 2, 1, 3)
-            outs.append(block.reshape(parts * piece, size * width).astype(F32))
-            low += width
+        outs = []
+        for array, wide in zip(arrays, widths):
+            low = 0
+            for width in wide:
+                block = array[:, :, :, low : low + width].transpose(0, 2, 1, 3)
+                outs.append(block.reshape(parts * piece, size * width).astype(F32))
+                low += width
         return outs
     return pl.pallas_call(
         functools.partial(unpack_kernel, widths),
         grid=(parts,),
-        out_shape=[jax.ShapeDtypeStruct((parts * piece, size * w), F32) for w in widths],
-        in_specs=[pl.BlockSpec((1, size, piece, cols), lambda i: (i, 0, 0, 0))],
-        out_specs=[pl.BlockSpec((piece, size * w), lambda i: (i, 0)) for w in widths],
-        cost_estimate=pl.CostEstimate(flops=0, bytes_accessed=every.size * 6, transcendentals=0),
+        out_shape=[jax.ShapeDtypeStruct((parts * piece, size * w), F32) for w in every],
+        in_specs=[
+            pl.BlockSpec((1, size, piece, a.shape[3]), lambda i: (i, 0, 0, 0)) for a in arrays
+        ],
+        out_specs=[pl.BlockSpec((piece, size * w), lambda i: (i, 0)) for w in every],
+        cost_estimate=pl.CostEstimate(
+            flops=0, bytes_accessed=6 * sum(a.size for a in arrays), transcendentals=0
+        ),
         name="unpack_grads",
-    )(every)
+    )(*arrays)
 
 
 def columns_piece(weights, part, parts):
@@ -1645,7 +1687,7 @@
     )
 
     gu_packed = pack_grads(parts, size, flat(normed_all), flat(grad_gu))
-    down_packed = dot_rows(flat(hidden), grad_down_all).astype(BF)
+    down_packed = down_grad(flat(hidden), grad_down_all)
     grad_middle, norm2_term, grad_branch_all, dqkv, grad_gated, gu_slots, down_every = back_part(
         4,
         lens_all,
@@ -1702,8 +1744,9 @@
         hidden,
         down_weight,
     )
-    gate_total, up_total = unpack_grads(gu_every, (gu_map.shape[1] // 2,) * 2)
-    query_total, key_total, value_total, out_total = unpack_grads(qkvo_every, (local,) * 4)
+    gate_total, up_total, query_total, key_total, value_total, out_total = unpack_grads(
+        (gu_every, qkvo_every), ((gu_map.shape[1] // 2,) * 2, (local,) * 4)
+    )
 
     layer_out = (live_mask * (middle + feed)).astype(BF)[None]
     return (

time: 629 us -> 643 us (1.022)
  Pallas kernels: 562 us -> 588 us
  matrix products: 9.64 us -> 0 us
    pallas_call x1, Pallas kernels: 179 us -> 206 us  [back_part(): pl.pallas_call(functools.partial(back_kernel, size, parts, lens.shape[1])...]
    dot_general x1 -> x0, matrix products: 9.64 us -> none  [dot_rows(): lax.dot_general(left, right, (((0,), (0,)), ((), ())), preferred_element_...]
    pallas_call x0 -> x1, Pallas kernels: none -> 9.21 us  [down_grad(): pl.pallas_call(down_kernel, grid=(2,), out_shape=jax.ShapeDtypeStruct((in...]
    pallas_call x1, Pallas kernels: 174 us -> 167 us  [close_part(): pl.pallas_call(functools.partial(close_kernel, size, parts, made), out_sh...]
    pallas_call x2 -> x1, Pallas kernels: 20.1 us -> 16.9 us  [unpack_grads(): pl.pallas_call(functools.partial(unpack_kernel, widths), grid=(parts,), o...]
where the time goes in v5:
time: 643 us; the launch traced here: 634 us
  Pallas kernels  588 us (91%)
  other arithmetic  23.5 us (4%)
  local copies, waits for them, and re-layouts  15.2 us (2%)
    pallas_call x1, Pallas kernels, back_part(): pl.pallas_call(functools.partial(back_kernel, size, parts, lens.shape[1])...  206 us
    pallas_call x1, Pallas kernels, forward_part(): pl.pallas_call(functools.partial(forward_kernel, size, parts, count), out...  175 us
    pallas_call x1, Pallas kernels, close_part(): pl.pallas_call(functools.partial(close_kernel, size, parts, made), out_sh...  167 us
    pallas_call x1, Pallas kernels, unpack_grads(): pl.pallas_call(functools.partial(unpack_kernel, widths), grid=(parts,), o...  16.9 us
    pallas_call x1, Pallas kernels, pack_grads(): pl.pallas_call(pack_kernel, grid=(size // 2,), out_shape=jax.ShapeDtypeSt...  15.1 us
  transfers between devices with their start and end apart: 2, of which 0 were waited for; matrix products, arithmetic and copies ran while one was open for 3% of the time, Pallas kernels for 0%

profile of v5, /device:TPU:0, one launch (start us, length us, event | category | flops | bytes accessed | tf_op | source)
XLA Modules:
  0.0 634.0 jit_solution(12315157236848443140)
XLA Ops:
  1.4 2.4 collective-permute-start
  3.8 0.9 constant_dynamic-slice_fusion.4
  4.8 1.3 constant_dynamic-slice_fusion
  9.6 1.1 constant_dynamic-slice_fusion.2
  10.7 1.3 maximum_bitcast_fusion.refs_6_
  12.0 1.1 fusion.10.refs_2_.refs_5_
  14.9 1.1 concatenate.17
  16.6 174.6 %forward_part.1 = (bf16[4,256,1792]{2,1,0:T(8,128)(2,1)}, bf16[4,256,1344]{2,1,0:T(8,128)(2,1)}, bf16[4,64,896]{2,1,0:T(8,128)(2,1)}, bf16[4,8,56,1344]{3,2,1,0:...) custom-call(bf16[256,1792]{1,0:T(8,128)(2,1)} %bitcast.42, ...), custom_call_target="tpu_custom_call" | custom-call | flops 19964887040 | bytes 500000000 | tf_op jit(solution)/shard_map/forward_part/pallas_call | solution.py:807
  193.5 1.4 fusion.19
  195.0 1.6 fusion.8
  197.5 9.2 %down_grad.1 = bf16[1216,1792]{1,0:T(8,128)(2,1)} custom-call(bf16[1024,1216]{1,0:T(8,128)(2,1)} %bitcast.68, bf16[1024,1792]{1,0:T(8,128)(2,1)} %bitcast.66), custom_call_target="tpu_custom_call" | custom-call | flops 4462739456 | bytes 10518528 | tf_op jit(solution)/shard_map/down_grad/pallas_call | solution.py:1491
  206.7 15.1 %pack_grads.1.refs_11_ = bf16[8,4,56,2432]{3,2,1,0:T(8,128)(2,1)} custom-call(bf16[1024,1792]{1,0:T(8,128)(2,1)} %bitcast.65, bf16[1024,2432]{1,0:T(8,128)(2,1)} %bitcast.61), custom_call_target="tpu_custom_call" | custom-call | flops 8925478912 | bytes 17367040 | tf_op jit(solution)/shard_map/pack_grads/pallas_call | solution.py:1531
  221.8 205.6 %back_part.1 = (f32[256,1792]{1,0:T(8,128)}, f32[1,1792]{1,0:T(1,128)}, bf16[4,256,1792]{2,1,0:T(8,128)(2,1)}, bf16[4,256,1344]{2,1,0:T(8,128)(2,1)}, f32[256,17...) custom-call(s32[4,1]{1,0:T(4,128)} %bitcast.56, ...), custom_call_target="tpu_custom_call" | custom-call | flops 15502147584 | bytes 400000000 | tf_op jit(solution)/shard_map/back_part/pallas_call | solution.py:1163
  427.4 1.7 fusion.3
  430.1 1.2 multiply_add_fusion
  431.6 1.5 fusion.5
  433.8 1.5 collective-permute-start.1
  435.4 4.4 bitcast_convert_fusion
  440.7 2.9 fusion.9
  443.7 167.1 %close_part.1 = (bf16[8,4,56,1792]{3,2,1,0:T(8,128)(2,1)}, bf16[8,4,56,2432]{3,2,1,0:T(8,128)(2,1)}, f32[256,1792]{1,0:T(8,128)}, f32[8,448]{1,0:T(8,128)}, bf16...) custom-call(bf16[1024,1792]{1,0:T(8,128)(2,1)} %bitcast.63, ...), custom_call_target="tpu_custom_call" | custom-call | flops 11039408128 | bytes 500000000 | tf_op jit(solution)/shard_map/close_part/pallas_call | solution.py:1421
  610.8 1.3 slice_bitcast_fusion
  612.1 1.4 fusion.18
  613.5 3.2 fusion.11
  616.7 16.9 %unpack_grads.1 = (f32[448,4864]{1,0:T(8,128)}, f32[448,4864]{1,0:T(8,128)}, f32[448,1792]{1,0:T(8,128)}, f32[448,1792]{1,0:T(8,128)}, f32[448,1792]{1,0:T(8,128)}, /*index=5*/f32[448,1792]{1,0:T(8,128)}) custom-call(bf16[8,4,56,2432]{3,2,1,0:T(8,128)(2,1)} %get-tuple-element.95.refs_0_, bf16[8,4,56,1792]{3,2,1,0:T(8,128)(2,1)} %get-tuple-element.96.refs_1_), custom_call_target="tpu_custom_call" | custom-call | bytes 45416448 | tf_op jit(solution)/shard_map/unpack_grads/pallas_call | solution.py:1568
  (71 shorter events, 11.4 us)
Async XLA Ops:
  1.4 14.6 %collective-permute-start = (bf16[2,1792]{1,0:T(2,128)(2,1)S(1)}, bf16[2,1792]{1,0:T(2,128)(2,1)S(1)}, u32[]{:S(2)}, u32[]{:S(2)}) collective-permute-start(bf16[2,1792]{1,0:T(2,128)(2,1)S(1)} %slice_bitcast_fusion.1), channel_id=1, source_target_pairs={{0,4},{4,8},{8,12},{12,16},{16,20},{20,24},{24,28},{1,5},{5,9},{9,... | collective-permute-start | bytes 21512 | tf_op jit(solution)/shard_map/ppermute | solution.py:27
  6.7 2.9 copy-start.9
  6.7 2.9 copy-start.10
  7.5 4.5 copy-start.2
  10.7 2.5 copy-start.8
  14.9 1.7 copy-start.7
  427.4 1.8 copy-start.1
  427.4 1.8 copy-start.4
  427.4 1.8 copy-start.5
  429.1 0.9 copy-start.3
  429.1 6.2 slice-start
  430.1 1.5 copy-start
  430.1 5.3 slice-start.1
  433.8 6.9 %collective-permute-start.1 = (f32[2,1792]{1,0:T(2,128)S(1)}, f32[2,1792]{1,0:T(2,128)S(1)}, u32[]{:S(2)}, u32[]{:S(2)}) collective-permute-start(f32[2,1792]{1,0:T(2,128)S(1)} %slice.141), channel_id=1, source_target_pairs={{4,0},{8,4},{12,8},{16,12},{20,16},{24,20},{28,24},{5,1},{9,5},{13... | collective-permute-start | bytes 43016 | tf_op jit(solution)/shard_map/ppermute | solution.py:27
  435.4 4.5 copy-start.6

commit v6 on v5

--- a/solution.py
+++ b/solution.py
@@ -464,8 +464,7 @@
 
 class ForwardRefs(NamedTuple):
     tokens: Any
-    edge_tok: Any
-    grad: Any
+    cot: Any
     gains: Any
     table: Any
     qkv_piece: Any
@@ -485,6 +484,7 @@
     gu_map_hbm: Any
     gains_all: Any
     table_all: Any
+    edge_tok: Any
     part: Any
     first: Any
     over: Any
@@ -512,6 +512,8 @@
     m_recv: Any
     halo_send: Any
     halo_recv: Any
+    edge_send: Any
+    edge_recv: Any
     loads: Any
     stores: Any
     hidden_store: Any
@@ -552,8 +554,23 @@
         copy.start()
     r.gains_all[me] = r.gains[...]
     r.table_all[me] = r.table[...]
-    r.grads[me] = r.grad[...]
+    own_table = r.table[...]
+    slots = slot + lax.broadcasted_iota(jnp.int32, (rows, 1), 0)
+    length = lambda j: own_table[0:1, j : j + 1]
+    start = lambda j: own_table[1:2, j : j + 1]
+    segment = segment_of(slots, count, length, start)
+    r.grads[me] = jnp.where(segment >= 0, r.cot[...].astype(F32), 0.0).astype(BF)
+
+    @pl.when(rank == 0)
+    def _():
+        r.edge_tok[...] = jnp.zeros_like(r.edge_tok)
+
+    def edge_rows():
+        last = r.tokens.at[pl.ds(rows - 8, 8)]
+        return remote(last, r.edge_tok, r.edge_send, r.edge_recv, seq=rank + 1)
+
     pl.semaphore_wait(barrier, size - 1 + known)
+    pl.when(rank < parts - 1)(lambda: edge_rows().start())
 
     def swap(k, step):
         peer = lax.rem(me + step, size)
@@ -574,14 +591,10 @@
             swap(k, step).wait_recv()
 
     gains = jnp.concatenate([r.gains_all[f] for f in range(size)], 1).astype(F32)
-    own_table = r.table_all[me]
-    slots = slot + lax.broadcasted_iota(jnp.int32, (rows, 1), 0)
-    length = lambda j: own_table[0:1, j : j + 1]
-    start = lambda j: own_table[1:2, j : j + 1]
-    segment = segment_of(slots, count, length, start)
     same_one = (segment == segment_of(slots - 1, count, length, start)).astype(F32)
     same_two = (segment == segment_of(slots - 2, count, length, start)).astype(F32)
     tokens = r.tokens[...].astype(F32)
+    pl.when(rank > 0)(lambda: edge_rows().wait_recv())
     edge = r.edge_tok[...].astype(F32)
 
     def norm(a):
@@ -589,9 +602,9 @@
 
     normed, edge = norm(tokens), norm(edge)
     row = lax.broadcasted_iota(jnp.int32, (rows, 1), 0)
-    back_one = jnp.where(row == 0, edge[1:2], pltpu.roll(normed, 1, 0))
+    back_one = jnp.where(row == 0, edge[7:8], pltpu.roll(normed, 1, 0))
     back_two = jnp.where(
-        row == 0, edge[0:1], jnp.where(row == 1, edge[1:2], pltpu.roll(normed, 2, 0))
+        row == 0, edge[6:7], jnp.where(row == 1, edge[7:8], pltpu.roll(normed, 2, 0))
     )
     mixed = (
         normed * gains[2:3]
@@ -779,6 +792,7 @@
 
     @pl.when(rank < parts - 1)
     def _():
+        edge_rows().wait_send()
         for step in range(size):
             halo(step).wait_send()
 
@@ -791,7 +805,7 @@
             copy.wait()
 
 
-def forward_part(ident, count, tokens, edge, grad, gains, table, qkv_piece, gu_piece, out_weight, down_weight):
+def forward_part(ident, count, tokens, cot, gains, table, qkv_piece, gu_piece, out_weight, down_weight):
     size, parts = lax.axis_size("fsdp"), lax.axis_size("seq")
     rows, width = tokens.shape
     local, inner = out_weight.shape[0], down_weight.shape[0]
@@ -820,9 +834,10 @@
             low(maps[1]),
             low((size,) + gains.shape),
             jax.ShapeDtypeStruct((size,) + table.shape, jnp.int32),
+            low((8, width)),
         ],
-        in_specs=[vmem] * 5 + [hbm, hbm, vmem, vmem],
-        out_specs=[hbm, hbm, vmem, hbm, vmem, vmem, hbm, hbm, hbm, hbm, hbm, vmem, vmem],
+        in_specs=[vmem] * 4 + [hbm, hbm, vmem, vmem],
+        out_specs=[hbm, hbm, vmem, hbm, vmem, vmem, hbm, hbm, hbm, hbm, hbm, vmem, vmem, vmem],
         scratch_shapes=scratch[:-2]
         + [
             pltpu.VMEM(shape(width), BF),
@@ -839,6 +854,7 @@
         + [dma(hop)] * 8
         + [dma(4, size - 1)] * 2
         + [dma(size)] * 2
+        + [pltpu.SemaphoreType.DMA] * 2
         + [dma(2), dma(size + 5), dma(2), dma(2)]
         + line_sems(parts)
         + line_sems(parts),
@@ -851,7 +867,7 @@
             transcendentals=0,
         ),
         name="forward_part",
-    )(tokens, edge, grad, gains, table, qkv_piece, gu_piece, out_weight, down_weight)
+    )(tokens, cot, gains, table, qkv_piece, gu_piece, out_weight, down_weight)
 
 
 def heads_back(group, slot, count, lens_ref, starts_ref, own, edge, grad):
@@ -904,7 +920,7 @@
     grad_gu_hbm: Any
     gu_map_hbm: Any
     middle: Any
-    grad: Any
+    grads_hbm: Any
     gain: Any
     out_map: Any
     edge: Any
@@ -953,6 +969,7 @@
     down_load: Any
     m_send: Any
     m_recv: Any
+    grad: Any
 
 
 def back_kernel(size, parts, count, *refs):
@@ -992,7 +1009,12 @@
     fetches = [
         pltpu.make_async_copy(src, dst, r.loads.at[k])
         for k, (src, dst) in enumerate(
-            ((r.grad_gu_hbm, r.grad_gu), (r.gu_map_hbm, r.gu_map), (r.qkv_map_hbm, r.qkv_map))
+            (
+                (r.grad_gu_hbm, r.grad_gu),
+                (r.gu_map_hbm, r.gu_map),
+                (r.qkv_map_hbm, r.qkv_map),
+                (r.grads_hbm.at[group.me], r.grad),
+            )
         )
     ]
     for fetch in fetches:
@@ -1008,6 +1030,7 @@
     gather = Gather(group, r.all, r.g_send, r.g_recv)
     fetches[0].wait()
     fetches[1].wait()
+    fetches[3].wait()
 
     def step_two(step, is_step):
         partial = dot_trans(r.grad_gu[group.to_own(step)], r.gu_map[...])
@@ -1059,9 +1082,9 @@
             down_sum.total()
             own_down.start()
             own_down.wait()
+            line.gather(lambda owner: r.down_every.at[owner])
             for m in range(1, n):
                 gu_sum.begin(m)
-            line.gather(lambda owner: r.down_every.at[owner])
 
         is_step(size - 1)(lambda: gu_sum.advance(1))
 
@@ -1078,6 +1101,7 @@
         pl.when(rank > 0)(lambda: halo(step).start())
 
     each_step(size, step_heads)
+    line.relay(1)
     scatter.finish()
     fetches[2].wait()
 
@@ -1106,7 +1130,6 @@
             is_step(k)(functools.partial(scatter.made, k))
 
     each_step(size, step_one)
-    line.relay(1)
     scatter.join()
     for t in range(2, n - 1):
         gu_sum.advance(t)
@@ -1147,7 +1170,7 @@
 
 
 def back_part(
-    ident, lens, starts, grad_gu, gu_map, middle, grad, gain, out_weight, edge, qkv, qkv_map, gu_x, down_x
+    ident, lens, starts, grad_gu, gu_map, middle, grads, gain, out_weight, edge, qkv, qkv_map, gu_x, down_x
 ):
     size, parts = lax.axis_size("fsdp"), lax.axis_size("seq")
     rows, width = middle.shape
@@ -1173,7 +1196,7 @@
         ]
         + [low(n, *gu)] * 3
         + [low(n, *down)] * 3,
-        in_specs=[smem, smem, hbm, hbm] + [vmem] * 6 + [hbm] * 3,
+        in_specs=[smem, smem, hbm, hbm, vmem, hbm] + [vmem] * 4 + [hbm] * 3,
         out_specs=[vmem] * 5 + [hbm] * 8,
         scratch_shapes=scatter_shapes(size, rows, width)
         + sems
@@ -1187,7 +1210,7 @@
             pltpu.VMEM((size, WINDOW, 3 * local), F32),
             dma(size),
             dma(size),
-            dma(3),
+            dma(4),
             pltpu.VMEM((n,) + gu, BF),
             pltpu.VMEM((2,) + gu, BF),
             dma(2),
@@ -1196,6 +1219,7 @@
             dma(2),
             dma(size - 1),
             dma(size - 1),
+            pltpu.VMEM((rows, width), BF),
         ]
         + line_sems(parts) * 3,
         compiler_params=pltpu.CompilerParams(
@@ -1207,7 +1231,7 @@
             transcendentals=0,
         ),
         name="back_part",
-    )(lens, starts, grad_gu, gu_map, middle, grad, gain, out_weight, edge, qkv, qkv_map, gu_x, down_x)
+    )(lens, starts, grad_gu, gu_map, middle, grads, gain, out_weight, edge, qkv, qkv_map, gu_x, down_x)
     return outs[:7]
 
 
@@ -1638,8 +1662,6 @@
     table = table.at[0, :count].set(seq_lengths[0]).at[1, :count].set(seq_offsets[0])
     qkv_piece = columns_piece((query_weight, key_weight, value_weight), part, parts)
     gu_piece = columns_piece((gate_weight, up_weight), part, parts)
-    edge_tokens = shifted(own_tokens[rows - 2 :], "seq", 1)
-    grad_down = (cotangent[0].astype(F32) * live_mask).astype(BF)
     (
         gated_all,
         qkv,
@@ -1654,12 +1676,12 @@
         gu_map,
         gains_all,
         table_all,
+        edge_tokens,
     ) = forward_part(
         0,
         count,
         own_tokens,
-        jnp.pad(edge_tokens, ((0, 6), (0, 0))),
-        grad_down,
+        cotangent[0],
         gains,
         table,
         qkv_piece,
@@ -1675,9 +1697,8 @@
     norm_two = gains_all[1].astype(F32)
     taps = gains_all[2:5].astype(F32)
     qkv_map, gu_map = qkv_map.reshape(width, -1), gu_map.reshape(width, -1)
-    grad_down_all = flat(grad_down_all)
-
-    extended = jnp.concatenate([edge_tokens, own_tokens], 0).astype(F32)
+
+    extended = jnp.concatenate([edge_tokens[6:], own_tokens], 0).astype(F32)
     scale_one = lax.rsqrt(jnp.mean(extended * extended, axis=1, keepdims=True) + EPS)
     normed = extended * scale_one * norm_one
     conv_mix = (
@@ -1687,7 +1708,7 @@
     )
 
     gu_packed = pack_grads(parts, size, flat(normed_all), flat(grad_gu))
-    down_packed = down_grad(flat(hidden), grad_down_all)
+    down_packed = down_grad(flat(hidden), flat(grad_down_all))
     grad_middle, norm2_term, grad_branch_all, dqkv, grad_gated, gu_slots, down_every = back_part(
         4,
         lens_all,
@@ -1695,7 +1716,7 @@
         grad_gu,
         gu_map,
         middle,
-        grad_down,
+        grad_down_all,
         norm_two[None],
         out_weight,
         edge,

time: 643 us -> 628 us (0.977)
  Pallas kernels: 588 us -> 571 us
    pallas_call x1, Pallas kernels: 206 us -> 171 us  [back_part(): pl.pallas_call(functools.partial(back_kernel, size, parts, lens.shape[1])...]
    pallas_call x1, Pallas kernels: 167 us -> 184 us  [close_part(): pl.pallas_call(functools.partial(close_kernel, size, parts, made), out_sh...]
  transfers between devices with their start and end apart: 2 -> 1, of which waited for: 0 -> 0; matrix products, arithmetic and copies ran while one was open for 3% -> 1% of each run, Pallas kernels for 0% -> 0%
where the time goes in v6:
time: 628 us; the launch traced here: 617 us
  Pallas kernels  571 us (91%)
  other arithmetic  25.6 us (4%)
  local copies, waits for them, and re-layouts  15.8 us (3%)
    pallas_call x1, Pallas kernels, close_part(): pl.pallas_call(functools.partial(close_kernel, size, parts, made), out_sh...  184 us
    pallas_call x1, Pallas kernels, forward_part(): pl.pallas_call(functools.partial(forward_kernel, size, parts, count), out...  175 us
    pallas_call x1, Pallas kernels, back_part(): pl.pallas_call(functools.partial(back_kernel, size, parts, lens.shape[1])...  171 us
    pallas_call x1, Pallas kernels, unpack_grads(): pl.pallas_call(functools.partial(unpack_kernel, widths), grid=(parts,), o...  16.9 us
    pallas_call x1, Pallas kernels, pack_grads(): pl.pallas_call(pack_kernel, grid=(size // 2,), out_shape=jax.ShapeDtypeSt...  14.9 us
  transfers between devices with their start and end apart: 1, of which 0 were waited for; matrix products, arithmetic and copies ran while one was open for 1% of the time, Pallas kernels for 0%

profile of v6, /device:TPU:0, one launch (start us, length us, event | category | flops | bytes accessed | tf_op | source)
XLA Modules:
  0.0 616.5 jit_solution(3501746501386459029)
XLA Ops:
  3.3 0.9 constant_dynamic-slice_fusion.4
  4.6 1.1 constant_dynamic-slice_fusion.2
  6.3 1.3 constant_dynamic-slice_fusion
  9.1 1.3 maximum_bitcast_fusion.refs_5_
  10.5 1.1 concatenate.17
  12.2 174.8 %forward_part.1 = (bf16[4,256,1792]{2,1,0:T(8,128)(2,1)}, bf16[4,256,1344]{2,1,0:T(8,128)(2,1)}, bf16[4,64,896]{2,1,0:T(8,128)(2,1)}, bf16[4,8,56,1344]{3,2,1,0:...) custom-call(bf16[256,1792]{1,0:T(8,128)(2,1)} %bitcast.38, ...), custom_call_target="tpu_custom_call" | custom-call | flops 19964887040 | bytes 500000000 | tf_op jit(solution)/shard_map/forward_part/pallas_call | solution.py:821
  187.0 0.9 fusion.11
  188.6 1.4 fusion.18
  191.5 1.6 fusion.8
  194.7 14.9 %pack_grads.1.refs_11_ = bf16[8,4,56,2432]{3,2,1,0:T(8,128)(2,1)} custom-call(bf16[1024,1792]{1,0:T(8,128)(2,1)} %bitcast.63, bf16[1024,2432]{1,0:T(8,128)(2,1)} %bitcast.58), custom_call_target="tpu_custom_call" | custom-call | flops 8925478912 | bytes 17367040 | tf_op jit(solution)/shard_map/pack_grads/pallas_call | solution.py:1555
  209.6 9.5 %down_grad.1 = bf16[1216,1792]{1,0:T(8,128)(2,1)} custom-call(bf16[1024,1216]{1,0:T(8,128)(2,1)} %bitcast.65, bf16[1024,1792]{1,0:T(8,128)(2,1)} %bitcast.62), custom_call_target="tpu_custom_call" | custom-call | flops 4462739456 | bytes 10518528 | tf_op jit(solution)/shard_map/down_grad/pallas_call | solution.py:1515
  219.1 1.7 fusion.3
  220.7 170.6 %back_part.1 = (f32[256,1792]{1,0:T(8,128)}, f32[1,1792]{1,0:T(1,128)}, bf16[4,256,1792]{2,1,0:T(8,128)(2,1)}, bf16[4,256,1344]{2,1,0:T(8,128)(2,1)}, f32[256,17...) custom-call(s32[4,1]{1,0:T(4,128)} %bitcast.52, ...), custom_call_target="tpu_custom_call" | custom-call | flops 15502147584 | bytes 400000000 | tf_op jit(solution)/shard_map/back_part/pallas_call | solution.py:1186
  391.4 4.2 multiply_reduce_fusion
  395.7 1.2 multiply_add_fusion
  397.1 1.4 fusion.5
  399.2 1.5 collective-permute-start
  400.8 4.4 bitcast_convert_fusion
  406.2 2.9 fusion.9
  409.1 184.2 %close_part.1 = (bf16[8,4,56,1792]{3,2,1,0:T(8,128)(2,1)}, bf16[8,4,56,2432]{3,2,1,0:T(8,128)(2,1)}, f32[256,1792]{1,0:T(8,128)}, f32[8,448]{1,0:T(8,128)}, bf16...) custom-call(bf16[1024,1792]{1,0:T(8,128)(2,1)} %bitcast.60, ...), custom_call_target="tpu_custom_call" | custom-call | flops 11039408128 | bytes 500000000 | tf_op jit(solution)/shard_map/close_part/pallas_call | solution.py:1445
  593.3 1.4 fusion.17
  594.7 1.3 slice_bitcast_fusion
  596.0 3.2 fusion.10
  599.2 16.9 %unpack_grads.1 = (f32[448,4864]{1,0:T(8,128)}, f32[448,4864]{1,0:T(8,128)}, f32[448,1792]{1,0:T(8,128)}, f32[448,1792]{1,0:T(8,128)}, f32[448,1792]{1,0:T(8,128)}, /*index=5*/f32[448,1792]{1,0:T(8,128)}) custom-call(bf16[8,4,56,2432]{3,2,1,0:T(8,128)(2,1)} %get-tuple-element.97.refs_0_, bf16[8,4,56,1792]{3,2,1,0:T(8,128)(2,1)} %get-tuple-element.98.refs_1_), custom_call_target="tpu_custom_call" | custom-call | bytes 45416448 | tf_op jit(solution)/shard_map/unpack_grads/pallas_call | solution.py:1592
  (65 shorter events, 10.1 us)
Async XLA Ops:
  9.0 2.5 copy-start.9
  10.5 1.8 copy-start.8
  209.6 9.5 %copy-start.1 = (bf16[1,256,1792]{2,1,0:T(8,128)(2,1)S(1)}, bf16[1,256,1792]{2,1,0:T(8,128)(2,1)}, u32[]{:S(2)}) copy-start(bf16[1,256,1792]{2,1,0:T(8,128)(2,1)} %param.18) | copy-start | bytes 2752516
  391.4 4.3 copy-start
  391.4 4.3 copy-start.3
  391.4 4.3 copy-start.4
  391.4 4.3 copy-start.5
  391.4 9.4 %slice-start = ((s8[4358144]{0:T(1024)(128)(4,1)}), s8[4194304]{0:T(1024)(128)(4,1)S(1)}, s32[]{:S(2)}) async-start(s8[4358144]{0:T(1024)(128)(4,1)} %bitcast.43), calls=%async_computation | async-start | bytes 8388608
  395.7 1.4 copy-start.2
  395.7 5.1 slice-start.1
  399.2 6.9 %collective-permute-start = (f32[2,1792]{1,0:T(2,128)S(1)}, f32[2,1792]{1,0:T(2,128)S(1)}, u32[]{:S(2)}, u32[]{:S(2)}) collective-permute-start(f32[2,1792]{1,0:T(2,128)S(1)} %slice.137), channel_id=1, source_target_pairs={{4,0},{8,4},{12,8},{16,12},{20,16},{24,20},{28,24},{5,1},{9,5},{13... | collective-permute-start | bytes 43016 | tf_op jit(solution)/shard_map/ppermute | solution.py:27
  400.8 4.5 copy-start.6
  409.1 186.9 %copy-start.7 = (f32[256]{0:T(256)S(1)}, f32[256]{0:T(256)}, u32[]{:S(2)}) copy-start(f32[256]{0:T(256)} %get-tuple-element.125) | copy-start | bytes 3076

commit v7 on v6

--- a/solution.py
+++ b/solution.py
@@ -1083,10 +1083,6 @@
             own_down.start()
             own_down.wait()
             line.gather(lambda owner: r.down_every.at[owner])
-            for m in range(1, n):
-                gu_sum.begin(m)
-
-        is_step(size - 1)(lambda: gu_sum.advance(1))
 
         for k in range(1, size):
             is_step(k)(functools.partial(gather.ready, k))
@@ -1101,6 +1097,9 @@
         pl.when(rank > 0)(lambda: halo(step).start())
 
     each_step(size, step_heads)
+    for m in range(1, n):
+        gu_sum.begin(m)
+    gu_sum.advance(1)
     line.relay(1)
     scatter.finish()
     fetches[2].wait()

time: 628 us -> 618 us (0.984)
  Pallas kernels: 571 us -> 561 us
    pallas_call x1, Pallas kernels: 184 us -> 171 us  [close_part(): pl.pallas_call(functools.partial(close_kernel, size, parts, made), out_sh...]
where the time goes in v7:
time: 618 us; the launch traced here: 607 us
  Pallas kernels  561 us (91%)
  other arithmetic  25.6 us (4%)
  local copies, waits for them, and re-layouts  15.8 us (3%)
    pallas_call x1, Pallas kernels, back_part(): pl.pallas_call(functools.partial(back_kernel, size, parts, lens.shape[1])...  175 us
    pallas_call x1, Pallas kernels, forward_part(): pl.pallas_call(functools.partial(forward_kernel, size, parts, count), out...  175 us
    pallas_call x1, Pallas kernels, close_part(): pl.pallas_call(functools.partial(close_kernel, size, parts, made), out_sh...  171 us
    pallas_call x1, Pallas kernels, unpack_grads(): pl.pallas_call(functools.partial(unpack_kernel, widths), grid=(parts,), o...  16.9 us
    pallas_call x1, Pallas kernels, pack_grads(): pl.pallas_call(pack_kernel, grid=(size // 2,), out_shape=jax.ShapeDtypeSt...  14.9 us
  transfers between devices with their start and end apart: 1, of which 0 were waited for; matrix products, arithmetic and copies ran while one was open for 1% of the time, Pallas kernels for 0%

profile of v7, /device:TPU:0, one launch (start us, length us, event | category | flops | bytes accessed | tf_op | source)
XLA Modules:
  0.0 607.1 jit_solution(3405616486224173609)
XLA Ops:
  3.3 0.9 constant_dynamic-slice_fusion.4
  4.6 1.1 constant_dynamic-slice_fusion.2
  6.3 1.3 constant_dynamic-slice_fusion
  9.1 1.3 maximum_bitcast_fusion.refs_5_
  10.5 1.1 concatenate.17
  12.2 174.8 %forward_part.1 = (bf16[4,256,1792]{2,1,0:T(8,128)(2,1)}, bf16[4,256,1344]{2,1,0:T(8,128)(2,1)}, bf16[4,64,896]{2,1,0:T(8,128)(2,1)}, bf16[4,8,56,1344]{3,2,1,0:...) custom-call(bf16[256,1792]{1,0:T(8,128)(2,1)} %bitcast.38, ...), custom_call_target="tpu_custom_call" | custom-call | flops 19964887040 | bytes 500000000 | tf_op jit(solution)/shard_map/forward_part/pallas_call | solution.py:821
  187.0 0.9 fusion.11
  188.6 1.4 fusion.18
  191.5 1.6 fusion.8
  194.7 14.9 %pack_grads.1.refs_11_ = bf16[8,4,56,2432]{3,2,1,0:T(8,128)(2,1)} custom-call(bf16[1024,1792]{1,0:T(8,128)(2,1)} %bitcast.63, bf16[1024,2432]{1,0:T(8,128)(2,1)} %bitcast.58), custom_call_target="tpu_custom_call" | custom-call | flops 8925478912 | bytes 17367040 | tf_op jit(solution)/shard_map/pack_grads/pallas_call | solution.py:1554
  209.6 9.5 %down_grad.1 = bf16[1216,1792]{1,0:T(8,128)(2,1)} custom-call(bf16[1024,1216]{1,0:T(8,128)(2,1)} %bitcast.65, bf16[1024,1792]{1,0:T(8,128)(2,1)} %bitcast.62), custom_call_target="tpu_custom_call" | custom-call | flops 4462739456 | bytes 10518528 | tf_op jit(solution)/shard_map/down_grad/pallas_call | solution.py:1514
  219.1 1.7 fusion.3
  220.7 174.8 %back_part.1 = (f32[256,1792]{1,0:T(8,128)}, f32[1,1792]{1,0:T(1,128)}, bf16[4,256,1792]{2,1,0:T(8,128)(2,1)}, bf16[4,256,1344]{2,1,0:T(8,128)(2,1)}, f32[256,17...) custom-call(s32[4,1]{1,0:T(4,128)} %bitcast.52, ...), custom_call_target="tpu_custom_call" | custom-call | flops 15502147584 | bytes 400000000 | tf_op jit(solution)/shard_map/back_part/pallas_call | solution.py:1185
  395.6 4.2 multiply_reduce_fusion
  399.9 1.2 multiply_add_fusion
  401.3 1.4 fusion.5
  403.5 1.5 collective-permute-start
  405.0 4.4 bitcast_convert_fusion
  410.4 2.9 fusion.9
  413.3 170.5 %close_part.1 = (bf16[8,4,56,1792]{3,2,1,0:T(8,128)(2,1)}, bf16[8,4,56,2432]{3,2,1,0:T(8,128)(2,1)}, f32[256,1792]{1,0:T(8,128)}, f32[8,448]{1,0:T(8,128)}, bf16...) custom-call(bf16[1024,1792]{1,0:T(8,128)(2,1)} %bitcast.60, ...), custom_call_target="tpu_custom_call" | custom-call | flops 11039408128 | bytes 500000000 | tf_op jit(solution)/shard_map/close_part/pallas_call | solution.py:1444
  583.8 1.4 fusion.17
  585.2 1.3 slice_bitcast_fusion
  586.5 3.2 fusion.10
  589.7 16.9 %unpack_grads.1 = (f32[448,4864]{1,0:T(8,128)}, f32[448,4864]{1,0:T(8,128)}, f32[448,1792]{1,0:T(8,128)}, f32[448,1792]{1,0:T(8,128)}, f32[448,1792]{1,0:T(8,128)}, /*index=5*/f32[448,1792]{1,0:T(8,128)}) custom-call(bf16[8,4,56,2432]{3,2,1,0:T(8,128)(2,1)} %get-tuple-element.97.refs_0_, bf16[8,4,56,1792]{3,2,1,0:T(8,128)(2,1)} %get-tuple-element.98.refs_1_), custom_call_target="tpu_custom_call" | custom-call | bytes 45416448 | tf_op jit(solution)/shard_map/unpack_grads/pallas_call | solution.py:1591
  (65 shorter events, 10.1 us)
Async XLA Ops:
  9.0 2.5 copy-start.9
  10.5 1.8 copy-start.8
  209.6 9.5 %copy-start.1 = (bf16[1,256,1792]{2,1,0:T(8,128)(2,1)S(1)}, bf16[1,256,1792]{2,1,0:T(8,128)(2,1)}, u32[]{:S(2)}) copy-start(bf16[1,256,1792]{2,1,0:T(8,128)(2,1)} %param.18) | copy-start | bytes 2752516
  395.6 4.3 copy-start
  395.6 4.3 copy-start.3
  395.6 4.3 copy-start.4
  395.6 4.3 copy-start.5
  395.6 9.4 %slice-start = ((s8[4358144]{0:T(1024)(128)(4,1)}), s8[4194304]{0:T(1024)(128)(4,1)S(1)}, s32[]{:S(2)}) async-start(s8[4358144]{0:T(1024)(128)(4,1)} %bitcast.43), calls=%async_computation | async-start | bytes 8388608
  399.9 1.4 copy-start.2
  399.9 5.1 slice-start.1
  403.5 6.9 %collective-permute-start = (f32[2,1792]{1,0:T(2,128)S(1)}, f32[2,1792]{1,0:T(2,128)S(1)}, u32[]{:S(2)}, u32[]{:S(2)}) collective-permute-start(f32[2,1792]{1,0:T(2,128)S(1)} %slice.137), channel_id=1, source_target_pairs={{4,0},{8,4},{12,8},{16,12},{20,16},{24,20},{28,24},{5,1},{9,5},{13... | collective-permute-start | bytes 43016 | tf_op jit(solution)/shard_map/ppermute | solution.py:27
  405.0 4.5 copy-start.6
  413.3 173.2 %copy-start.7 = (f32[256]{0:T(256)S(1)}, f32[256]{0:T(256)}, u32[]{:S(2)}) copy-start(f32[256]{0:T(256)} %get-tuple-element.125) | copy-start | bytes 3076

commit v8 on v7

--- a/solution.py
+++ b/solution.py
@@ -1097,9 +1097,9 @@
         pl.when(rank > 0)(lambda: halo(step).start())
 
     each_step(size, step_heads)
+    gu_sum.advance(1)
     for m in range(1, n):
         gu_sum.begin(m)
-    gu_sum.advance(1)
     line.relay(1)
     scatter.finish()
     fetches[2].wait()
@@ -1750,9 +1750,6 @@
         ]
     )
     terms = jnp.pad(terms, ((0, 3), (0, 0))).reshape(8, size, slice_width).transpose(1, 0, 2)
-    gu_slots, terms, down_total, tokens_grad = lax.optimization_barrier(
-        (gu_slots, terms, down_total, tokens_grad)
-    )
     qkvo_every, gu_every, feed, terms = close_part(
         5,
         flat(gated_all),

time: 618 us -> 616 us (level)
  transfers between devices with their start and end apart: 1 -> 1, of which waited for: 0 -> 0; matrix products, arithmetic and copies ran while one was open for 1% -> 2% of each run, Pallas kernels for 0% -> 31%
where the time goes in v8:
time: 616 us; the launch traced here: 606 us
  Pallas kernels  560 us (91%)
  other arithmetic  25.7 us (4%)
  local copies, waits for them, and re-layouts  16.9 us (3%)
    pallas_call x1, Pallas kernels, forward_part(): pl.pallas_call(functools.partial(forward_kernel, size, parts, count), out...  175 us
    pallas_call x1, Pallas kernels, back_part(): pl.pallas_call(functools.partial(back_kernel, size, parts, lens.shape[1])...  172 us
    pallas_call x1, Pallas kernels, close_part(): pl.pallas_call(functools.partial(close_kernel, size, parts, made), out_sh...  171 us
    pallas_call x1, Pallas kernels, unpack_grads(): pl.pallas_call(functools.partial(unpack_kernel, widths), grid=(parts,), o...  17 us
    pallas_call x1, Pallas kernels, pack_grads(): pl.pallas_call(pack_kernel, grid=(size // 2,), out_shape=jax.ShapeDtypeSt...  14.9 us
  transfers between devices with their start and end apart: 1, of which 0 were waited for; matrix products, arithmetic and copies ran while one was open for 2% of the time, Pallas kernels for 31%

profile of v8, /device:TPU:0, one launch (start us, length us, event | category | flops | bytes accessed | tf_op | source)
XLA Modules:
  0.0 606.4 jit_solution(13052243516655738003)
XLA Ops:
  3.3 0.9 constant_dynamic-slice_fusion.4
  4.6 1.1 constant_dynamic-slice_fusion.2
  6.3 1.3 constant_dynamic-slice_fusion
  9.1 1.3 maximum_bitcast_fusion.refs_5_
  10.5 1.1 concatenate.17
  12.2 174.8 %forward_part.1 = (bf16[4,256,1792]{2,1,0:T(8,128)(2,1)}, bf16[4,256,1344]{2,1,0:T(8,128)(2,1)}, bf16[4,64,896]{2,1,0:T(8,128)(2,1)}, bf16[4,8,56,1344]{3,2,1,0:...) custom-call(bf16[256,1792]{1,0:T(8,128)(2,1)} %bitcast.39, ...), custom_call_target="tpu_custom_call" | custom-call | flops 19964887040 | bytes 500000000 | tf_op jit(solution)/shard_map/forward_part/pallas_call | solution.py:821
  188.6 1.4 fusion.19
  191.5 1.6 fusion.8
  194.7 14.9 %pack_grads.1.refs_11_ = bf16[8,4,56,2432]{3,2,1,0:T(8,128)(2,1)} custom-call(bf16[1024,1792]{1,0:T(8,128)(2,1)} %bitcast.61, bf16[1024,2432]{1,0:T(8,128)(2,1)} %bitcast.56), custom_call_target="tpu_custom_call" | custom-call | flops 8925478912 | bytes 17367040 | tf_op jit(solution)/shard_map/pack_grads/pallas_call | solution.py:1554
  209.6 9.5 %down_grad.1 = bf16[1216,1792]{1,0:T(8,128)(2,1)} custom-call(bf16[1024,1216]{1,0:T(8,128)(2,1)} %bitcast.63, bf16[1024,1792]{1,0:T(8,128)(2,1)} %bitcast.60), custom_call_target="tpu_custom_call" | custom-call | flops 4462739456 | bytes 10518528 | tf_op jit(solution)/shard_map/down_grad/pallas_call | solution.py:1514
  219.1 1.7 fusion.3
  220.7 172.3 %back_part.1 = (f32[256,1792]{1,0:T(8,128)}, f32[1,1792]{1,0:T(1,128)}, bf16[4,256,1792]{2,1,0:T(8,128)(2,1)}, bf16[4,256,1344]{2,1,0:T(8,128)(2,1)}, f32[256,17...) custom-call(s32[4,1]{1,0:T(4,128)} %bitcast.50, ...), custom_call_target="tpu_custom_call" | custom-call | flops 15502147584 | bytes 400000000 | tf_op jit(solution)/shard_map/back_part/pallas_call | solution.py:1185
  393.1 4.2 multiply_reduce_fusion
  397.4 1.2 multiply_add_fusion
  398.6 1.4 fusion.5
  400.7 1.2 copy-done.3
  402.0 1.5 collective-permute-start
  404.4 171.1 %close_part.1 = (bf16[8,4,56,1792]{3,2,1,0:T(8,128)(2,1)}, bf16[8,4,56,2432]{3,2,1,0:T(8,128)(2,1)}, f32[256,1792]{1,0:T(8,128)}, f32[8,448]{1,0:T(8,128)}, bf16...) custom-call(bf16[1024,1792]{1,0:T(8,128)(2,1)} %bitcast.58, ...), custom_call_target="tpu_custom_call" | custom-call | flops 11039408128 | bytes 500000000 | tf_op jit(solution)/shard_map/close_part/pallas_call | solution.py:1444
  575.6 1.3 slice_bitcast_fusion
  576.9 6.5 %bitcast_convert_fusion = f32[1216,1792]{1,0:T(8,128)} fusion(bf16[8,152,1792]{2,1,0:T(8,128)(2,1)} %get-tuple-element.97), kind=kLoop, calls=%fused_computation | loop fusion | flops 2179072 | bytes 13074432 | tf_op jit(solution)/shard_map/convert_element_type | solution.py:1728
  583.5 1.1 fusion.11
  584.6 1.4 fusion.18
  586.0 17.0 %unpack_grads.1 = (f32[448,4864]{1,0:T(8,128)}, f32[448,4864]{1,0:T(8,128)}, f32[448,1792]{1,0:T(8,128)}, f32[448,1792]{1,0:T(8,128)}, f32[448,1792]{1,0:T(8,128)}, /*index=5*/f32[448,1792]{1,0:T(8,128)}) custom-call(bf16[8,4,56,2432]{3,2,1,0:T(8,128)(2,1)} %get-tuple-element.89.refs_0_, bf16[8,4,56,1792]{3,2,1,0:T(8,128)(2,1)} %get-tuple-element.90.refs_1_), custom_call_target="tpu_custom_call" | custom-call | bytes 45416448 | tf_op jit(solution)/shard_map/unpack_grads/pallas_call | solution.py:1591
  603.0 2.9 fusion.10
  (68 shorter events, 10.8 us)
Async XLA Ops:
  9.0 2.5 copy-start.13
  10.5 1.8 copy-start.12
  209.6 9.5 %copy-start.1 = (bf16[1,256,1792]{2,1,0:T(8,128)(2,1)S(1)}, bf16[1,256,1792]{2,1,0:T(8,128)(2,1)}, u32[]{:S(2)}) copy-start(bf16[1,256,1792]{2,1,0:T(8,128)(2,1)} %param.18) | copy-start | bytes 2752516
  393.0 4.3 copy-start
  393.0 4.3 copy-start.5
  393.1 4.3 copy-start.8
  393.1 4.3 copy-start.9
  397.4 1.2 copy-start.2
  400.0 3.5 copy-start.10
  400.7 1.2 copy-start.3
  402.0 201.0 %collective-permute-start = (f32[2,1792]{1,0:T(2,128)S(1)}, f32[2,1792]{1,0:T(2,128)S(1)}, u32[]{:S(2)}, u32[]{:S(2)}) collective-permute-start(f32[2,1792]{1,0:T(2,128)S(1)} %slice.137), channel_id=1, source_target_pairs={{4,0},{8,4},{12,8},{16,12},{20,16},{24,20},{28,24},{5,1},{9,5},{13... | collective-permute-start | bytes 43016 | tf_op jit(solution)/shard_map/ppermute | solution.py:27
  576.9 6.6 %copy-start.6 = (f32[256,1792]{1,0:T(8,128)S(1)}, f32[256,1792]{1,0:T(8,128)}, u32[]{:S(2)}) copy-start(f32[256,1792]{1,0:T(8,128)} %get-tuple-element.67.refs_4_) | copy-start | bytes 5505028
  576.9 6.6 %copy-start.7 = (f32[256,1792]{1,0:T(8,128)S(1)}, f32[256,1792]{1,0:T(8,128)}, u32[]{:S(2)}) copy-start(f32[256,1792]{1,0:T(8,128)} %get-tuple-element.86) | copy-start | bytes 5505028
  576.9 6.6 %copy-start.11 = (f32[256]{0:T(256)S(1)}, f32[256]{0:T(256)}, u32[]{:S(2)}) copy-start(f32[256]{0:T(256)} %get-tuple-element.117) | copy-start | bytes 3076
  586.0 17.1 %copy-start.4 = (f32[258,1792]{1,0:T(8,128)S(1)}, f32[258,1792]{1,0:T(8,128)}, u32[]{:S(2)}) copy-start(f32[258,1792]{1,0:T(8,128)} %copy-done.3) | copy-start | bytes 5548036

commit v9 on v8

--- a/solution.py
+++ b/solution.py
@@ -639,7 +639,6 @@
         pl.when(z == n - 1 - j)(line_u.own_down)
     for step in others:
         gather.ready(step)
-    grads.relay()
     line_q.gathered()
     keeps = [
         pltpu.make_async_copy(all_ref, r.gated_hbm, r.stores.at[size]),
@@ -715,6 +714,7 @@
 
     each_step(size, mix)
     scatter.join()
+    grads.relay()
     for j in range(2, n):
         line_u.relay(j)
     gather = Gather(group, all_ref, r.g_send, r.g_recv)

time: 616 us -> 625 us (1.015)
  Pallas kernels: 560 us -> 570 us
    pallas_call x1, Pallas kernels: 175 us -> 184 us  [forward_part(): pl.pallas_call(functools.partial(forward_kernel, size, parts, count), out...]
  transfers between devices with their start and end apart: 1 -> 1, of which waited for: 0 -> 0; matrix products, arithmetic and copies ran while one was open for 2% -> 2% of each run, Pallas kernels for 31% -> 30%
where the time goes in v9:
time: 625 us; the launch traced here: 616 us
  Pallas kernels  570 us (91%)
  other arithmetic  25.7 us (4%)
  local copies, waits for them, and re-layouts  16.9 us (3%)
    pallas_call x1, Pallas kernels, forward_part(): pl.pallas_call(functools.partial(forward_kernel, size, parts, count), out...  184 us
    pallas_call x1, Pallas kernels, back_part(): pl.pallas_call(functools.partial(back_kernel, size, parts, lens.shape[1])...  174 us
    pallas_call x1, Pallas kernels, close_part(): pl.pallas_call(functools.partial(close_kernel, size, parts, made), out_sh...  171 us
    pallas_call x1, Pallas kernels, unpack_grads(): pl.pallas_call(functools.partial(unpack_kernel, widths), grid=(parts,), o...  17 us
    pallas_call x1, Pallas kernels, pack_grads(): pl.pallas_call(pack_kernel, grid=(size // 2,), out_shape=jax.ShapeDtypeSt...  14.9 us
  transfers between devices with their start and end apart: 1, of which 0 were waited for; matrix products, arithmetic and copies ran while one was open for 2% of the time, Pallas kernels for 30%

profile of v9, /device:TPU:0, one launch (start us, length us, event | category | flops | bytes accessed | tf_op | source)
XLA Modules:
  0.0 616.4 jit_solution(6758670831332917546)
XLA Ops:
  3.3 0.9 constant_dynamic-slice_fusion.4
  4.6 1.1 constant_dynamic-slice_fusion.2
  6.3 1.3 constant_dynamic-slice_fusion
  9.1 1.3 maximum_bitcast_fusion.refs_5_
  10.5 1.1 concatenate.17
  12.2 183.5 %forward_part.1 = (bf16[4,256,1792]{2,1,0:T(8,128)(2,1)}, bf16[4,256,1344]{2,1,0:T(8,128)(2,1)}, bf16[4,64,896]{2,1,0:T(8,128)(2,1)}, bf16[4,8,56,1344]{3,2,1,0:...) custom-call(bf16[256,1792]{1,0:T(8,128)(2,1)} %bitcast.39, ...), custom_call_target="tpu_custom_call" | custom-call | flops 19964887040 | bytes 500000000 | tf_op jit(solution)/shard_map/forward_part/pallas_call | solution.py:821
  197.4 1.4 fusion.19
  200.3 1.6 fusion.8
  203.5 14.9 %pack_grads.1.refs_11_ = bf16[8,4,56,2432]{3,2,1,0:T(8,128)(2,1)} custom-call(bf16[1024,1792]{1,0:T(8,128)(2,1)} %bitcast.61, bf16[1024,2432]{1,0:T(8,128)(2,1)} %bitcast.56), custom_call_target="tpu_custom_call" | custom-call | flops 8925478912 | bytes 17367040 | tf_op jit(solution)/shard_map/pack_grads/pallas_call | solution.py:1554
  218.4 9.5 %down_grad.1 = bf16[1216,1792]{1,0:T(8,128)(2,1)} custom-call(bf16[1024,1216]{1,0:T(8,128)(2,1)} %bitcast.63, bf16[1024,1792]{1,0:T(8,128)(2,1)} %bitcast.60), custom_call_target="tpu_custom_call" | custom-call | flops 4462739456 | bytes 10518528 | tf_op jit(solution)/shard_map/down_grad/pallas_call | solution.py:1514
  227.9 1.7 fusion.3
  229.5 173.7 %back_part.1 = (f32[256,1792]{1,0:T(8,128)}, f32[1,1792]{1,0:T(1,128)}, bf16[4,256,1792]{2,1,0:T(8,128)(2,1)}, bf16[4,256,1344]{2,1,0:T(8,128)(2,1)}, f32[256,17...) custom-call(s32[4,1]{1,0:T(4,128)} %bitcast.50, ...), custom_call_target="tpu_custom_call" | custom-call | flops 15502147584 | bytes 400000000 | tf_op jit(solution)/shard_map/back_part/pallas_call | solution.py:1185
  403.3 4.2 multiply_reduce_fusion
  407.6 1.2 multiply_add_fusion
  408.8 1.4 fusion.5
  411.0 1.2 copy-done.3
  412.2 1.5 collective-permute-start
  414.7 170.9 %close_part.1 = (bf16[8,4,56,1792]{3,2,1,0:T(8,128)(2,1)}, bf16[8,4,56,2432]{3,2,1,0:T(8,128)(2,1)}, f32[256,1792]{1,0:T(8,128)}, f32[8,448]{1,0:T(8,128)}, bf16...) custom-call(bf16[1024,1792]{1,0:T(8,128)(2,1)} %bitcast.58, ...), custom_call_target="tpu_custom_call" | custom-call | flops 11039408128 | bytes 500000000 | tf_op jit(solution)/shard_map/close_part/pallas_call | solution.py:1444
  585.6 1.3 slice_bitcast_fusion
  586.9 6.5 %bitcast_convert_fusion = f32[1216,1792]{1,0:T(8,128)} fusion(bf16[8,152,1792]{2,1,0:T(8,128)(2,1)} %get-tuple-element.97), kind=kLoop, calls=%fused_computation | loop fusion | flops 2179072 | bytes 13074432 | tf_op jit(solution)/shard_map/convert_element_type | solution.py:1728
  593.5 1.1 fusion.11
  594.6 1.4 fusion.18
  596.0 17.0 %unpack_grads.1 = (f32[448,4864]{1,0:T(8,128)}, f32[448,4864]{1,0:T(8,128)}, f32[448,1792]{1,0:T(8,128)}, f32[448,1792]{1,0:T(8,128)}, f32[448,1792]{1,0:T(8,128)}, /*index=5*/f32[448,1792]{1,0:T(8,128)}) custom-call(bf16[8,4,56,2432]{3,2,1,0:T(8,128)(2,1)} %get-tuple-element.89.refs_0_, bf16[8,4,56,1792]{3,2,1,0:T(8,128)(2,1)} %get-tuple-element.90.refs_1_), custom_call_target="tpu_custom_call" | custom-call | bytes 45416448 | tf_op jit(solution)/shard_map/unpack_grads/pallas_call | solution.py:1591
  613.0 2.9 fusion.10
  (68 shorter events, 10.8 us)
Async XLA Ops:
  9.0 2.5 copy-start.13
  10.5 1.8 copy-start.12
  218.4 9.5 %copy-start.1 = (bf16[1,256,1792]{2,1,0:T(8,128)(2,1)S(1)}, bf16[1,256,1792]{2,1,0:T(8,128)(2,1)}, u32[]{:S(2)}) copy-start(bf16[1,256,1792]{2,1,0:T(8,128)(2,1)} %param.18) | copy-start | bytes 2752516
  403.3 4.3 copy-start
  403.3 4.3 copy-start.5
  403.3 4.3 copy-start.8
  403.3 4.3 copy-start.9
  407.6 1.2 copy-start.2
  410.3 3.5 copy-start.10
  411.0 1.2 copy-start.3
  412.2 200.8 %collective-permute-start = (f32[2,1792]{1,0:T(2,128)S(1)}, f32[2,1792]{1,0:T(2,128)S(1)}, u32[]{:S(2)}, u32[]{:S(2)}) collective-permute-start(f32[2,1792]{1,0:T(2,128)S(1)} %slice.137), channel_id=1, source_target_pairs={{4,0},{8,4},{12,8},{16,12},{20,16},{24,20},{28,24},{5,1},{9,5},{13... | collective-permute-start | bytes 43016 | tf_op jit(solution)/shard_map/ppermute | solution.py:27
  586.9 6.6 %copy-start.6 = (f32[256,1792]{1,0:T(8,128)S(1)}, f32[256,1792]{1,0:T(8,128)}, u32[]{:S(2)}) copy-start(f32[256,1792]{1,0:T(8,128)} %get-tuple-element.67.refs_4_) | copy-start | bytes 5505028
  586.9 6.6 %copy-start.7 = (f32[256,1792]{1,0:T(8,128)S(1)}, f32[256,1792]{1,0:T(8,128)}, u32[]{:S(2)}) copy-start(f32[256,1792]{1,0:T(8,128)} %get-tuple-element.86) | copy-start | bytes 5505028
  586.9 6.6 %copy-start.11 = (f32[256]{0:T(256)S(1)}, f32[256]{0:T(256)}, u32[]{:S(2)}) copy-start(f32[256]{0:T(256)} %get-tuple-element.117) | copy-start | bytes 3076
  596.0 17.1 %copy-start.4 = (f32[258,1792]{1,0:T(8,128)S(1)}, f32[258,1792]{1,0:T(8,128)}, u32[]{:S(2)}) copy-start(f32[258,1792]{1,0:T(8,128)} %copy-done.3) | copy-start | bytes 5548036
